TPU v7x, 32 devices: a whole 2x2x4 slice. The times are simulated.
32 devices in a mesh: fsdp: 16 (over z, x, core), tp: 2 (over y).
Axes of the slice: x: 2, y: 2, z: 4, core: 2. Of those that a mesh axis runs over, the one named last changes fastest.
Arguments:
- block_input: bfloat16 [3072, 2304], P(('fsdp', 'tp')), may hold values from -6 to 6
- lengths: int32 [16, 9], P('fsdp'), may hold values from 1 to 96, 192 in all within a row
- attention_norm_gain: bfloat16 [2304], P('fsdp'), may hold values from 0.25 to 1.75
- attention_post_gain: bfloat16 [2304], P('fsdp'), may hold values from 0.25 to 1.75
- feedforward_norm_gain: bfloat16 [2304], P('fsdp'), may hold values from 0.25 to 1.75
- feedforward_post_gain: bfloat16 [2304], P('fsdp'), may hold values from 0.25 to 1.75
- query_weight: bfloat16 [2304, 2048], P('fsdp', 'tp'), may hold values from -0.125 to 0.125
- key_weight: bfloat16 [2304, 1024], P('fsdp', 'tp'), may hold values from -0.125 to 0.125
- value_weight: bfloat16 [2304, 1024], P('fsdp', 'tp'), may hold values from -0.125 to 0.125
- output_weight: bfloat16 [2304, 2048], P('fsdp', 'tp'), may hold values from -0.125 to 0.125
- gate_weight: bfloat16 [2304, 9216], P('fsdp', 'tp'), may hold values from -0.125 to 0.125
- up_weight: bfloat16 [2304, 9216], P('fsdp', 'tp'), may hold values from -0.125 to 0.125
- down_weight: bfloat16 [2304, 9216], P('fsdp', 'tp'), may hold values from -0.0625 to 0.0625
- output_cotangent: bfloat16 [3072, 2304], P(('fsdp', 'tp')), may hold values from -6 to 6
Outputs:
- block_output: bfloat16 [3072, 2304], P(('fsdp', 'tp'))
- input_gradient: float32 [3072, 2304], P(('fsdp', 'tp'))
- attention_norm_gain_gradient: float32 [2304], P('fsdp')
- attention_post_gain_gradient: float32 [2304], P('fsdp')
- feedforward_norm_gain_gradient: float32 [2304], P('fsdp')
- feedforward_post_gain_gradient: float32 [2304], P('fsdp')
- query_weight_gradient: float32 [2304, 2048], P('fsdp', 'tp')
- key_weight_gradient: float32 [2304, 1024], P('fsdp', 'tp')
- value_weight_gradient: float32 [2304, 1024], P('fsdp', 'tp')
- output_weight_gradient: float32 [2304, 2048], P('fsdp', 'tp')
- gate_weight_gradient: float32 [2304, 9216], P('fsdp', 'tp')
- up_weight_gradient: float32 [2304, 9216], P('fsdp', 'tp')
- down_weight_gradient: float32 [2304, 9216], P('fsdp', 'tp')
Inputs may be any that keep to these rules, and one draw needn't show every extreme that they name: `lengths`: row g gives the length of group g's prompt (column 0) and of its 8 continuations; each row sums to 192, and its largest entry is 96.
All inputs are finite; a program needn't handle non-finite values.
Results may differ from a plain program's by a relative error of at most 0.017.
Values may be sent and summed in bfloat16 or wider, within the bound.
A program may use at most 512 MiB of HBM per device.

v0:
```python
import math

import jax
import jax.numpy as jnp
from jax import lax
from jax.sharding import PartitionSpec as P

HEAD_SIZE = 256


EPSILON = 1e-06
SOFTCAP = 50.0
NEGATIVE = -1e30


def contract_last(left_rows, right_rows):
    return lax.dot_general(
        left_rows, right_rows, (((1,), (1,)), ((), ())), preferred_element_type=jnp.float32
    )


def contract_first(left_rows, right_rows):
    return lax.dot_general(
        left_rows, right_rows, (((0,), (0,)), ((), ())), preferred_element_type=jnp.float32
    )


def normalize_parts(value_rows):
    inverse = lax.rsqrt(jnp.mean(value_rows * value_rows, axis=-1, keepdims=True) + EPSILON)
    return (value_rows * inverse, inverse)


def norm_backward(unit_rows, inverse, norm_gain, upstream):
    scaled = upstream * norm_gain
    return inverse * (scaled - unit_rows * jnp.mean(scaled * unit_rows, axis=-1, keepdims=True))


def layout(lengths_row, grouped_rows):
    segment_ends = jnp.cumsum(lengths_row)
    segment_starts = segment_ends - lengths_row
    row_index = jnp.arange(grouped_rows, dtype=jnp.int32)
    segment = jnp.sum((row_index[:, None] >= segment_ends[None, :]).astype(jnp.int32), axis=1)
    onehot = segment[:, None] == jnp.arange(lengths_row.shape[0], dtype=jnp.int32)[None, :]
    segment_begin = jnp.sum(jnp.where(onehot, segment_starts[None, :], 0), axis=1)
    prompt_shift = jnp.where(segment > 0, lengths_row[0], 0)
    return (segment, row_index - segment_begin + prompt_shift)


def rotary_tables(position):
    frequency = jnp.exp(
        jnp.arange(HEAD_SIZE // 2, dtype=jnp.float32) * (-2.0 * math.log(10000.0) / HEAD_SIZE)
    )
    angles = position.astype(jnp.float32)[:, None] * frequency[None, :]
    return (jnp.cos(angles), jnp.sin(angles))


def apply_rotary(value_rows, cosine_lookup, sine_lookup):
    half_width = value_rows.shape[-1] // 2
    first_half = value_rows[..., :half_width]
    second_half = value_rows[..., half_width:]
    cosine_part = cosine_lookup[:, None, :]
    sine_part = sine_lookup[:, None, :]
    return jnp.concatenate(
        [
            first_half * cosine_part - second_half * sine_part,
            second_half * cosine_part + first_half * sine_part,
        ],
        axis=-1,
    )


def unrotate(value_rows, cosine_lookup, sine_lookup):
    half_width = value_rows.shape[-1] // 2
    first_half = value_rows[..., :half_width]
    second_half = value_rows[..., half_width:]
    cosine_part = cosine_lookup[:, None, :]
    sine_part = sine_lookup[:, None, :]
    return jnp.concatenate(
        [
            first_half * cosine_part + second_half * sine_part,
            second_half * cosine_part - first_half * sine_part,
        ],
        axis=-1,
    )


def visible(segment):
    row_index = jnp.arange(segment.shape[0], dtype=jnp.int32)
    same_segment = (segment[:, None] == segment[None, :]) & (
        row_index[None, :] <= row_index[:, None]
    )
    from_prompt = (segment[None, :] == 0) & (segment[:, None] > 0)
    return same_segment | from_prompt


def masked_scores(rotated_query, rotated_key, visible_mask):
    raw_scores = jnp.einsum(
        "qgrd,kgd->grqk", rotated_query, rotated_key, preferred_element_type=jnp.float32
    )
    tanh_value = jnp.tanh(raw_scores * HEAD_SIZE ** (-0.5) / SOFTCAP)
    return (jnp.where(visible_mask[None, None], SOFTCAP * tanh_value, NEGATIVE), tanh_value)


def gelu_product(gate_value, up_value):
    return jax.nn.gelu(gate_value, approximate=True) * up_value


def shards(
    block_input,
    lengths,
    attention_norm_gain,
    attention_post_gain,
    feedforward_norm_gain,
    feedforward_post_gain,
    query_weight,
    key_weight,
    value_weight,
    output_weight,
    gate_weight,
    up_weight,
    down_weight,
    output_cotangent,
):
    query_full, key_full, value_full, output_full, gain_one, gain_two = (
        lax.all_gather(query_weight, "fsdp", axis=0, tiled=True),
        lax.all_gather(key_weight, "fsdp", axis=0, tiled=True),
        lax.all_gather(value_weight, "fsdp", axis=0, tiled=True),
        lax.all_gather(output_weight, "fsdp", axis=0, tiled=True),
        lax.all_gather(attention_norm_gain, "fsdp", axis=0, tiled=True),
        lax.all_gather(attention_post_gain, "fsdp", axis=0, tiled=True),
    )
    gate_full, up_full, down_full, gain_three, gain_four = (
        lax.all_gather(gate_weight, "fsdp", axis=0, tiled=True),
        lax.all_gather(up_weight, "fsdp", axis=0, tiled=True),
        lax.all_gather(down_weight, "fsdp", axis=0, tiled=True),
        lax.all_gather(feedforward_norm_gain, "fsdp", axis=0, tiled=True),
        lax.all_gather(feedforward_post_gain, "fsdp", axis=0, tiled=True),
    )
    gain_one = gain_one.astype(jnp.float32)
    gain_two = gain_two.astype(jnp.float32)
    gain_three = gain_three.astype(jnp.float32)
    gain_four = gain_four.astype(jnp.float32)
    rows_local = block_input.shape[0]
    grouped_rows = rows_local * lax.axis_size("tp")
    segment, position = layout(lengths[0], grouped_rows)
    cosine_lookup, sine_lookup = rotary_tables(position)
    visible_mask = visible(segment)
    residual = block_input.astype(jnp.float32)
    unit_one, inverse_one = normalize_parts(residual)
    normed_local = (unit_one * gain_one).astype(jnp.bfloat16)
    normed = lax.all_gather(normed_local, "tp", axis=0, tiled=True)
    query_raw = jnp.dot(normed, query_full, preferred_element_type=jnp.float32)
    key_raw = jnp.dot(normed, key_full, preferred_element_type=jnp.float32)
    value_raw = jnp.dot(normed, value_full, preferred_element_type=jnp.float32)
    heads_local = query_raw.shape[1] // HEAD_SIZE
    kv_local = key_raw.shape[1] // HEAD_SIZE
    repeat_heads = heads_local // kv_local
    rotated_query = apply_rotary(
        query_raw.reshape(grouped_rows, heads_local, HEAD_SIZE), cosine_lookup, sine_lookup
    ).astype(jnp.bfloat16)
    rotated_query = rotated_query.reshape(grouped_rows, kv_local, repeat_heads, HEAD_SIZE)
    rotated_key = apply_rotary(
        key_raw.reshape(grouped_rows, kv_local, HEAD_SIZE), cosine_lookup, sine_lookup
    ).astype(jnp.bfloat16)
    value_reduced = value_raw.astype(jnp.bfloat16).reshape(grouped_rows, kv_local, HEAD_SIZE)
    capped, tanh_value = masked_scores(rotated_query, rotated_key, visible_mask)
    row_peak = jnp.max(capped, axis=-1, keepdims=True)
    log_total = row_peak + jnp.log(jnp.sum(jnp.exp(capped - row_peak), axis=-1, keepdims=True))
    softmax_probs = jnp.exp(capped - log_total)
    mixed_heads = jnp.einsum(
        "grqk,kgd->qgrd",
        softmax_probs.astype(jnp.bfloat16),
        value_reduced,
        preferred_element_type=jnp.float32,
    )
    attended = mixed_heads.reshape(grouped_rows, heads_local * HEAD_SIZE).astype(jnp.bfloat16)
    row_piece = attended
    branch_one = lax.psum_scatter(
        contract_last(row_piece, output_full), "tp", scatter_dimension=0, tiled=True
    )
    unit_two, inverse_two = normalize_parts(branch_one)
    middle = residual + unit_two * gain_two
    unit_three, inverse_three = normalize_parts(middle)
    feed_local = (unit_three * gain_three).astype(jnp.bfloat16)
    feed_input = lax.all_gather(feed_local, "tp", axis=0, tiled=True)
    gate_value = jnp.dot(feed_input, gate_full, preferred_element_type=jnp.float32)
    up_value = jnp.dot(feed_input, up_full, preferred_element_type=jnp.float32)
    hidden = gelu_product(gate_value, up_value).astype(jnp.bfloat16)
    row_piece = hidden
    branch_two = lax.psum_scatter(
        contract_last(row_piece, down_full), "tp", scatter_dimension=0, tiled=True
    )
    unit_four, inverse_four = normalize_parts(branch_two)
    block_output = (middle + unit_four * gain_four).astype(jnp.bfloat16)
    upstream = output_cotangent.astype(jnp.float32)
    gain_four_grad = jnp.sum(upstream * unit_four, axis=0)
    branch_two_grad = norm_backward(unit_four, inverse_four, gain_four, upstream).astype(
        jnp.bfloat16
    )
    held_back = lax.optimization_barrier(
        (
            query_weight,
            key_weight,
            value_weight,
            output_weight,
            gate_weight,
            up_weight,
            down_weight,
            branch_two_grad,
        )
    )
    query_full, key_full, value_full, output_full, gate_full, up_full, down_full = (
        lax.all_gather(held_back[0], "fsdp", axis=0, tiled=True),
        lax.all_gather(held_back[1], "fsdp", axis=0, tiled=True),
        lax.all_gather(held_back[2], "fsdp", axis=0, tiled=True),
        lax.all_gather(held_back[3], "fsdp", axis=0, tiled=True),
        lax.all_gather(held_back[4], "fsdp", axis=0, tiled=True),
        lax.all_gather(held_back[5], "fsdp", axis=0, tiled=True),
        lax.all_gather(held_back[6], "fsdp", axis=0, tiled=True),
    )
    branch_two_grad = held_back[7]
    feed_grad_rows = lax.all_gather(branch_two_grad, "tp", axis=0, tiled=True)
    hidden_grad = jnp.dot(feed_grad_rows, down_full, preferred_element_type=jnp.float32)
    unused_out, pullback = jax.vjp(gelu_product, gate_value, up_value)
    gate_grad, up_grad = pullback(hidden_grad)
    gate_up_grad = jnp.concatenate(
        [gate_grad.astype(jnp.bfloat16), up_grad.astype(jnp.bfloat16)], axis=1
    )
    feed_split = gate_full.shape[1]
    shard_rows = query_weight.shape[0]
    left_rows = feed_input
    feed_weight_grads = lax.psum_scatter(
        jnp.concatenate(
            [contract_first(left_rows, gate_up_grad), contract_first(feed_grad_rows, hidden)],
            axis=1,
        ),
        "fsdp",
        scatter_dimension=0,
        tiled=True,
    )
    row_piece = gate_up_grad
    normed_three_grad = lax.psum_scatter(
        contract_last(row_piece[:, :feed_split], gate_full)
        + contract_last(row_piece[:, feed_split:], up_full),
        "tp",
        scatter_dimension=0,
        tiled=True,
    )
    gain_three_grad = jnp.sum(normed_three_grad * unit_three, axis=0)
    middle_grad = upstream + norm_backward(unit_three, inverse_three, gain_three, normed_three_grad)
    gain_two_grad = jnp.sum(middle_grad * unit_two, axis=0)
    branch_one_grad = norm_backward(unit_two, inverse_two, gain_two, middle_grad).astype(
        jnp.bfloat16
    )
    attention_grad_rows = lax.all_gather(branch_one_grad, "tp", axis=0, tiled=True)
    mixed_grad = jnp.dot(
        attention_grad_rows, output_full, preferred_element_type=jnp.float32
    ).astype(jnp.bfloat16)
    mixed_grad = mixed_grad.reshape(grouped_rows, kv_local, repeat_heads, HEAD_SIZE)
    capped_again, tanh_again = masked_scores(rotated_query, rotated_key, visible_mask)
    probs_again = jnp.exp(capped_again - log_total)
    value_grad = jnp.einsum(
        "grqk,qgrd->kgd",
        probs_again.astype(jnp.bfloat16),
        mixed_grad,
        preferred_element_type=jnp.float32,
    )
    probs_grad = jnp.einsum(
        "qgrd,kgd->grqk", mixed_grad, value_reduced, preferred_element_type=jnp.float32
    )
    score_grad = probs_again * (
        probs_grad - jnp.sum(probs_again * probs_grad, axis=-1, keepdims=True)
    )
    raw_grad = (score_grad * (1.0 - tanh_again * tanh_again) * HEAD_SIZE ** (-0.5)).astype(
        jnp.bfloat16
    )
    query_grad = jnp.einsum(
        "grqk,kgd->qgrd", raw_grad, rotated_key, preferred_element_type=jnp.float32
    )
    key_grad = jnp.einsum(
        "grqk,qgrd->kgd", raw_grad, rotated_query, preferred_element_type=jnp.float32
    )
    query_grad = unrotate(
        query_grad.reshape(grouped_rows, heads_local, HEAD_SIZE), cosine_lookup, sine_lookup
    )
    key_grad = unrotate(key_grad, cosine_lookup, sine_lookup)
    projected_grad = jnp.concatenate(
        [
            query_grad.reshape(grouped_rows, heads_local * HEAD_SIZE).astype(jnp.bfloat16),
            key_grad.reshape(grouped_rows, kv_local * HEAD_SIZE).astype(jnp.bfloat16),
            value_grad.reshape(grouped_rows, kv_local * HEAD_SIZE).astype(jnp.bfloat16),
        ],
        axis=1,
    )
    query_width = query_full.shape[1]
    key_width = key_full.shape[1]
    left_rows = normed
    attention_weight_grads = lax.psum_scatter(
        jnp.concatenate(
            [
                contract_first(left_rows, projected_grad),
                contract_first(attention_grad_rows, attended),
            ],
            axis=1,
        ),
        "fsdp",
        scatter_dimension=0,
        tiled=True,
    )
    row_piece = projected_grad
    total = contract_last(row_piece[:, :query_width], query_full)
    total = total + contract_last(row_piece[:, query_width : query_width + key_width], key_full)
    normed_one_grad = lax.psum_scatter(
        (total + contract_last(row_piece[:, query_width + key_width :], value_full)).astype(
            jnp.bfloat16
        ),
        "tp",
        scatter_dimension=0,
        tiled=True,
    ).astype(jnp.float32)
    gain_one_grad = jnp.sum(normed_one_grad * unit_one, axis=0)
    input_gradient = middle_grad + norm_backward(unit_one, inverse_one, gain_one, normed_one_grad)
    gain_sums = lax.psum(
        (gain_one_grad, gain_two_grad, gain_three_grad, gain_four_grad), ("fsdp", "tp")
    )
    offset = lax.axis_index("fsdp") * shard_rows
    gain_shards = [
        lax.dynamic_slice_in_dim(total_sum, offset, shard_rows) for total_sum in gain_sums
    ]
    value_start = query_width + key_width
    output_start = value_start + key_width
    return (
        block_output,
        input_gradient,
        gain_shards[0],
        gain_shards[1],
        gain_shards[2],
        gain_shards[3],
        attention_weight_grads[:, :query_width],
        attention_weight_grads[:, query_width:value_start],
        attention_weight_grads[:, value_start:output_start],
        attention_weight_grads[:, output_start:],
        feed_weight_grads[:, :feed_split],
        feed_weight_grads[:, feed_split : 2 * feed_split],
        feed_weight_grads[:, 2 * feed_split :],
    )


def solution(mesh):
    placed = (
        P(("fsdp", "tp"), None),
        P("fsdp", None),
        P("fsdp"),
        P("fsdp"),
        P("fsdp"),
        P("fsdp"),
        P("fsdp", "tp"),
        P("fsdp", "tp"),
        P("fsdp", "tp"),
        P("fsdp", "tp"),
        P("fsdp", "tp"),
        P("fsdp", "tp"),
        P("fsdp", "tp"),
        P(("fsdp", "tp"), None),
    )
    return jax.shard_map(
        shards,
        mesh=mesh,
        in_specs=placed,
        out_specs=(
            P(("fsdp", "tp"), None),
            P(("fsdp", "tp"), None),
            P("fsdp"),
            P("fsdp"),
            P("fsdp"),
            P("fsdp"),
            P("fsdp", "tp"),
            P("fsdp", "tp"),
            P("fsdp", "tp"),
            P("fsdp", "tp"),
            P("fsdp", "tp"),
            P("fsdp", "tp"),
            P("fsdp", "tp"),
        ),
        check_vma=False,
    )
```

profile of v0, /device:TPU:0, one launch (start us, length us, event | category | flops | bytes accessed | tf_op | source)
XLA Modules:
  0.0 2708.5 jit_solution(12363852051479386329)
XLA Ops:
  15.4 63.9 %all-reduce.5 = (bf16[2304]{0:T(1024)(128)(2,1)S(1)}, bf16[2304]{0:T(1024)(128)(2,1)S(1)}, bf16[2304]{0:T(1024)(128)(2,1)S(1)}, bf16[2304]{0:T(1024)(128)(2,1)S(1)}) all-reduce(bf16[2304]{0:T(1024)(128)(2,1)S(1)} %dynamic-update-slice, bf16[2304]{0:T(1024)(128)(2,1)S(1)} %dynamic-update-slice.1, ...), channel_id=1, replica_groups=mesh['fsdp'=16,'tp'=2] {'fsdp'}, use_global_device_ids=true, to_apply=%add | all-reduce | flops 9216 | bytes 36864
  83.3 9.0 all_gather.67
  93.0 2.3 fusion.107
  95.6 3.4 all-gather.15.cloned.1.call-done
  101.6 51.6 %all-gather.19.cloned.1.call-done = bf16[2304,1024]{1,0:T(8,128)(2,1)} async-done(((bf16[144,1024]{1,0:T(8,128)(2,1)}), bf16[2304,1024]{1,0:T(8,128)(2,1)}) %all-gather.19.cloned.1.call-update) | async-done | bytes 4718608 | tf_op jit(solution)/shard_map/all_gather | solution.py:125
  153.2 3.4 fusion.108
  159.3 47.7 %all-gather.21.cloned.1.call-done = bf16[2304,1024]{1,0:T(8,128)(2,1)} async-done(((bf16[144,1024]{1,0:T(8,128)(2,1)}), bf16[2304,1024]{1,0:T(8,128)(2,1)}) %all-gather.21.cloned.1.call-update) | async-done | bytes 4718608 | tf_op jit(solution)/shard_map/all_gather | solution.py:128
  207.0 5.2 fusion.109
  214.4 24.9 reduce-scatter.9.cloned.1.call-done
  242.3 13.0 all_gather.74
  255.3 95.5 %all-gather.23.cloned.1.call-done = bf16[2304,4608]{1,0:T(8,128)(2,1)} async-done(((bf16[144,4608]{1,0:T(8,128)(2,1)}), bf16[2304,4608]{1,0:T(8,128)(2,1)}) %all-gather.23.cloned.1.call-update) | async-done | bytes 21233680 | tf_op jit(solution)/shard_map/all_gather | solution.py:133
  350.8 11.4 fusion.110
  362.1 100.3 %all-gather.25.cloned.1.call-done = bf16[2304,4608]{1,0:T(8,128)(2,1)} async-done(((bf16[144,4608]{1,0:T(8,128)(2,1)}), bf16[2304,4608]{1,0:T(8,128)(2,1)}) %all-gather.25.cloned.1.call-update) | async-done | bytes 21233680 | tf_op jit(solution)/shard_map/all_gather | solution.py:134
  462.4 14.7 multiply_convert_fusion.1
  477.1 96.9 %all-gather.27.cloned.1.call-done = bf16[2304,4608]{1,0:T(8,128)(2,1)} async-done(((bf16[144,4608]{1,0:T(8,128)(2,1)}), bf16[2304,4608]{1,0:T(8,128)(2,1)}) %all-gather.27.cloned.1.call-update) | async-done | bytes 21233680 | tf_op jit(solution)/shard_map/all_gather | solution.py:135
  574.0 12.6 fusion.111
  586.7 28.4 %reduce-scatter.11.cloned.1.call-done = f32[96,2304]{1,0:T(8,128)} async-done(((f32[192,2304]{1,0:T(8,128)}), f32[96,2304]{1,0:T(8,128)}) %reduce-scatter.11.cloned.1.call-update) | async-done | bytes 884752 | tf_op jit(solution)/shard_map/reduce_scatter | solution.py:190
  622.1 12.6 all_gather.79
  634.7 96.2 %all-gather.29.cloned.1.call-done = bf16[2304,4608]{1,0:T(8,128)(2,1)} async-done(((bf16[144,4608]{1,0:T(8,128)(2,1)}), bf16[2304,4608]{1,0:T(8,128)(2,1)}) %all-gather.29.cloned.1.call-update) | async-done | bytes 21233680 | tf_op jit(solution)/shard_map/all_gather | solution.py:219
  730.9 14.2 multiply_convert_fusion
  745.1 97.4 %all-gather.31.cloned.1.call-done = bf16[2304,4608]{1,0:T(8,128)(2,1)} async-done(((bf16[144,4608]{1,0:T(8,128)(2,1)}), bf16[2304,4608]{1,0:T(8,128)(2,1)}) %all-gather.31.cloned.1.call-update) | async-done | bytes 21233680 | tf_op jit(solution)/shard_map/all_gather | solution.py:217
  842.6 12.6 fusion.112
  855.2 98.8 %all-gather.33.cloned.1.call-done = bf16[2304,4608]{1,0:T(8,128)(2,1)} async-done(((bf16[144,4608]{1,0:T(8,128)(2,1)}), bf16[2304,4608]{1,0:T(8,128)(2,1)}) %all-gather.33.cloned.1.call-update) | async-done | bytes 21233680 | tf_op jit(solution)/shard_map/all_gather | solution.py:218
  954.0 13.1 convolution_add_fusion.2
  969.6 26.1 reduce-scatter.13.cloned.1.call-done
  1000.9 12.6 all_gather.83
  1013.5 37.5 %all-gather.35.cloned.1.call-done = bf16[2304,1024]{1,0:T(8,128)(2,1)} async-done(((bf16[144,1024]{1,0:T(8,128)(2,1)}), bf16[2304,1024]{1,0:T(8,128)(2,1)}) %all-gather.35.cloned.1.call-update) | async-done | bytes 4718608 | tf_op jit(solution)/shard_map/all_gather | solution.py:216
  1051.0 4.2 convolution_convert_fusion
  1058.8 2.3 convolution_bitcast_fusion.2
  1061.9 3.1 fusion.39
  1067.1 37.7 %all-gather.37.cloned.1.call-done = bf16[2304,1024]{1,0:T(8,128)(2,1)} async-done(((bf16[144,1024]{1,0:T(8,128)(2,1)}), bf16[2304,1024]{1,0:T(8,128)(2,1)}) %all-gather.37.cloned.1.call-update) | async-done | bytes 4718608 | tf_op jit(solution)/shard_map/all_gather | solution.py:213
  1104.8 5.3 fusion.113
  1110.1 37.7 %all-gather.39.cloned.1.call-done = bf16[2304,512]{1,0:T(8,128)(2,1)} async-done(((bf16[144,512]{1,0:T(8,128)(2,1)}), bf16[2304,512]{1,0:T(8,128)(2,1)}) %all-gather.39.cloned.1.call-update) | async-done | bytes 2359312 | tf_op jit(solution)/shard_map/all_gather | solution.py:214
  1147.8 3.2 convolution_add_fusion.1
  1151.1 5.0 fusion.114
  1156.1 8.0 fusion.44
  1164.1 26.9 all-gather.41.cloned.1.call-done
  1191.0 3.5 fusion.1
  1194.6 18.8 pad_maximum_fusion.1
  1213.4 27.7 %copy.111 = f32[2304,3072]{1,0:T(8,128)} copy(f32[2304,3072]{0,1:T(8,128)} %pad_maximum_fusion.1) | data formatting | bytes 56623104
  1242.4 27.8 %fusion.115 = f32[2304,4608]{1,0:T(8,128)} fusion(bf16[192,2304]{1,0:T(8,128)(2,1)S(1)} %copy-done.6, bf16[192,4608]{1,0:T(8,128)(2,1)} %get-tuple-element.129), kind=kOutput, calls=%fused_computation.171 | convolution fusion | flops 4076863488 | bytes 45121536 | tf_op jit(solution)/shard_map/dot_general | solution.py:23
  1270.1 32.5 %fusion.9 = f32[2304,9216]{1,0:T(8,128)} fusion(bf16[192,2304]{1,0:T(8,128)(2,1)S(1)} %copy-done.9, bf16[192,4608]{1,0:T(8,128)(2,1)S(1)} %copy-done.17, bf16[192,4608]{1,0:T(8,128)(2,1)S(1)} %copy-done.18), kind=kOutput, calls=%fused_computation.16 | convolution fusion | flops 8160804864 | bytes 89358336 | tf_op jit(solution)/shard_map/dot_general | solution.py:23
  1302.7 85.9 %pad_maximum_fusion = f32[2304,13824]{1,0:T(8,128)} fusion(f32[2304,4608]{1,0:T(8,128)} %fusion.115, f32[2304,9216]{1,0:T(8,128)} %fusion.9), kind=kLoop, calls=%fused_computation.1 | loop fusion | flops 31850496 | bytes 254803968 | tf_op jit(solution)/shard_map/concatenate | solution.py:233
  1391.0 40.1 %all-reduce.4 = (f32[2304]{0:T(1024)S(1)}, f32[2304]{0:T(1024)S(1)}, f32[2304]{0:T(1024)S(1)}, f32[2304]{0:T(1024)S(1)}) all-reduce(f32[2304]{0:T(1024)S(1)} %get-tuple-element.87, f32[2304]{0:T(1024)S(1)} %copy-done.40, f32[2304]{0:T(1024)S(1)} %copy-done.39, f32[2304]{0:T(1024)S(1)} %copy-done.38), channel_id=1, replica_groups=mesh['fsdp'=16,'tp'=2] {'fsdp','tp'}, use_global_device_ids=true, to_apply=%region_19.20 | all-reduce | flops 9216 | bytes 73728 | tf_op jit(solution)/shard_map/psum | solution.py:323
  1436.0 76.9 %reduce-scatter.19.cloned.1.call-done = f32[144,3072]{1,0:T(8,128)} async-done(((f32[2304,3072]{1,0:T(8,128)}), f32[144,3072]{1,0:T(8,128)}) %reduce-scatter.19.cloned.1.call-update) | async-done | bytes 1769488
  1514.8 2.4 fusion.103
  1517.1 1177.4 %reduce-scatter.17.cloned.1.call-done = f32[144,13824]{1,0:T(8,128)} async-done(((f32[2304,13824]{1,0:T(8,128)}), f32[144,13824]{1,0:T(8,128)}) %reduce-scatter.17.cloned.1.call-update) | async-done | bytes 7962640 | tf_op jit(solution)/shard_map/reduce_scatter | solution.py:232
  2694.6 6.8 fusion.102
  (212 shorter events, 53.8 us)
Async XLA Ops:
  7.2 85.1 %copy-start.47 = (s32[1,9]{1,0:T(1,128)S(1)}, s32[1,9]{1,0:T(1,128)}, u32[]{:S(2)}) copy-start(s32[1,9]{1,0:T(1,128)} %param.15) | copy-start | bytes 112
  7.2 85.8 %all-gather.17.cloned.1.call-start = ((), (), s32[]{:S(2)}) async-start(), calls=%async_computation.7 | async-start | bytes 2506752 | tf_op jit(solution)/shard_map/all_gather | solution.py:126
  7.9 91.1 %all-gather.15.cloned.1.call-start = ((), (), s32[]{:S(2)}) async-start(), calls=%async_computation.6 | async-start | bytes 2506752 | tf_op jit(solution)/shard_map/all_gather | solution.py:127
  8.7 144.5 %all-gather.19.cloned.1.call-start = ((), (), s32[]{:S(2)}) async-start(), calls=%async_computation.8 | async-start | bytes 5013504 | tf_op jit(solution)/shard_map/all_gather | solution.py:125
  9.4 197.6 %all-gather.21.cloned.1.call-start = ((), (), s32[]{:S(2)}) async-start(), calls=%async_computation.9 | async-start | bytes 5013504 | tf_op jit(solution)/shard_map/all_gather | solution.py:128
  10.0 229.3 %reduce-scatter.9.cloned.1.call-start = ((), (), s32[]{:S(2)}) async-start(), calls=%async_computation.10 | async-start | bytes 2654208 | tf_op jit(solution)/shard_map/reduce_scatter | solution.py:178
  79.2 13.7 copy-start.27
  92.5 65.4 %copy-start.29 = (pred[192,192]{0,1:T(8,128)(4,1)}, pred[192,192]{0,1:T(8,128)(4,1)S(1)}, u32[]{:S(2)}) copy-start(pred[192,192]{0,1:T(8,128)(4,1)S(1)} %fusion.77) | copy-start | bytes 110596
  92.9 64.0 %copy-start.10 = (f32[192,128]{1,0:T(8,128)}, f32[192,128]{1,0:T(8,128)S(1)}, u32[]{:S(2)}) copy-start(f32[192,128]{1,0:T(8,128)S(1)} %get-tuple-element.125) | copy-start | bytes 294916
  92.9 64.0 %copy-start.12 = (f32[192,128]{1,0:T(8,128)}, f32[192,128]{1,0:T(8,128)S(1)}, u32[]{:S(2)}) copy-start(f32[192,128]{1,0:T(8,128)S(1)} %get-tuple-element.126) | copy-start | bytes 294916
  101.3 56.6 %copy-start.25 = (bf16[192,2,256]{2,1,0:T(2,128)(2,1)}, bf16[192,2,256]{2,1,0:T(2,128)(2,1)S(1)}, u32[]{:S(2)}) copy-start(bf16[192,2,256]{2,1,0:T(2,128)(2,1)S(1)} %reshape.267) | copy-start | bytes 589828
  101.6 55.7 %copy-start.35 = (bf16[192,2,128]{2,0,1:T(8,128)(2,1)}, bf16[192,2,128]{2,0,1:T(8,128)(2,1)S(1)}, u32[]{:S(2)}) copy-start(bf16[192,2,128]{2,0,1:T(8,128)(2,1)S(1)} %get-tuple-element.121) | copy-start | bytes 294916
  101.6 55.7 %copy-start.37 = (bf16[192,2,128]{2,0,1:T(8,128)(2,1)}, bf16[192,2,128]{2,0,1:T(8,128)(2,1)S(1)}, u32[]{:S(2)}) copy-start(bf16[192,2,128]{2,0,1:T(8,128)(2,1)S(1)} %get-tuple-element.122) | copy-start | bytes 294916
  157.9 54.3 %copy-start.45 = (f32[2,2,192]{2,1,0:T(2,128)}, f32[2,2,192]{2,1,0:T(2,128)S(1)}, u32[]{:S(2)}) copy-start(f32[2,2,192]{2,1,0:T(2,128)S(1)} %log_add_fusion) | copy-start | bytes 9220
  159.2 53.0 %copy-start.19 = (bf16[192,1024]{1,0:T(8,128)(2,1)}, bf16[192,1024]{1,0:T(8,128)(2,1)S(1)}, u32[]{:S(2)}) copy-start(bf16[192,1024]{1,0:T(8,128)(2,1)S(1)} %convert_element_type.109) | copy-start | bytes 1179652
  212.2 28.4 %copy-start.1 = (bf16[96,2304]{1,0:T(8,128)(2,1)S(1)}, bf16[96,2304]{1,0:T(8,128)(2,1)}, u32[]{:S(2)}) copy-start(bf16[96,2304]{1,0:T(8,128)(2,1)} %param.14) | copy-start | bytes 1327108
  212.3 138.5 %all-gather.23.cloned.1.call-start = ((), (), s32[]{:S(2)}) async-start(), calls=%async_computation.11 | async-start | bytes 22560768 | tf_op jit(solution)/shard_map/all_gather | solution.py:133
  212.8 249.6 %all-gather.25.cloned.1.call-start = ((), (), s32[]{:S(2)}) async-start(), calls=%async_computation.12 | async-start | bytes 22560768 | tf_op jit(solution)/shard_map/all_gather | solution.py:134
  213.6 360.4 %all-gather.27.cloned.1.call-start = ((), (), s32[]{:S(2)}) async-start(), calls=%async_computation.13 | async-start | bytes 22560768 | tf_op jit(solution)/shard_map/all_gather | solution.py:135
  214.3 400.8 %reduce-scatter.11.cloned.1.call-start = ((), (), s32[]{:S(2)}) async-start(), calls=%async_computation.14 | async-start | bytes 2654208 | tf_op jit(solution)/shard_map/reduce_scatter | solution.py:190
  214.4 27.8 %copy-start.33 = (f32[2304]{0:T(1024)}, f32[2304]{0:T(1024)S(1)}, u32[]{:S(2)}) copy-start(f32[2304]{0:T(1024)S(1)} %convert_element_type.111) | copy-start | bytes 27652
  255.3 207.1 %copy-start.8 = (bf16[192,2304]{1,0:T(8,128)(2,1)}, bf16[192,2304]{1,0:T(8,128)(2,1)S(1)}, u32[]{:S(2)}) copy-start(bf16[192,2304]{1,0:T(8,128)(2,1)S(1)} %all_gather.74) | copy-start | bytes 2654212
  574.0 42.5 %copy-start.7 = (bf16[96,2304]{1,0:T(8,128)(2,1)S(1)}, bf16[96,2304]{1,0:T(8,128)(2,1)}, u32[]{:S(2)}) copy-start(bf16[96,2304]{1,0:T(8,128)(2,1)} %param.27) | copy-start | bytes 1327108
  586.7 144.3 %all-gather.29.cloned.1.call-start = ((), (), s32[]{:S(2)}) async-start(), calls=%async_computation.15 | async-start | bytes 22560768 | tf_op jit(solution)/shard_map/all_gather | solution.py:219
  620.8 221.8 %all-gather.31.cloned.1.call-start = ((), (), s32[]{:S(2)}) async-start(), calls=%async_computation.16 | async-start | bytes 22560768 | tf_op jit(solution)/shard_map/all_gather | solution.py:217
  621.5 332.5 %all-gather.33.cloned.1.call-start = ((), (), s32[]{:S(2)}) async-start(), calls=%async_computation.17 | async-start | bytes 22560768 | tf_op jit(solution)/shard_map/all_gather | solution.py:218
  622.1 373.6 %reduce-scatter.13.cloned.1.call-start = ((), (), s32[]{:S(2)}) async-start(), calls=%async_computation.18 | async-start | bytes 2654208 | tf_op jit(solution)/shard_map/reduce_scatter | solution.py:242
  634.7 110.4 %copy-start.5 = (bf16[192,2304]{1,0:T(8,128)(2,1)}, bf16[192,2304]{1,0:T(8,128)(2,1)S(1)}, u32[]{:S(2)}) copy-start(bf16[192,2304]{1,0:T(8,128)(2,1)S(1)} %all_gather.79) | copy-start | bytes 2654212
  954.0 41.6 %copy-start.34 = (f32[2304]{0:T(1024)S(1)}, f32[2304]{0:T(1024)}, u32[]{:S(2)}) copy-start(f32[2304]{0:T(1024)} %copy-done.33) | copy-start | bytes 27652
  967.2 30.5 %copy-start = (f32[96,2304]{1,0:T(8,128)S(1)}, f32[96,2304]{1,0:T(8,128)}, u32[]{:S(2)}) copy-start(f32[96,2304]{1,0:T(8,128)} %reduce-scatter.9.cloned.1.call-done) | copy-start | bytes 2654212
  967.2 30.5 %copy-start.44 = (f32[96]{0:T(128)S(1)}, f32[96]{0:T(128)}, u32[]{:S(2)}) copy-start(f32[96]{0:T(128)} %copy-done.43) | copy-start | bytes 1156
  967.2 83.8 %all-gather.35.cloned.1.call-start = ((), (), s32[]{:S(2)}) async-start(), calls=%async_computation.19 | async-start | bytes 5013504 | tf_op jit(solution)/shard_map/all_gather | solution.py:216
  967.8 137.0 %all-gather.37.cloned.1.call-start = ((), (), s32[]{:S(2)}) async-start(), calls=%async_computation.20 | async-start | bytes 5013504 | tf_op jit(solution)/shard_map/all_gather | solution.py:213
  968.4 179.5 %all-gather.39.cloned.1.call-start = ((), (), s32[]{:S(2)}) async-start(), calls=%async_computation.21 | async-start | bytes 2506752 | tf_op jit(solution)/shard_map/all_gather | solution.py:214
  969.0 222.1 %all-gather.41.cloned.1.call-start = ((), (), s32[]{:S(2)}) async-start(), calls=%async_computation.22 | async-start | bytes 2506752 | tf_op jit(solution)/shard_map/all_gather | solution.py:215
  969.5 419.1 %reduce-scatter.15.cloned.1.call-start = ((), (), s32[]{:S(2)}) async-start(), calls=%async_computation.23 | async-start | bytes 1327104 | tf_op jit(solution)/shard_map/reduce_scatter | solution.py:313
  1013.5 43.0 %copy-start.24 = (f32[2,192,192,2]{2,1,3,0:T(8,128)S(1)}, f32[2,192,192,2]{2,1,3,0:T(8,128)}, u32[]{:S(2)}) copy-start(f32[2,192,192,2]{2,1,3,0:T(8,128)} %copy-done.23) | copy-start | bytes 1769476
  1013.5 43.0 %copy-start.30 = (pred[192,192]{0,1:T(8,128)(4,1)S(1)}, pred[192,192]{0,1:T(8,128)(4,1)}, u32[]{:S(2)}) copy-start(pred[192,192]{0,1:T(8,128)(4,1)} %copy-done.29) | copy-start | bytes 110596
  1013.5 43.0 %copy-start.46 = (f32[2,2,192]{2,1,0:T(2,128)S(1)}, f32[2,2,192]{2,1,0:T(2,128)}, u32[]{:S(2)}) copy-start(f32[2,2,192]{2,1,0:T(2,128)} %copy-done.45) | copy-start | bytes 9220
  1013.5 44.1 %copy-start.26 = (bf16[192,2,256]{2,1,0:T(2,128)(2,1)S(1)}, bf16[192,2,256]{2,1,0:T(2,128)(2,1)}, u32[]{:S(2)}) copy-start(bf16[192,2,256]{2,1,0:T(2,128)(2,1)} %copy-done.25) | copy-start | bytes 589828
  1067.1 43.0 %copy-start.21 = (bf16[24,8,4,256]{3,1,2,0:T(8,128)(2,1)}, bf16[24,8,4,256]{3,1,2,0:T(8,128)(2,1)S(1)}, u32[]{:S(2)}) copy-start(bf16[24,8,4,256]{3,1,2,0:T(8,128)(2,1)S(1)} %copy.123) | copy-start | bytes 1179652
  1156.1 34.9 %copy-start.15 = (bf16[2,24,8,256]{3,2,0,1:T(8,128)(2,1)S(1)}, bf16[2,24,8,256]{3,2,0,1:T(8,128)(2,1)}, u32[]{:S(2)}) copy-start(bf16[2,24,8,256]{3,2,0,1:T(8,128)(2,1)} %copy.122) | copy-start | bytes 589828
  1194.6 318.3 %reduce-scatter.19.cloned.1.call-start = ((), (), s32[]{:S(2)}) async-start(), calls=%async_computation.25 | async-start | bytes 30081024
  1241.2 28.9 %copy-start.9 = (bf16[192,2304]{1,0:T(8,128)(2,1)S(1)}, bf16[192,2304]{1,0:T(8,128)(2,1)}, u32[]{:S(2)}) copy-start(bf16[192,2304]{1,0:T(8,128)(2,1)} %copy-done.8) | copy-start | bytes 2654212
  1241.2 28.9 %copy-start.17 = (bf16[192,4608]{1,0:T(8,128)(2,1)S(1)}, bf16[192,4608]{1,0:T(8,128)(2,1)}, u32[]{:S(2)}) copy-start(bf16[192,4608]{1,0:T(8,128)(2,1)} %get-tuple-element.105) | copy-start | bytes 5308420
  1241.2 1453.4 %reduce-scatter.17.cloned.1.call-start = ((), (), s32[]{:S(2)}) async-start(), calls=%async_computation.24 | async-start | bytes 135364608 | tf_op jit(solution)/shard_map/reduce_scatter | solution.py:232
  1242.4 27.8 %copy-start.18 = (bf16[192,4608]{1,0:T(8,128)(2,1)S(1)}, bf16[192,4608]{1,0:T(8,128)(2,1)}, u32[]{:S(2)}) copy-start(bf16[192,4608]{1,0:T(8,128)(2,1)} %get-tuple-element.106) | copy-start | bytes 5308420
  1388.6 45.1 %copy-start.4 = (f32[96,2304]{1,0:T(8,128)S(1)}, f32[96,2304]{1,0:T(8,128)}, u32[]{:S(2)}) copy-start(f32[96,2304]{1,0:T(8,128)} %copy-done.3) | copy-start | bytes 2654212
  (20 other events, 63.2 us)
Sparse Core Ops, SparseCore 0:
  10.3 45.2 all-gather.16
  57.8 41.0 all-gather.14
  101.3 51.8 all-gather.18
  155.3 51.6 all-gather.20
  212.4 26.8 reduce-scatter.8
  240.7 109.9 all-gather.22
  352.4 109.9 all-gather.24
  464.0 109.9 all-gather.26
  586.8 28.2 reduce-scatter.10
  620.9 109.9 all-gather.28
  732.5 109.9 all-gather.30
  844.0 109.9 all-gather.32
  967.3 28.3 reduce-scatter.12
  997.8 53.1 all-gather.34
  1053.1 51.6 all-gather.36
  1106.9 40.8 all-gather.38
  1150.0 41.0 all-gather.40
  1194.7 17.2 reduce-scatter.14
  1241.3 271.4 reduce-scatter.18
  1517.0 1177.5 reduce-scatter.16
where the time goes:
time: 2720 us; the launch traced here: 2710 us
  waiting for transfers between devices  2170 us (80%)
  matrix products  189 us (7%)
  blocking collectives  151 us (6%)
  other arithmetic  127 us (5%)
  local copies, waits for them, and re-layouts  54.2 us (2%)
    reduce_scatter x1, waiting for transfers between devices, shards(): lax.psum_scatter(jnp.concatenate([contract_first(left_rows, gate_up_grad)...  1180 us
    all_gather x1, waiting for transfers between devices, shards(): lax.all_gather(up_weight, 'fsdp', axis=0, tiled=True)  100 us
    all_gather x1, waiting for transfers between devices, shards(): lax.all_gather(held_back[5], 'fsdp', axis=0, tiled=True)  98.8 us
    all_gather x1, waiting for transfers between devices, shards(): lax.all_gather(held_back[4], 'fsdp', axis=0, tiled=True)  97.4 us
    all_gather x1, waiting for transfers between devices, shards(): lax.all_gather(down_weight, 'fsdp', axis=0, tiled=True)  96.9 us
    all_gather x1, waiting for transfers between devices, shards(): lax.all_gather(held_back[6], 'fsdp', axis=0, tiled=True)  96.2 us
    all_gather x1, waiting for transfers between devices, shards(): lax.all_gather(gate_weight, 'fsdp', axis=0, tiled=True)  95.5 us
    concatenate x1, other arithmetic, shards(): jnp.concatenate([contract_first(left_rows, gate_up_grad), contract_first(...  85.9 us
  transfers between devices with their start and end apart: 20, of which 18 were waited for; matrix products, arithmetic and copies ran while one was open for 12% of the time, Pallas kernels for 0%

commit v1 on v0

v1 whole, which is shorter than its diff:
```python
import functools
import math

import jax
import jax.numpy as jnp
from jax import lax
from jax.experimental import pallas as pl
from jax.experimental.pallas import tpu as pltpu
from jax.sharding import PartitionSpec as P

HEAD_SIZE = 256
MESH = pl.DeviceIdType.MESH
ANY = pl.BlockSpec(memory_space=pl.ANY)
LANES = 128

EPSILON = 1e-06
SOFTCAP = 50.0
NEGATIVE = -1e30

KERNEL_FSDP = 16


def place():
    index = lax.axis_index("fsdp")
    return index // 4, (index // 2) % 2, index % 2, lax.axis_index("tp")


def fsdp_index(z, x, c):
    return (z * 2 + x) * 2 + c


def remote(source, target, send_sem, receive_sem, device):
    return pltpu.make_async_remote_copy(
        src_ref=source,
        dst_ref=target,
        send_sem=send_sem,
        recv_sem=receive_sem,
        device_id=device,
        device_id_type=MESH,
    )


def greet(devices):
    barrier = pltpu.get_barrier_semaphore()
    for device in devices:
        pl.semaphore_signal(barrier, inc=1, device_id=device, device_id_type=MESH)
    pl.semaphore_wait(barrier, len(devices))


def greet_line(z, devices, down, up):
    barrier = pltpu.get_barrier_semaphore()
    for device in devices:
        pl.semaphore_signal(barrier, inc=1, device_id=device, device_id_type=MESH)

    @pl.when(z > 0)
    def _():
        pl.semaphore_signal(barrier, inc=1, device_id=down, device_id_type=MESH)

    @pl.when(z < 3)
    def _():
        pl.semaphore_signal(barrier, inc=1, device_id=up, device_id_type=MESH)

    pl.semaphore_wait(barrier, len(devices) + (z + 2) // 3 + (5 - z) // 3)


def stage_through(source, stage, target, sems):
    inward = pltpu.make_async_copy(source, stage, sems.at[0])
    inward.start()

    def finish():
        inward.wait()
        outward = pltpu.make_async_copy(stage, target, sems.at[1])
        outward.start()
        return outward

    return finish


def gather_kernel(block_ref, out_ref, stage, send_sem, receive_sem, local_sem):
    z, x, c, t = place()
    down, up = (fsdp_index(z - 1, x, c), t), (fsdp_index(z + 1, x, c), t)
    across, other = (fsdp_index(z, 1 - x, c), t), (fsdp_index(z, x, 1 - c), t)
    greet_line(z, (across, other), down, up)
    finish_own = stage_through(block_ref, stage, out_ref.at[fsdp_index(z, x, c)], local_sem)

    def send(source, index, send_slot, device):
        return remote(source, out_ref.at[index], send_sem.at[send_slot], receive_sem.at[index], device)

    def arrived(index):
        remote(block_ref, out_ref.at[index], send_sem.at[0], receive_sem.at[index], other).wait_recv()

    own = fsdp_index(z, x, c)

    @pl.when(z < 3)
    def _():
        send(block_ref, own, 0, up).start()

    @pl.when(z > 0)
    def _():
        send(block_ref, own, 1, down).start()

    send(block_ref, own, 2, across).start()
    send(block_ref, own, 3, other).start()
    outward = finish_own()
    for d in (1, 2, 3):

        @pl.when(z >= d)
        def _():
            index = fsdp_index(z - d, x, c)
            base = 4 + 3 * (d - 1)
            arrived(index)

            @pl.when(z < 3)
            def _():
                send(out_ref.at[index], index, base, up).start()

            send(out_ref.at[index], index, base + 1, across).start()
            send(out_ref.at[index], index, base + 2, other).start()

        @pl.when(z + d <= 3)
        def _():
            index = fsdp_index(z + d, x, c)
            base = 13 + 3 * (d - 1)
            arrived(index)

            @pl.when(z > 0)
            def _():
                send(out_ref.at[index], index, base, down).start()

            send(out_ref.at[index], index, base + 1, across).start()
            send(out_ref.at[index], index, base + 2, other).start()

        if d == 1:
            index = fsdp_index(z, 1 - x, c)
            arrived(index)
            send(out_ref.at[index], index, 22, other).start()
    for d in (1, 2, 3):

        @pl.when(z >= d)
        def _():
            index = fsdp_index(z - d, 1 - x, c)
            arrived(index)
            send(out_ref.at[index], index, 22 + d, other).start()

        @pl.when(z + d <= 3)
        def _():
            index = fsdp_index(z + d, 1 - x, c)
            arrived(index)
            send(out_ref.at[index], index, 25 + d, other).start()

    for zi in range(4):
        for xi in range(2):
            arrived(fsdp_index(zi, xi, 1 - c))
    outward.wait()

    def sent(send_slot):
        send(block_ref, own, send_slot, other).wait_send()

    @pl.when(z < 3)
    def _():
        sent(0)

    @pl.when(z > 0)
    def _():
        sent(1)

    sent(2)
    sent(3)
    sent(22)
    for d in (1, 2, 3):

        @pl.when(z >= d)
        def _():
            base = 4 + 3 * (d - 1)

            @pl.when(z < 3)
            def _():
                sent(base)

            sent(base + 1)
            sent(base + 2)
            sent(22 + d)

        @pl.when(z + d <= 3)
        def _():
            base = 13 + 3 * (d - 1)

            @pl.when(z > 0)
            def _():
                sent(base)

            sent(base + 1)
            sent(base + 2)
            sent(25 + d)


def scratch_call(kernel, outputs, scratch, collective_id, *operands):
    return pl.pallas_call(
        kernel,
        out_shape=outputs,
        in_specs=[ANY] * len(operands),
        out_specs=jax.tree.map(lambda _: ANY, outputs),
        scratch_shapes=scratch,
        compiler_params=pltpu.CompilerParams(
            collective_id=collective_id, has_side_effects=True, vmem_limit_bytes=60 * 1024 * 1024
        ),
    )(*operands)


def gather_fsdp(block, collective_id):
    size = lax.axis_size("fsdp")
    if size != KERNEL_FSDP:
        return lax.all_gather(block, "fsdp", axis=0)
    return scratch_call(
        gather_kernel,
        jax.ShapeDtypeStruct((size,) + block.shape, block.dtype),
        [
            pltpu.VMEM(block.shape, block.dtype),
            pltpu.SemaphoreType.DMA((29,)),
            pltpu.SemaphoreType.DMA((size,)),
            pltpu.SemaphoreType.DMA((2,)),
        ],
        collective_id,
        block,
    )


def add_rows(rows, step, target, *sources):
    def body(i, carry):
        at = pl.ds(pl.multiple_of(i * step, step), step)
        total = sources[0][at, :].astype(jnp.float32)
        for source in sources[1:]:
            total = total + source[at, :].astype(jnp.float32)
        target[at, :] = total.astype(target.dtype)
        return carry

    lax.fori_loop(0, rows // step, body, 0)


def scatter_kernel(parts_ref, out_ref, held, from_core, from_across, from_below, from_above, total,
                   send_sem, core_sem, across_sem, below_sem, above_sem, local_sem):
    z, x, c, t = place()
    rows = out_ref.shape[0]
    down, up = (fsdp_index(z - 1, x, c), t), (fsdp_index(z + 1, x, c), t)
    across, other = (fsdp_index(z, 1 - x, c), t), (fsdp_index(z, x, 1 - c), t)
    half = z // 2
    mirrored = z + half * (3 - 2 * z)

    def target_of(i):
        if i == 3:
            return z
        base = 3 - i - (i + mirrored) // 3
        return base + half * (3 - 2 * base)

    local = []
    for k in range(8):
        owner_x = 1 - x if k < 4 else x
        copy = pltpu.make_async_copy(
            parts_ref.at[fsdp_index(target_of(k % 4), owner_x, c)], held.at[k], local_sem.at[k]
        )
        copy.start()
        local.append(copy)
    greet_line(z, (across, other), down, up)
    to_core = []
    for k in range(8):
        owner_x = 1 - x if k < 4 else x
        copy = remote(
            parts_ref.at[fsdp_index(target_of(k % 4), owner_x, 1 - c)],
            from_core.at[k],
            send_sem.at[k],
            core_sem.at[k],
            other,
        )
        copy.start()
        to_core.append(copy)
    to_across = []
    for i in range(4):
        local[i].wait()
        to_core[i].wait_recv()
        add_rows(rows, 16, held.at[i], held.at[i], from_core.at[i])
        copy = remote(held.at[i], from_across.at[i], send_sem.at[8 + i], across_sem.at[i], across)
        copy.start()
        to_across.append(copy)
    for i in range(3):
        k = 4 + i
        target = target_of(i)
        local[k].wait()
        to_core[k].wait_recv()
        to_across[i].wait_recv()

        @pl.when(target > z)
        def _():
            @pl.when(z > 0)
            def _():
                remote(held.at[k], from_below.at[target], send_sem.at[12 + i], below_sem.at[target], up).wait_recv()
                add_rows(rows, 16, held.at[k], held.at[k], from_core.at[k], from_across.at[i], from_below.at[target])

            @pl.when(z == 0)
            def _():
                add_rows(rows, 16, held.at[k], held.at[k], from_core.at[k], from_across.at[i])

            remote(held.at[k], from_below.at[target], send_sem.at[12 + i], below_sem.at[target], up).start()

        @pl.when(target < z)
        def _():
            @pl.when(z < 3)
            def _():
                remote(held.at[k], from_above.at[target], send_sem.at[12 + i], above_sem.at[target], down).wait_recv()
                add_rows(rows, 16, held.at[k], held.at[k], from_core.at[k], from_across.at[i], from_above.at[target])

            @pl.when(z == 3)
            def _():
                add_rows(rows, 16, held.at[k], held.at[k], from_core.at[k], from_across.at[i])

            remote(held.at[k], from_above.at[target], send_sem.at[12 + i], above_sem.at[target], down).start()

    local[7].wait()
    to_core[7].wait_recv()
    to_across[3].wait_recv()
    add_rows(rows, 16, total, held.at[7], from_core.at[7], from_across.at[3])

    @pl.when(z > 0)
    def _():
        remote(held.at[7], from_below.at[z], send_sem.at[12], below_sem.at[z], up).wait_recv()
        add_rows(rows, 16, total, total, from_below.at[z])

    @pl.when(z < 3)
    def _():
        remote(held.at[7], from_above.at[z], send_sem.at[12], above_sem.at[z], down).wait_recv()
        add_rows(rows, 16, total, total, from_above.at[z])

    outward = pltpu.make_async_copy(total, out_ref, local_sem.at[8])
    outward.start()
    for copy in to_core + to_across:
        copy.wait_send()
    for i in range(3):
        remote(held.at[4 + i], from_below.at[0], send_sem.at[12 + i], below_sem.at[0], other).wait_send()
    outward.wait()


def scatter_fsdp(parts, collective_id):
    size, rows, columns = parts.shape
    if size != KERNEL_FSDP:
        return lax.psum_scatter(parts, "fsdp", scatter_dimension=0, tiled=False).astype(jnp.float32)
    block = (rows, columns)
    return scratch_call(
        scatter_kernel,
        jax.ShapeDtypeStruct(block, jnp.float32),
        [
            pltpu.VMEM((8,) + block, parts.dtype),
            pltpu.VMEM((8,) + block, parts.dtype),
            pltpu.VMEM((4,) + block, parts.dtype),
            pltpu.VMEM((4,) + block, parts.dtype),
            pltpu.VMEM((4,) + block, parts.dtype),
            pltpu.VMEM(block, jnp.float32),
            pltpu.SemaphoreType.DMA((15,)),
            pltpu.SemaphoreType.DMA((8,)),
            pltpu.SemaphoreType.DMA((4,)),
            pltpu.SemaphoreType.DMA((4,)),
            pltpu.SemaphoreType.DMA((4,)),
            pltpu.SemaphoreType.DMA((9,)),
        ],
        collective_id,
        parts,
    )


def exchange_kernel(block_ref, out_ref, send_sem, receive_sem):
    index, t = lax.axis_index("fsdp"), lax.axis_index("tp")
    partner = (index, 1 - t)
    greet((partner,))
    copy = remote(block_ref, out_ref, send_sem.at[0], receive_sem.at[0], partner)
    copy.start()
    copy.wait()


def exchange_tp(block, collective_id):
    if lax.axis_size("fsdp") != KERNEL_FSDP:
        return lax.ppermute(block, "tp", [(0, 1), (1, 0)])
    return scratch_call(
        exchange_kernel,
        jax.ShapeDtypeStruct(block.shape, block.dtype),
        [pltpu.SemaphoreType.DMA((1,)), pltpu.SemaphoreType.DMA((1,))],
        collective_id,
        block,
    )


def peer(z, x, c, k):
    kz, kx, kc = k // 4, (k // 2) % 2, k % 2
    high, low = z // 2, z % 2
    high = 1 - high if kz // 2 else high
    low = 1 - low if kz % 2 else low
    return fsdp_index(high * 2 + low, 1 - x if kx else x, 1 - c if kc else c)


def resplit_kernel(parts_ref, out_ref, stage, send_sem, receive_sem, on_sem, pair_sem, local_sem):
    z, x, c, t = place()
    own = fsdp_index(z, x, c)
    partner = (own, 1 - t)
    greet([(peer(z, x, c, k), t) for k in range(1, 16)] + [partner])
    finish_own = stage_through(parts_ref.at[own], stage, out_ref.at[t, own], local_sem)
    onward = [remote(parts_ref.at[own], out_ref.at[t, own], on_sem.at[0], pair_sem.at[0], partner)]
    onward[0].start()
    direct = []
    for k in range(1, 16):
        to = peer(z, x, c, k)
        copy = remote(parts_ref.at[to], out_ref.at[t, own], send_sem.at[k], receive_sem.at[k], (to, t))
        copy.start()
        direct.append(copy)
    outward = finish_own()
    for k in range(1, 16):
        source = peer(z, x, c, k)
        direct[k - 1].wait_recv()
        copy = remote(out_ref.at[t, source], out_ref.at[t, source], on_sem.at[k], pair_sem.at[k], partner)
        copy.start()
        onward.append(copy)
    outward.wait()
    for copy in onward:
        copy.wait_recv()
    for copy in direct + onward:
        copy.wait_send()


def resplit(parts, collective_id):
    size = parts.shape[0]
    if size != KERNEL_FSDP:
        mine = lax.all_to_all(parts, "fsdp", split_axis=0, concat_axis=0, tiled=True)
        return lax.all_gather(mine, "tp", axis=0)
    return scratch_call(
        resplit_kernel,
        jax.ShapeDtypeStruct((2,) + parts.shape, parts.dtype),
        [
            pltpu.VMEM(parts.shape[1:], parts.dtype),
            pltpu.SemaphoreType.DMA((16,)),
            pltpu.SemaphoreType.DMA((16,)),
            pltpu.SemaphoreType.DMA((16,)),
            pltpu.SemaphoreType.DMA((16,)),
            pltpu.SemaphoreType.DMA((2,)),
        ],
        collective_id,
        parts,
    )


def unsplit_kernel(parts_ref, out_ref, held, received, send_sem, receive_sem, on_sem, pair_sem, local_sem):
    z, x, c, t = place()
    own = fsdp_index(z, x, c)
    rows = out_ref.shape[1]
    partner = (own, 1 - t)
    order = list(range(15, -1, -1))
    local = {}
    for k in order:
        copy = pltpu.make_async_copy(parts_ref.at[t, peer(z, x, c, k)], held.at[k], local_sem.at[k])
        copy.start()
        local[k] = copy
    greet([(peer(z, x, c, k), t) for k in range(1, 16)] + [partner])
    pair = {}
    for k in order:
        copy = remote(
            parts_ref.at[1 - t, peer(z, x, c, k)], received.at[k], on_sem.at[k], pair_sem.at[k], partner
        )
        copy.start()
        pair[k] = copy
    direct = []
    for k in order:
        local[k].wait()
        pair[k].wait_recv()
        add_rows(rows, 16, held.at[k], held.at[k], received.at[k])
        if k:
            copy = remote(held.at[k], out_ref.at[own], send_sem.at[k], receive_sem.at[k], (peer(z, x, c, k), t))
            copy.start()
            direct.append(copy)
    keep = pltpu.make_async_copy(held.at[0], out_ref.at[own], local_sem.at[16])
    keep.start()
    for copy in direct:
        copy.wait_recv()
    keep.wait()
    for copy in direct + list(pair.values()):
        copy.wait_send()


def unsplit(parts, collective_id):
    pairs, size, rows, columns = parts.shape
    if size != KERNEL_FSDP:
        mine = lax.psum_scatter(parts, "tp", scatter_dimension=0, tiled=False)
        return lax.all_to_all(mine, "fsdp", split_axis=0, concat_axis=0, tiled=True)
    return scratch_call(
        unsplit_kernel,
        jax.ShapeDtypeStruct((size, rows, columns), parts.dtype),
        [
            pltpu.VMEM((size, rows, columns), parts.dtype),
            pltpu.VMEM((size, rows, columns), parts.dtype),
            pltpu.SemaphoreType.DMA((16,)),
            pltpu.SemaphoreType.DMA((16,)),
            pltpu.SemaphoreType.DMA((16,)),
            pltpu.SemaphoreType.DMA((16,)),
            pltpu.SemaphoreType.DMA((17,)),
        ],
        collective_id,
        parts,
    )


def contract_last(left_rows, right_rows):
    return lax.dot_general(
        left_rows, right_rows, (((1,), (1,)), ((), ())), preferred_element_type=jnp.float32
    )


def contract_first(left_rows, right_rows):
    return lax.dot_general(
        left_rows, right_rows, (((0,), (0,)), ((), ())), preferred_element_type=jnp.float32
    )


def normalize_parts(value_rows):
    inverse = lax.rsqrt(jnp.mean(value_rows * value_rows, axis=-1, keepdims=True) + EPSILON)
    return (value_rows * inverse, inverse)


def norm_backward(unit_rows, inverse, norm_gain, upstream):
    scaled = upstream * norm_gain
    return inverse * (scaled - unit_rows * jnp.mean(scaled * unit_rows, axis=-1, keepdims=True))


def layout(lengths_row, row_index):
    segment_ends = jnp.cumsum(lengths_row)
    segment_starts = segment_ends - lengths_row
    segment = jnp.sum((row_index[:, None] >= segment_ends[None, :]).astype(jnp.int32), axis=1)
    onehot = segment[:, None] == jnp.arange(lengths_row.shape[0], dtype=jnp.int32)[None, :]
    segment_begin = jnp.sum(jnp.where(onehot, segment_starts[None, :], 0), axis=1)
    prompt_shift = jnp.where(segment > 0, lengths_row[0], 0)
    return (segment, row_index - segment_begin + prompt_shift)


def rotary_tables(position):
    frequency = jnp.exp(
        jnp.arange(HEAD_SIZE // 2, dtype=jnp.float32) * (-2.0 * math.log(10000.0) / HEAD_SIZE)
    )
    angles = position.astype(jnp.float32)[:, None] * frequency[None, :]
    return (jnp.cos(angles), jnp.sin(angles))


def apply_rotary(value_rows, cosine_lookup, sine_lookup):
    half_width = value_rows.shape[-1] // 2
    first_half = value_rows[..., :half_width]
    second_half = value_rows[..., half_width:]
    cosine_part = cosine_lookup[:, None, :]
    sine_part = sine_lookup[:, None, :]
    return jnp.concatenate(
        [
            first_half * cosine_part - second_half * sine_part,
            second_half * cosine_part + first_half * sine_part,
        ],
        axis=-1,
    )


def unrotate(value_rows, cosine_lookup, sine_lookup):
    half_width = value_rows.shape[-1] // 2
    first_half = value_rows[..., :half_width]
    second_half = value_rows[..., half_width:]
    cosine_part = cosine_lookup[:, None, :]
    sine_part = sine_lookup[:, None, :]
    return jnp.concatenate(
        [
            first_half * cosine_part + second_half * sine_part,
            second_half * cosine_part - first_half * sine_part,
        ],
        axis=-1,
    )


def visible(segment, row_index):
    same_segment = (segment[:, None] == segment[None, :]) & (
        row_index[None, :] <= row_index[:, None]
    )
    from_prompt = (segment[None, :] == 0) & (segment[:, None] > 0)
    return same_segment | from_prompt


def masked_scores(rotated_query, rotated_key, visible_mask):
    raw_scores = jnp.einsum(
        "qgrd,kgd->grqk", rotated_query, rotated_key, preferred_element_type=jnp.float32
    )
    tanh_value = jnp.tanh(raw_scores * HEAD_SIZE ** (-0.5) / SOFTCAP)
    return (jnp.where(visible_mask[None, None], SOFTCAP * tanh_value, NEGATIVE), tanh_value)


def gelu_product(gate_value, up_value):
    return jax.nn.gelu(gate_value, approximate=True) * up_value


def split_columns(width, size):
    main = width // size // LANES * LANES
    return main, width // size - main


def pack_units(weights, size):
    rows, width = weights[0].shape
    main, rest = split_columns(width, size)
    pieces = []
    if main:
        pieces += [
            jnp.transpose(w[:, : main * size].reshape(rows, size, main), (1, 0, 2)) for w in weights
        ]
    if rest:
        pieces += [
            jnp.transpose(w[:, main * size :].reshape(rows, size, rest), (1, 0, 2)) for w in weights
        ]
    packed = jnp.concatenate(pieces, axis=2)
    return jnp.pad(packed, ((0, 0), (0, 0), (0, -packed.shape[2] % LANES)))


def unpack_units(packed, width, amount):
    size, rows, _ = packed.shape
    main, rest = split_columns(width, size)
    arrays = []
    for i in range(amount):
        pieces = []
        if main:
            piece = packed[:, :, i * main : (i + 1) * main]
            pieces.append(jnp.transpose(piece, (1, 0, 2)).reshape(rows, size * main))
        if rest:
            start = amount * main + i * rest
            piece = packed[:, :, start : start + rest]
            pieces.append(jnp.transpose(piece, (1, 0, 2)).reshape(rows, size * rest))
        arrays.append(jnp.concatenate(pieces, axis=1))
    return arrays


def join_units(halves, width, size, amount):
    main, rest = split_columns(width, size)
    arrays = []
    for i in range(amount):
        start = amount * main + i * rest
        pieces = [half[:, i * main : (i + 1) * main] for half in halves]
        pieces += [half[:, start : start + rest] for half in halves]
        joined = jnp.concatenate(pieces, axis=1)
        arrays.append(jnp.pad(joined, ((0, 0), (0, -joined.shape[1] % LANES))))
    return arrays


def part_units(arrays, width, size, pairs):
    main, rest = split_columns(width, size)
    halves = []
    for t in range(pairs):
        pieces = [array[:, t * main : (t + 1) * main] for array in arrays]
        start = pairs * main + t * rest
        pieces += [array[:, start : start + rest] for array in arrays]
        packed = jnp.concatenate(pieces, axis=1)
        halves.append(jnp.pad(packed, ((0, 0), (0, -packed.shape[1] % LANES))))
    return jnp.stack(halves)


def shards(
    block_input,
    lengths,
    attention_norm_gain,
    attention_post_gain,
    feedforward_norm_gain,
    feedforward_post_gain,
    query_weight,
    key_weight,
    value_weight,
    output_weight,
    gate_weight,
    up_weight,
    down_weight,
    output_cotangent,
):
    low = jnp.bfloat16
    size, pairs = lax.axis_size("fsdp"), lax.axis_size("tp")
    rows_local, width = block_input.shape
    shard_rows, feed_width = gate_weight.shape
    query_width, key_width = query_weight.shape[1], key_weight.shape[1]
    output_start = query_width + 2 * key_width
    gain_start = output_start + query_width
    grouped_rows = rows_local * pairs

    gain_columns = jnp.stack(
        [attention_norm_gain, attention_post_gain, feedforward_norm_gain, feedforward_post_gain],
        axis=1,
    )
    attention_block = jnp.concatenate(
        [
            query_weight,
            key_weight,
            value_weight,
            output_weight,
            jnp.pad(gain_columns, ((0, 0), (0, LANES - 4))),
        ],
        axis=1,
    )
    attention_full = gather_fsdp(attention_block, 1).reshape(size * shard_rows, gain_start + LANES)
    gains = jnp.transpose(attention_full[:, gain_start : gain_start + 4]).astype(jnp.float32)
    gain_one, gain_two, gain_three, gain_four = gains[0], gains[1], gains[2], gains[3]
    other_input = exchange_tp(block_input, 2)

    feed_halves = resplit(pack_units((gate_weight, up_weight, down_weight), size), 3)
    feed_halves = feed_halves.reshape(pairs, size * shard_rows, feed_halves.shape[-1])
    gate_full, up_full, down_full = join_units(feed_halves, feed_width, size, 3)
    units = gate_full.shape[1]

    row_index = (
        jnp.arange(grouped_rows, dtype=jnp.int32) + lax.axis_index("tp") * rows_local
    ) % grouped_rows
    segment, position = layout(lengths[0], row_index)
    cosine_lookup, sine_lookup = rotary_tables(position)
    visible_mask = visible(segment, row_index)
    residual_both = jnp.concatenate([block_input, other_input], axis=0).astype(jnp.float32)
    unit_one_both, inverse_one_both = normalize_parts(residual_both)
    residual = residual_both[:rows_local]
    unit_one, inverse_one = unit_one_both[:rows_local], inverse_one_both[:rows_local]
    normed = (unit_one_both * gain_one).astype(low)
    projected = jnp.dot(
        normed, attention_full[:, :output_start], preferred_element_type=jnp.float32
    )
    query_raw = projected[:, :query_width]
    key_raw = projected[:, query_width : query_width + key_width]
    value_raw = projected[:, query_width + key_width :]
    heads_local = query_width // HEAD_SIZE
    kv_local = key_width // HEAD_SIZE
    repeat_heads = heads_local // kv_local
    rotated_query = apply_rotary(
        query_raw.reshape(grouped_rows, heads_local, HEAD_SIZE), cosine_lookup, sine_lookup
    ).astype(low)
    rotated_query = rotated_query.reshape(grouped_rows, kv_local, repeat_heads, HEAD_SIZE)
    rotated_key = apply_rotary(
        key_raw.reshape(grouped_rows, kv_local, HEAD_SIZE), cosine_lookup, sine_lookup
    ).astype(low)
    value_reduced = value_raw.astype(low).reshape(grouped_rows, kv_local, HEAD_SIZE)
    capped, tanh_value = masked_scores(rotated_query, rotated_key, visible_mask)
    row_peak = jnp.max(capped, axis=-1, keepdims=True)
    exponentials = jnp.exp(capped - row_peak)
    softmax_probs = exponentials / jnp.sum(exponentials, axis=-1, keepdims=True)
    probs_low = softmax_probs.astype(low)
    mixed_heads = jnp.einsum(
        "grqk,kgd->qgrd", probs_low, value_reduced, preferred_element_type=jnp.float32
    )
    attended = mixed_heads.reshape(grouped_rows, heads_local * HEAD_SIZE).astype(low)
    output_full = attention_full[:, output_start:gain_start]
    branch_parts = contract_last(attended, output_full)
    branch_one = branch_parts[:rows_local] + exchange_tp(
        branch_parts[rows_local:].astype(low), 4
    ).astype(jnp.float32)
    unit_two, inverse_two = normalize_parts(branch_one)
    middle = residual + unit_two * gain_two
    unit_three, inverse_three = normalize_parts(middle)

    feed_input = gather_fsdp((unit_three * gain_three).astype(low), 5).reshape(-1, width)
    gate_value = jnp.dot(feed_input, gate_full, preferred_element_type=jnp.float32)
    up_value = jnp.dot(feed_input, up_full, preferred_element_type=jnp.float32)
    hidden = gelu_product(gate_value, up_value).astype(low)
    branch_two = scatter_fsdp(
        contract_last(hidden, down_full).astype(low).reshape(size, rows_local, width), 6
    )
    unit_four, inverse_four = normalize_parts(branch_two)
    block_output = (middle + unit_four * gain_four).astype(low)
    upstream = output_cotangent.astype(jnp.float32)
    gain_four_grad = jnp.sum(upstream * unit_four, axis=0)
    branch_two_grad = norm_backward(unit_four, inverse_four, gain_four, upstream).astype(low)
    feed_grad_rows = gather_fsdp(branch_two_grad, 7).reshape(-1, width)
    hidden_grad = jnp.dot(feed_grad_rows, down_full, preferred_element_type=jnp.float32)
    unused_out, pullback = jax.vjp(gelu_product, gate_value, up_value)
    gate_grad, up_grad = pullback(hidden_grad)
    gate_grad, up_grad = gate_grad.astype(low), up_grad.astype(low)
    normed_three_grad = scatter_fsdp(
        (contract_last(gate_grad, gate_full) + contract_last(up_grad, up_full))
        .astype(low)
        .reshape(size, rows_local, width),
        8,
    )
    feed_grads = part_units(
        (
            contract_first(feed_input, gate_grad),
            contract_first(feed_input, up_grad),
            contract_first(feed_grad_rows, hidden),
        ),
        feed_width,
        size,
        pairs,
    ).astype(low)
    feed_grads = feed_grads.reshape(pairs, size, shard_rows, feed_grads.shape[-1])
    gate_weight_grad, up_weight_grad, down_weight_grad = unpack_units(
        unsplit(feed_grads, 9).astype(jnp.float32), feed_width, 3
    )

    gain_three_grad = jnp.sum(normed_three_grad * unit_three, axis=0)
    middle_grad = upstream + norm_backward(unit_three, inverse_three, gain_three, normed_three_grad)
    gain_two_grad = jnp.sum(middle_grad * unit_two, axis=0)
    branch_one_grad = norm_backward(unit_two, inverse_two, gain_two, middle_grad).astype(low)
    attention_grad_rows = jnp.concatenate(
        [branch_one_grad, exchange_tp(branch_one_grad, 10)], axis=0
    )
    mixed_grad = jnp.dot(
        attention_grad_rows, output_full, preferred_element_type=jnp.float32
    ).astype(low)
    mixed_grad = mixed_grad.reshape(grouped_rows, kv_local, repeat_heads, HEAD_SIZE)
    value_grad = jnp.einsum(
        "grqk,qgrd->kgd", probs_low, mixed_grad, preferred_element_type=jnp.float32
    )
    probs_grad = jnp.einsum(
        "qgrd,kgd->grqk", mixed_grad, value_reduced, preferred_element_type=jnp.float32
    )
    score_grad = softmax_probs * (
        probs_grad - jnp.sum(softmax_probs * probs_grad, axis=-1, keepdims=True)
    )
    raw_grad = (score_grad * (1.0 - tanh_value * tanh_value) * HEAD_SIZE ** (-0.5)).astype(low)
    query_grad = jnp.einsum(
        "grqk,kgd->qgrd", raw_grad, rotated_key, preferred_element_type=jnp.float32
    )
    key_grad = jnp.einsum(
        "grqk,qgrd->kgd", raw_grad, rotated_query, preferred_element_type=jnp.float32
    )
    query_grad = unrotate(
        query_grad.reshape(grouped_rows, heads_local, HEAD_SIZE), cosine_lookup, sine_lookup
    )
    key_grad = unrotate(key_grad, cosine_lookup, sine_lookup)
    projected_grad = jnp.concatenate(
        [
            query_grad.reshape(grouped_rows, heads_local * HEAD_SIZE).astype(low),
            key_grad.reshape(grouped_rows, kv_local * HEAD_SIZE).astype(low),
            value_grad.reshape(grouped_rows, kv_local * HEAD_SIZE).astype(low),
        ],
        axis=1,
    )
    input_parts = contract_last(projected_grad, attention_full[:, :output_start])

    gain_grads = jnp.stack(
        [
            jnp.sum(input_parts * unit_one_both, axis=0),
            gain_two_grad,
            gain_three_grad,
            gain_four_grad,
        ]
    )
    sent = jnp.concatenate(
        [input_parts[rows_local:].astype(low), jnp.pad(gain_grads, ((0, 12), (0, 0))).astype(low)]
    )
    received = exchange_tp(sent, 11).astype(jnp.float32)
    normed_one_grad = input_parts[:rows_local] + received[:rows_local]
    gain_grads = gain_grads + received[rows_local : rows_local + 4]
    input_gradient = middle_grad + norm_backward(unit_one, inverse_one, gain_one, normed_one_grad)

    attention_grads = jnp.concatenate(
        [
            contract_first(normed, projected_grad).astype(low),
            contract_first(attention_grad_rows, attended).astype(low),
            jnp.pad(jnp.transpose(gain_grads), ((0, 0), (0, LANES - 4))).astype(low),
        ],
        axis=1,
    )
    attention_grads = scatter_fsdp(
        attention_grads.reshape(size, shard_rows, gain_start + LANES), 12
    )
    gain_shards = jnp.transpose(attention_grads[:, gain_start : gain_start + 4])
    return (
        block_output,
        input_gradient,
        gain_shards[0],
        gain_shards[1],
        gain_shards[2],
        gain_shards[3],
        attention_grads[:, :query_width],
        attention_grads[:, query_width : query_width + key_width],
        attention_grads[:, query_width + key_width : output_start],
        attention_grads[:, output_start:gain_start],
        gate_weight_grad,
        up_weight_grad,
        down_weight_grad,
    )


def solution(mesh):
    placed = (
        P(("fsdp", "tp"), None),
        P("fsdp", None),
        P("fsdp"),
        P("fsdp"),
        P("fsdp"),
        P("fsdp"),
        P("fsdp", "tp"),
        P("fsdp", "tp"),
        P("fsdp", "tp"),
        P("fsdp", "tp"),
        P("fsdp", "tp"),
        P("fsdp", "tp"),
        P("fsdp", "tp"),
        P(("fsdp", "tp"), None),
    )
    return jax.shard_map(
        shards,
        mesh=mesh,
        in_specs=placed,
        out_specs=(
            P(("fsdp", "tp"), None),
            P(("fsdp", "tp"), None),
            P("fsdp"),
            P("fsdp"),
            P("fsdp"),
            P("fsdp"),
            P("fsdp", "tp"),
            P("fsdp", "tp"),
            P("fsdp", "tp"),
            P("fsdp", "tp"),
            P("fsdp", "tp"),
            P("fsdp", "tp"),
            P("fsdp", "tp"),
        ),
        check_vma=False,
    )
```

time: 2720 us -> 947 us (0.35)
  waiting for transfers between devices: 2170 us -> 0 us
  Pallas kernels: 0 us -> 626 us
  blocking collectives: 151 us -> 0 us
  matrix products: 189 us -> 114 us
  local copies, waits for them, and re-layouts: 54.2 us -> 125 us
  other arithmetic: 127 us -> 69 us
    reduce_scatter x5 -> x0, waiting for transfers between devices: 1260 us -> none  [the longest x1 1180 us: shards(): lax.psum_scatter(jnp.concatenate([contract_first(left_rows, gate_up_grad)...]
    all_gather x14 -> x0, waiting for transfers between devices: 828 us -> none  [the longest x1 100 us: shards(): lax.all_gather(up_weight, 'fsdp', axis=0, tiled=True)]
    pallas_call x0 -> x12, Pallas kernels: none -> 626 us  [scratch_call(): pl.pallas_call(kernel, out_shape=outputs, in_specs=[ANY] * len(operands),...]
    unnamed x21 -> x0, waiting for transfers between devices: 84.8 us -> none
    concatenate x2 -> x5, other arithmetic: 105 us -> 34.6 us  [the longest x1 27 us: shards(): jnp.concatenate([contract_first(normed, projected_grad).astype(low), cont...]
    unnamed x1 -> x0, blocking collectives: 63.9 us -> none
    dot_general x4 -> x5, matrix products: 73.3 us -> 19.8 us  [contract_first(): lax.dot_general(left_rows, right_rows, (((0,), (0,)), ((), ())), preferre...]
    all_gather x4 -> x0, blocking collectives: 47.1 us -> none  [the longest x1 13 us: shards(): feed_input = lax.all_gather(feed_local, 'tp', axis=0, tiled=True)]
  transfers between devices with their start and end apart: 20 -> 0, of which waited for: 18 -> 0; matrix products, arithmetic and copies ran while one was open for 12% -> 0% of each run, Pallas kernels for 0% -> 0%
where the time goes in v1:
time: 947 us; the launch traced here: 937 us
  Pallas kernels  626 us (66%)
  local copies, waits for them, and re-layouts  125 us (13%)
  matrix products  114 us (12%)
  other arithmetic  69 us (7%)
    pallas_call x12, Pallas kernels, scratch_call(): pl.pallas_call(kernel, out_shape=outputs, in_specs=[ANY] * len(operands),...  626 us
    dot_general x5, matrix products, contract_last(): lax.dot_general(left_rows, right_rows, (((1,), (1,)), ((), ())), preferre...  40.9 us
    unnamed x185, local copies, waits for them, and re-layouts  30 us
    concatenate x1, other arithmetic, shards(): jnp.concatenate([contract_first(normed, projected_grad).astype(low), cont...  27 us
    dot_general x5, matrix products, contract_first(): lax.dot_general(left_rows, right_rows, (((0,), (0,)), ((), ())), preferre...  19.8 us
    concatenate x1, local copies, waits for them, and re-layouts, shards(): jnp.concatenate([contract_first(normed, projected_grad).astype(low), cont...  19.3 us

profile of v1, /device:TPU:0, one launch (start us, length us, event | category | flops | bytes accessed | tf_op | source)
XLA Modules:
  0.0 936.5 jit_solution(3917580220537076197)
XLA Ops:
  13.0 13.5 %shard_map.237 = bf16[96,2304]{1,0:T(8,128)(2,1)} custom-call(bf16[96,2304]{1,0:T(8,128)(2,1)} %block_ref.1), custom_call_target="tpu_custom_call" | custom-call | tf_op jit(solution)/shard_map/pallas_call | solution.py:198
  35.0 7.1 concatenate.76
  42.1 4.5 pad.38.parts_ref
  48.0 103.4 %shard_map.241 = bf16[2,16,144,896]{3,2,1,0:T(8,128)(2,1)} custom-call(bf16[16,144,896]{2,1,0:T(8,128)(2,1)} %pad.38.parts_ref), custom_call_target="tpu_custom_call" | custom-call | tf_op jit(solution)/shard_map/pallas_call | solution.py:198
  151.4 3.8 fusion.114
  162.2 88.0 %shard_map.238 = bf16[16,144,3200]{2,1,0:T(8,128)(2,1)} custom-call(bf16[144,3200]{1,0:T(8,128)(2,1)} %constant_dynamic-update-slice_fusion.block_ref), custom_call_target="tpu_custom_call" | custom-call | tf_op jit(solution)/shard_map/pallas_call | solution.py:198
  251.8 5.7 fusion.6
  266.9 4.2 fusion.22
  272.0 12.8 %shard_map.239 = bf16[96,2304]{1,0:T(8,128)(2,1)} custom-call(bf16[96,2304]{1,0:T(8,128)(2,1)} %slice.453.block_ref), custom_call_target="tpu_custom_call" | custom-call | tf_op jit(solution)/shard_map/pallas_call | solution.py:198
  289.2 46.4 %shard_map.240 = bf16[16,96,2304]{2,1,0:T(8,128)(2,1)} custom-call(bf16[96,2304]{1,0:T(8,128)(2,1)} %multiply_convert_fusion.4.block_ref), custom_call_target="tpu_custom_call" | custom-call | tf_op jit(solution)/shard_map/pallas_call | solution.py:198
  335.6 9.0 fusion.110
  344.7 8.3 multiply_convert_fusion.1
  353.1 8.0 convolution_convert_fusion.1
  361.1 47.6 %shard_map.242 = f32[96,2304]{1,0:T(8,128)} custom-call(bf16[16,96,2304]{2,1,0:T(8,128)(2,1)} %bitcast.185), custom_call_target="tpu_custom_call" | custom-call | tf_op jit(solution)/shard_map/pallas_call | solution.py:198
  411.6 2.4 fusion.59
  414.0 42.6 %shard_map.243 = bf16[16,96,2304]{2,1,0:T(8,128)(2,1)} custom-call(bf16[96,2304]{1,0:T(8,128)(2,1)} %get-tuple-element.74.block_ref), custom_call_target="tpu_custom_call" | custom-call | tf_op jit(solution)/shard_map/pallas_call | solution.py:198
  456.6 15.8 %multiply_convert_fusion = (bf16[1536,640]{1,0:T(8,128)(2,1)S(1)}, bf16[1536,640]{1,0:T(8,128)(2,1)}) fusion(f32[1536,640]{1,0:T(8,128)} %copy-done.78, f32[1536,640]{1,0:T(8,128)} %get-tuple-element.91, bf16[1536,2304]{1,0:T(8,128)(2,1)} %bitcast.182, bf16[2304,32]{1,0:T(8,128)(2,1)} %get-tuple-element.51, bf16[2304,32]{1,0:T(8,128)(2,1)} %get-tuple-element.48, ...), kind=kOutput, calls=%fused_computation.43 | convolution fusion | flops 4572610560 | bytes 21528576 | tf_op jit(solution)/shard_map/dot_general | solution.py:765
  472.5 5.4 convolution_convert_fusion.3
  477.9 4.9 convolution_convert_fusion.4
  482.8 4.9 convolution_convert_fusion.5
  494.6 6.7 copy.178
  501.4 4.5 pad.44.clone
  505.8 6.3 copy.179
  512.2 4.7 pad.45.clone
  516.9 6.2 pad_maximum_fusion.parts_ref
  523.1 112.9 %shard_map.248 = bf16[16,144,896]{2,1,0:T(8,128)(2,1)} custom-call(bf16[2,16,144,896]{3,2,1,0:T(8,128)(2,1)} %pad_maximum_fusion.parts_ref), custom_call_target="tpu_custom_call" | custom-call | tf_op jit(solution)/shard_map/pallas_call | solution.py:198
  636.0 2.7 convert_element_type.158
  638.7 2.5 slice_bitcast_fusion.3
  641.1 2.1 slice_bitcast_fusion
  644.9 2.6 copy.157
  648.7 3.4 pad_maximum_fusion.3
  652.1 2.6 copy.154
  656.7 2.6 copy.151
  660.5 1.9 copy.186
  667.8 8.9 fusion.112
  676.7 11.6 %add_convert_fusion = bf16[1536,2304]{1,0:T(8,128)(2,1)} fusion(f32[1536,2304]{1,0:T(8,128)} %fusion.112, bf16[1536,640]{1,0:T(8,128)(2,1)S(1)} %copy-done.73, bf16[2304,32]{1,0:T(8,128)(2,1)S(1)} %copy-done.37, bf16[2304,32]{1,0:T(8,128)(2,1)S(1)} %copy-done.41, bf16[2304,256]{1,0:T(8,128)(2,1)S(1)} %copy-done.24, bf16[2304,256]{1,0:T(8,128)(2,1)S(1)} %copy-done.28), kind=kOutput, calls=%fused_computation.5 | convolution fusion | flops 4556095488 | bytes 25853952 | tf_op jit(solution)/shard_map/dot_general | solution.py:506
  688.3 50.4 %shard_map.244 = f32[96,2304]{1,0:T(8,128)} custom-call(bf16[16,96,2304]{2,1,0:T(8,128)(2,1)} %bitcast.184), custom_call_target="tpu_custom_call" | custom-call | tf_op jit(solution)/shard_map/pallas_call | solution.py:198
  743.3 12.3 %shard_map.245 = bf16[96,2304]{1,0:T(8,128)(2,1)} custom-call(bf16[96,2304]{1,0:T(8,128)(2,1)} %multiply_convert_fusion.3.block_ref), custom_call_target="tpu_custom_call" | custom-call | tf_op jit(solution)/shard_map/pallas_call | solution.py:198
  755.7 3.8 fusion.48
  761.7 2.1 convolution_bitcast_fusion.2
  763.9 3.1 fusion.62
  769.3 8.3 multiply_reduce_fusion
  778.6 13.0 %shard_map.246 = bf16[112,2304]{1,0:T(8,128)(2,1)} custom-call(bf16[112,2304]{1,0:T(8,128)(2,1)} %fusion.70.block_ref), custom_call_target="tpu_custom_call" | custom-call | tf_op jit(solution)/shard_map/pallas_call | solution.py:198
  797.2 3.2 convolution_convert_fusion
  800.5 27.0 %fusion.3 = bf16[2304,3200]{0,1:T(8,128)(2,1)} fusion(bf16[2304,4]{0,1:T(4,128)(2,1)S(1)} %fusion.85, bf16[2304,1024]{0,1:T(8,128)(2,1)S(1)} %convolution_convert_fusion.2, bf16[2304,2048]{0,1:T(8,128)(2,1)S(1)} %convolution_convert_fusion), kind=kLoop, calls=%fused_computation.4 | loop fusion | flops 58982400 | bytes 28919808 | tf_op jit(solution)/shard_map/concatenate | solution.py:847
  827.5 19.3 %copy.147 = bf16[2304,3200]{1,0:T(8,128)(2,1)} copy(bf16[2304,3200]{0,1:T(8,128)(2,1)} %fusion.3) | data formatting | bytes 29491200 | tf_op jit(solution)/shard_map/concatenate | solution.py:847
  846.8 83.5 %shard_map.247 = f32[144,3200]{1,0:T(8,128)} custom-call(bf16[16,144,3200]{2,1,0:T(8,128)(2,1)} %bitcast.161), custom_call_target="tpu_custom_call" | custom-call | tf_op jit(solution)/shard_map/pallas_call | solution.py:198
  933.9 2.4 fusion.119
  (291 shorter events, 85.2 us)
Async XLA Ops:
  1.5 25.0 %copy-start.6 = (bf16[96,2304]{1,0:T(8,128)(2,1)S(1)}, bf16[96,2304]{1,0:T(8,128)(2,1)}, u32[]{:S(2)}) copy-start(bf16[96,2304]{1,0:T(8,128)(2,1)} %block_ref.1) | copy-start | bytes 1327108
  6.0 258.9 %copy-start.64 = (pred[192,192]{0,1:T(8,128)(4,1)}, pred[192,192]{0,1:T(8,128)(4,1)S(1)}, u32[]{:S(2)}) copy-start(pred[192,192]{0,1:T(8,128)(4,1)S(1)} %and_or_fusion) | copy-start | bytes 110596
  7.1 20.6 %copy-start.47 = (bf16[144,1024]{1,0:T(8,128)(2,1)S(1)}, bf16[144,1024]{1,0:T(8,128)(2,1)}, u32[]{:S(2)}) copy-start(bf16[144,1024]{1,0:T(8,128)(2,1)} %param.20) | copy-start | bytes 884740
  9.3 20.8 %copy-start.59 = (bf16[144,512]{1,0:T(8,128)(2,1)S(1)}, bf16[144,512]{1,0:T(8,128)(2,1)}, u32[]{:S(2)}) copy-start(bf16[144,512]{1,0:T(8,128)(2,1)} %param.22) | copy-start | bytes 442372
  9.3 21.4 %copy-start.48 = (bf16[144,1024]{1,0:T(8,128)(2,1)S(1)}, bf16[144,1024]{1,0:T(8,128)(2,1)}, u32[]{:S(2)}) copy-start(bf16[144,1024]{1,0:T(8,128)(2,1)} %param.23) | copy-start | bytes 884740
  9.8 252.4 %copy-start.12 = (f32[192,128]{1,0:T(8,128)}, f32[192,128]{1,0:T(8,128)S(1)}, u32[]{:S(2)}) copy-start(f32[192,128]{1,0:T(8,128)S(1)} %get-tuple-element.86) | copy-start | bytes 294916
  9.8 252.4 %copy-start.14 = (f32[192,128]{1,0:T(8,128)}, f32[192,128]{1,0:T(8,128)S(1)}, u32[]{:S(2)}) copy-start(f32[192,128]{1,0:T(8,128)S(1)} %get-tuple-element.87) | copy-start | bytes 294916
  13.0 19.2 %slice-start.2 = ((bf16[144,4608]{1,0:T(8,128)(2,1)}), bf16[144,4096]{1,0:T(8,128)(2,1)S(1)}, s32[]{:S(2)}) async-start(bf16[144,4608]{1,0:T(8,128)(2,1)} %param.24), calls=%async_computation.2 | async-start | bytes 2359296 | tf_op jit(solution)/shard_map/slice | solution.py:606
  27.7 224.1 %copy-start.65 = (f32[192]{0:T(256)}, f32[192]{0:T(256)S(1)}, u32[]{:S(2)}) copy-start(f32[192]{0:T(256)S(1)} %add_rsqrt_fusion) | copy-start | bytes 2308
  251.8 5.8 copy-start.45
  251.8 34.2 %copy-start.49 = (f32[2304]{0:T(1024)}, f32[2304]{0:T(1024)S(1)}, u32[]{:S(2)}) copy-start(f32[2304]{0:T(1024)S(1)} %get-tuple-element.25) | copy-start | bytes 27652
  251.8 35.9 %copy-start.51 = (f32[2304]{0:T(1024)}, f32[2304]{0:T(1024)S(1)}, u32[]{:S(2)}) copy-start(f32[2304]{0:T(1024)S(1)} %get-tuple-element.24) | copy-start | bytes 27652
  258.8 6.1 copy-start.34
  271.1 16.6 %copy-start.2 = (f32[192,2304]{1,0:T(8,128)}, f32[192,2304]{1,0:T(8,128)S(1)}, u32[]{:S(2)}) copy-start(f32[192,2304]{1,0:T(8,128)S(1)} %fusion.22) | copy-start | bytes 5308420
  289.2 46.4 %copy-start.25 = (bf16[2304,256]{1,0:T(8,128)(2,1)S(1)}, bf16[2304,256]{1,0:T(8,128)(2,1)}, u32[]{:S(2)}) copy-start(bf16[2304,256]{1,0:T(8,128)(2,1)} %get-tuple-element.47) | copy-start | bytes 3538948
  289.2 46.4 %copy-start.29 = (bf16[2304,256]{1,0:T(8,128)(2,1)S(1)}, bf16[2304,256]{1,0:T(8,128)(2,1)}, u32[]{:S(2)}) copy-start(bf16[2304,256]{1,0:T(8,128)(2,1)} %get-tuple-element.44) | copy-start | bytes 3538948
  289.2 46.4 %copy-start.38 = (bf16[2304,32]{1,0:T(8,128)(2,1)S(1)}, bf16[2304,32]{1,0:T(8,128)(2,1)}, u32[]{:S(2)}) copy-start(bf16[2304,32]{1,0:T(8,128)(2,1)} %get-tuple-element.53) | copy-start | bytes 442372
  335.6 9.1 copy-start.4
  335.6 9.1 copy-start.23
  335.6 9.1 copy-start.27
  335.6 9.1 copy-start.36
  335.6 9.1 copy-start.40
  344.7 8.4 copy-start.78
  344.7 8.4 copy-start.31
  344.7 8.4 copy-start.32
  344.7 8.4 copy-start.43
  344.7 8.4 copy-start.44
  353.1 8.0 copy-start.76
  361.1 48.9 %copy-start.10 = (bf16[96,2304]{1,0:T(8,128)(2,1)S(1)}, bf16[96,2304]{1,0:T(8,128)(2,1)}, u32[]{:S(2)}) copy-start(bf16[96,2304]{1,0:T(8,128)(2,1)} %param.27) | copy-start | bytes 1327108
  414.0 63.8 %slice-start = ((s8[7077888]{0:T(1024)(128)(4,1)}), s8[2883584]{0:T(1024)(128)(4,1)S(1)}, s32[]{:S(2)}) async-start(s8[7077888]{0:T(1024)(128)(4,1)} %bitcast.178), calls=%async_computation | async-start | bytes 5767168
  456.6 15.9 %copy-start.5 = (bf16[16,96,2304]{2,1,0:T(8,128)(2,1)S(1)}, bf16[16,96,2304]{2,1,0:T(8,128)(2,1)}, u32[]{:S(2)}) copy-start(bf16[16,96,2304]{2,1,0:T(8,128)(2,1)} %shard_map.243) | copy-start | bytes 21233668
  456.6 15.9 %copy-start.77 = (bf16[1536,640]{1,0:T(8,128)(2,1)S(1)}, bf16[1536,640]{1,0:T(8,128)(2,1)}, u32[]{:S(2)}) copy-start(bf16[1536,640]{1,0:T(8,128)(2,1)} %copy-done.76) | copy-start | bytes 5898244
  456.6 21.2 %slice-start.1 = ((s8[7077888]{0:T(1024)(128)(4,1)}), s8[4194304]{0:T(1024)(128)(4,1)S(1)}, s32[]{:S(2)}) async-start(s8[7077888]{0:T(1024)(128)(4,1)} %bitcast.178), calls=%async_computation.1 | async-start | bytes 8388608
  472.5 5.4 copy-start.72
  667.7 8.9 copy-start.24
  667.7 8.9 copy-start.28
  667.8 8.9 copy-start.37
  667.8 8.9 copy-start.41
  667.8 8.9 copy-start.73
  688.2 50.5 %copy-start.52 = (f32[2304]{0:T(1024)S(1)}, f32[2304]{0:T(1024)}, u32[]{:S(2)}) copy-start(f32[2304]{0:T(1024)} %copy-done.51) | copy-start | bytes 27652
  688.2 50.5 %copy-start.69 = (f32[96]{0:T(128)S(1)}, f32[96]{0:T(128)}, u32[]{:S(2)}) copy-start(f32[96]{0:T(128)} %copy-done.68) | copy-start | bytes 1156
  688.2 52.0 %copy-start.1 = (bf16[96,2304]{1,0:T(8,128)(2,1)S(1)}, bf16[96,2304]{1,0:T(8,128)(2,1)}, u32[]{:S(2)}) copy-start(bf16[96,2304]{1,0:T(8,128)(2,1)} %shard_map.239) | copy-start | bytes 1327108
  688.2 52.0 %copy-start.3 = (f32[192,2304]{1,0:T(8,128)S(1)}, f32[192,2304]{1,0:T(8,128)}, u32[]{:S(2)}) copy-start(f32[192,2304]{1,0:T(8,128)} %copy-done.2) | copy-start | bytes 5308420
  688.2 52.0 %copy-start.50 = (f32[2304]{0:T(1024)S(1)}, f32[2304]{0:T(1024)}, u32[]{:S(2)}) copy-start(f32[2304]{0:T(1024)} %copy-done.49) | copy-start | bytes 27652
  688.2 52.0 %copy-start.71 = (f32[96]{0:T(128)S(1)}, f32[96]{0:T(128)}, u32[]{:S(2)}) copy-start(f32[96]{0:T(128)} %copy-done.70) | copy-start | bytes 1156
  769.3 8.4 copy-start.16
  777.6 15.3 %copy-start.46 = (f32[2304]{0:T(1024)S(1)}, f32[2304]{0:T(1024)}, u32[]{:S(2)}) copy-start(f32[2304]{0:T(1024)} %copy-done.45) | copy-start | bytes 27652
  777.8 16.8 %slice-start.5 = ((f32[192]{0:T(256)}), f32[96]{0:T(128)S(1)}, s32[]{:S(2)}) async-start(f32[192]{0:T(256)} %copy-done.65), calls=%async_computation.5 | async-start | bytes 1024 | tf_op jit(solution)/shard_map/slice | solution.py:715
  (39 other events, 108.0 us)

commit v2 on v1

--- a/solution.py
+++ b/solution.py
@@ -76,122 +76,146 @@
     return finish
 
 
-def gather_kernel(block_ref, out_ref, stage, send_sem, receive_sem, local_sem):
-    z, x, c, t = place()
-    down, up = (fsdp_index(z - 1, x, c), t), (fsdp_index(z + 1, x, c), t)
-    across, other = (fsdp_index(z, 1 - x, c), t), (fsdp_index(z, x, 1 - c), t)
-    greet_line(z, (across, other), down, up)
-    finish_own = stage_through(block_ref, stage, out_ref.at[fsdp_index(z, x, c)], local_sem)
-
-    def send(source, index, send_slot, device):
-        return remote(source, out_ref.at[index], send_sem.at[send_slot], receive_sem.at[index], device)
-
-    def arrived(index):
-        remote(block_ref, out_ref.at[index], send_sem.at[0], receive_sem.at[index], other).wait_recv()
-
-    own = fsdp_index(z, x, c)
-
-    @pl.when(z < 3)
-    def _():
-        send(block_ref, own, 0, up).start()
-
-    @pl.when(z > 0)
-    def _():
-        send(block_ref, own, 1, down).start()
-
-    send(block_ref, own, 2, across).start()
-    send(block_ref, own, 3, other).start()
-    outward = finish_own()
-    for d in (1, 2, 3):
+class Gather:
+    slots = 29
+
+    def __init__(self, block, out_ref, send_sem, receive_sem):
+        self.block, self.out, self.send_sem, self.receive_sem = block, out_ref, send_sem, receive_sem
+        self.z, self.x, self.c, t = place()
+        z, x, c = self.z, self.x, self.c
+        self.own = fsdp_index(z, x, c)
+        self.down, self.up = (fsdp_index(z - 1, x, c), t), (fsdp_index(z + 1, x, c), t)
+        self.across, self.other = (fsdp_index(z, 1 - x, c), t), (fsdp_index(z, x, 1 - c), t)
+
+    def copy(self, source, index, slot, device):
+        return remote(source, self.out.at[index], self.send_sem.at[slot], self.receive_sem.at[index], device)
+
+    def relay(self, index, slot, device):
+        self.copy(self.out.at[index], index, slot, device).start()
+
+    def arrived(self, index):
+        self.copy(self.block, index, 0, self.other).wait_recv()
+
+    def sent(self, slot):
+        self.copy(self.block, self.own, slot, self.other).wait_send()
+
+    def start(self):
+        @pl.when(self.z < 3)
+        def _():
+            self.copy(self.block, self.own, 0, self.up).start()
+
+        @pl.when(self.z > 0)
+        def _():
+            self.copy(self.block, self.own, 1, self.down).start()
+
+        self.copy(self.block, self.own, 2, self.across).start()
+        self.copy(self.block, self.own, 3, self.other).start()
+
+    def line(self, d):
+        z, x, c = self.z, self.x, self.c
 
         @pl.when(z >= d)
         def _():
             index = fsdp_index(z - d, x, c)
             base = 4 + 3 * (d - 1)
-            arrived(index)
+            self.arrived(index)
 
             @pl.when(z < 3)
             def _():
-                send(out_ref.at[index], index, base, up).start()
-
-            send(out_ref.at[index], index, base + 1, across).start()
-            send(out_ref.at[index], index, base + 2, other).start()
+                self.relay(index, base, self.up)
+
+            self.relay(index, base + 1, self.across)
+            self.relay(index, base + 2, self.other)
 
         @pl.when(z + d <= 3)
         def _():
             index = fsdp_index(z + d, x, c)
             base = 13 + 3 * (d - 1)
-            arrived(index)
+            self.arrived(index)
 
             @pl.when(z > 0)
             def _():
-                send(out_ref.at[index], index, base, down).start()
-
-            send(out_ref.at[index], index, base + 1, across).start()
-            send(out_ref.at[index], index, base + 2, other).start()
-
-        if d == 1:
+                self.relay(index, base, self.down)
+
+            self.relay(index, base + 1, self.across)
+            self.relay(index, base + 2, self.other)
+
+    def side(self, d):
+        z, x, c = self.z, self.x, self.c
+        if d == 0:
             index = fsdp_index(z, 1 - x, c)
-            arrived(index)
-            send(out_ref.at[index], index, 22, other).start()
-    for d in (1, 2, 3):
+            self.arrived(index)
+            self.relay(index, 22, self.other)
+            return
 
         @pl.when(z >= d)
         def _():
             index = fsdp_index(z - d, 1 - x, c)
-            arrived(index)
-            send(out_ref.at[index], index, 22 + d, other).start()
+            self.arrived(index)
+            self.relay(index, 22 + d, self.other)
 
         @pl.when(z + d <= 3)
         def _():
             index = fsdp_index(z + d, 1 - x, c)
-            arrived(index)
-            send(out_ref.at[index], index, 25 + d, other).start()
-
-    for zi in range(4):
-        for xi in range(2):
-            arrived(fsdp_index(zi, xi, 1 - c))
+            self.arrived(index)
+            self.relay(index, 25 + d, self.other)
+
+    def finish(self):
+        z = self.z
+        for zi in range(4):
+            for xi in range(2):
+                self.arrived(fsdp_index(zi, xi, 1 - self.c))
+
+        @pl.when(z < 3)
+        def _():
+            self.sent(0)
+
+        @pl.when(z > 0)
+        def _():
+            self.sent(1)
+
+        for slot in (2, 3, 22):
+            self.sent(slot)
+        for d in (1, 2, 3):
+
+            @pl.when(z >= d)
+            def _():
+                base = 4 + 3 * (d - 1)
+
+                @pl.when(z < 3)
+                def _():
+                    self.sent(base)
+
+                for slot in (base + 1, base + 2, 22 + d):
+                    self.sent(slot)
+
+            @pl.when(z + d <= 3)
+            def _():
+                base = 13 + 3 * (d - 1)
+
+                @pl.when(z > 0)
+                def _():
+                    self.sent(base)
+
+                for slot in (base + 1, base + 2, 25 + d):
+                    self.sent(slot)
+
+
+def gather_kernel(block_ref, out_ref, stage, send_sem, receive_sem, local_sem):
+    gather = Gather(block_ref, out_ref, send_sem, receive_sem)
+    greet_line(gather.z, (gather.across, gather.other), gather.down, gather.up)
+    finish_own = stage_through(block_ref, stage, out_ref.at[gather.own], local_sem)
+    gather.start()
+    outward = finish_own()
+    gather.line(1)
+    gather.side(0)
+    gather.line(2)
+    gather.side(1)
+    gather.line(3)
+    gather.side(2)
+    gather.side(3)
+    gather.finish()
     outward.wait()
-
-    def sent(send_slot):
-        send(block_ref, own, send_slot, other).wait_send()
-
-    @pl.when(z < 3)
-    def _():
-        sent(0)
-
-    @pl.when(z > 0)
-    def _():
-        sent(1)
-
-    sent(2)
-    sent(3)
-    sent(22)
-    for d in (1, 2, 3):
-
-        @pl.when(z >= d)
-        def _():
-            base = 4 + 3 * (d - 1)
-
-            @pl.when(z < 3)
-            def _():
-                sent(base)
-
-            sent(base + 1)
-            sent(base + 2)
-            sent(22 + d)
-
-        @pl.when(z + d <= 3)
-        def _():
-            base = 13 + 3 * (d - 1)
-
-            @pl.when(z > 0)
-            def _():
-                sent(base)
-
-            sent(base + 1)
-            sent(base + 2)
-            sent(25 + d)
 
 
 def scratch_call(kernel, outputs, scratch, collective_id, *operands):
@@ -237,8 +261,10 @@
     lax.fori_loop(0, rows // step, body, 0)
 
 
-def scatter_kernel(parts_ref, out_ref, held, from_core, from_across, from_below, from_above, total,
-                   send_sem, core_sem, across_sem, below_sem, above_sem, local_sem):
+def scatter_kernel(amount, *refs):
+    parts_refs, out_ref = refs[:amount], refs[amount]
+    held, from_core, from_across, from_below, from_above, total = refs[amount + 1 : amount + 7]
+    send_sem, core_send_sem, core_sem, across_sem, below_sem, above_sem, local_sem = refs[amount + 7 :]
     z, x, c, t = place()
     rows = out_ref.shape[0]
     down, up = (fsdp_index(z - 1, x, c), t), (fsdp_index(z + 1, x, c), t)
@@ -252,116 +278,134 @@
         base = 3 - i - (i + mirrored) // 3
         return base + half * (3 - 2 * base)
 
+    columns, start = [], 0
+    for ref in parts_refs:
+        columns.append(pl.ds(start, ref.shape[2]))
+        start += ref.shape[2]
     local = []
     for k in range(8):
-        owner_x = 1 - x if k < 4 else x
-        copy = pltpu.make_async_copy(
-            parts_ref.at[fsdp_index(target_of(k % 4), owner_x, c)], held.at[k], local_sem.at[k]
-        )
-        copy.start()
-        local.append(copy)
+        index = fsdp_index(target_of(k % 4), 1 - x if k < 4 else x, c)
+        copies = [
+            pltpu.make_async_copy(ref.at[index], held.at[k, :, at], local_sem.at[k * amount + i])
+            for i, (ref, at) in enumerate(zip(parts_refs, columns))
+        ]
+        for copy in copies:
+            copy.start()
+        local.append(copies)
     greet_line(z, (across, other), down, up)
     to_core = []
     for k in range(8):
-        owner_x = 1 - x if k < 4 else x
-        copy = remote(
-            parts_ref.at[fsdp_index(target_of(k % 4), owner_x, 1 - c)],
-            from_core.at[k],
-            send_sem.at[k],
-            core_sem.at[k],
-            other,
-        )
-        copy.start()
-        to_core.append(copy)
+        index = fsdp_index(target_of(k % 4), 1 - x if k < 4 else x, 1 - c)
+        copies = [
+            remote(
+                ref.at[index],
+                from_core.at[k, :, at],
+                core_send_sem.at[k * amount + i],
+                core_sem.at[k * amount + i],
+                other,
+            )
+            for i, (ref, at) in enumerate(zip(parts_refs, columns))
+        ]
+        for copy in copies:
+            copy.start()
+        to_core.append(copies)
+
+    def both(k):
+        for copy in local[k]:
+            copy.wait()
+        for copy in to_core[k]:
+            copy.wait_recv()
+
     to_across = []
     for i in range(4):
-        local[i].wait()
-        to_core[i].wait_recv()
+        both(i)
         add_rows(rows, 16, held.at[i], held.at[i], from_core.at[i])
-        copy = remote(held.at[i], from_across.at[i], send_sem.at[8 + i], across_sem.at[i], across)
+        copy = remote(held.at[i], from_across.at[i], send_sem.at[3 + i], across_sem.at[i], across)
         copy.start()
         to_across.append(copy)
     for i in range(3):
         k = 4 + i
         target = target_of(i)
-        local[k].wait()
-        to_core[k].wait_recv()
+        both(k)
         to_across[i].wait_recv()
 
         @pl.when(target > z)
         def _():
             @pl.when(z > 0)
             def _():
-                remote(held.at[k], from_below.at[target], send_sem.at[12 + i], below_sem.at[target], up).wait_recv()
+                remote(held.at[k], from_below.at[target], send_sem.at[i], below_sem.at[target], up).wait_recv()
                 add_rows(rows, 16, held.at[k], held.at[k], from_core.at[k], from_across.at[i], from_below.at[target])
 
             @pl.when(z == 0)
             def _():
                 add_rows(rows, 16, held.at[k], held.at[k], from_core.at[k], from_across.at[i])
 
-            remote(held.at[k], from_below.at[target], send_sem.at[12 + i], below_sem.at[target], up).start()
+            remote(held.at[k], from_below.at[target], send_sem.at[i], below_sem.at[target], up).start()
 
         @pl.when(target < z)
         def _():
             @pl.when(z < 3)
             def _():
-                remote(held.at[k], from_above.at[target], send_sem.at[12 + i], above_sem.at[target], down).wait_recv()
+                remote(held.at[k], from_above.at[target], send_sem.at[i], above_sem.at[target], down).wait_recv()
                 add_rows(rows, 16, held.at[k], held.at[k], from_core.at[k], from_across.at[i], from_above.at[target])
 
             @pl.when(z == 3)
             def _():
                 add_rows(rows, 16, held.at[k], held.at[k], from_core.at[k], from_across.at[i])
 
-            remote(held.at[k], from_above.at[target], send_sem.at[12 + i], above_sem.at[target], down).start()
-
-    local[7].wait()
-    to_core[7].wait_recv()
+            remote(held.at[k], from_above.at[target], send_sem.at[i], above_sem.at[target], down).start()
+
+    both(7)
     to_across[3].wait_recv()
     add_rows(rows, 16, total, held.at[7], from_core.at[7], from_across.at[3])
 
     @pl.when(z > 0)
     def _():
-        remote(held.at[7], from_below.at[z], send_sem.at[12], below_sem.at[z], up).wait_recv()
+        remote(held.at[7], from_below.at[z], send_sem.at[0], below_sem.at[z], up).wait_recv()
         add_rows(rows, 16, total, total, from_below.at[z])
 
     @pl.when(z < 3)
     def _():
-        remote(held.at[7], from_above.at[z], send_sem.at[12], above_sem.at[z], down).wait_recv()
+        remote(held.at[7], from_above.at[z], send_sem.at[0], above_sem.at[z], down).wait_recv()
         add_rows(rows, 16, total, total, from_above.at[z])
 
-    outward = pltpu.make_async_copy(total, out_ref, local_sem.at[8])
+    outward = pltpu.make_async_copy(total, out_ref, local_sem.at[8 * amount])
     outward.start()
-    for copy in to_core + to_across:
+    for copy in sum(to_core, to_across):
         copy.wait_send()
     for i in range(3):
-        remote(held.at[4 + i], from_below.at[0], send_sem.at[12 + i], below_sem.at[0], other).wait_send()
+        remote(held.at[4 + i], from_below.at[0], send_sem.at[i], below_sem.at[0], other).wait_send()
     outward.wait()
 
 
 def scatter_fsdp(parts, collective_id):
-    size, rows, columns = parts.shape
+    size, rows, _ = parts[0].shape
+    columns = sum(part.shape[2] for part in parts)
     if size != KERNEL_FSDP:
-        return lax.psum_scatter(parts, "fsdp", scatter_dimension=0, tiled=False).astype(jnp.float32)
-    block = (rows, columns)
+        return lax.psum_scatter(
+            jnp.concatenate(parts, axis=2), "fsdp", scatter_dimension=0, tiled=False
+        ).astype(jnp.float32)
+    block, amount, kind = (rows, columns), len(parts), parts[0].dtype
     return scratch_call(
-        scatter_kernel,
+        functools.partial(scatter_kernel, amount),
         jax.ShapeDtypeStruct(block, jnp.float32),
         [
-            pltpu.VMEM((8,) + block, parts.dtype),
-            pltpu.VMEM((8,) + block, parts.dtype),
-            pltpu.VMEM((4,) + block, parts.dtype),
-            pltpu.VMEM((4,) + block, parts.dtype),
-            pltpu.VMEM((4,) + block, parts.dtype),
+            pltpu.VMEM((8,) + block, kind),
+            pltpu.VMEM((8,) + block, kind),
+            pltpu.VMEM((4,) + block, kind),
+            pltpu.VMEM((4,) + block, kind),
+            pltpu.VMEM((4,) + block, kind),
             pltpu.VMEM(block, jnp.float32),
-            pltpu.SemaphoreType.DMA((15,)),
-            pltpu.SemaphoreType.DMA((8,)),
+            pltpu.SemaphoreType.DMA((7,)),
+            pltpu.SemaphoreType.DMA((8 * amount,)),
+            pltpu.SemaphoreType.DMA((8 * amount,)),
             pltpu.SemaphoreType.DMA((4,)),
             pltpu.SemaphoreType.DMA((4,)),
             pltpu.SemaphoreType.DMA((4,)),
-            pltpu.SemaphoreType.DMA((9,)),
+            pltpu.SemaphoreType.DMA((8 * amount + 1,)),
         ],
         collective_id,
-        parts,
+        *parts,
     )
 
 
@@ -394,112 +438,414 @@
     return fsdp_index(high * 2 + low, 1 - x if kx else x, 1 - c if kc else c)
 
 
-def resplit_kernel(parts_ref, out_ref, stage, send_sem, receive_sem, on_sem, pair_sem, local_sem):
+MAIN = 2 * LANES
+REST = LANES
+FIRST_REST = KERNEL_FSDP * MAIN
+UNITS = 2 * MAIN + REST
+
+
+def main_of(owner):
+    return pl.ds(pl.multiple_of(owner * MAIN, MAIN), MAIN)
+
+
+def rest_of(z):
+    return pl.ds(pl.multiple_of(FIRST_REST + z * REST, REST), REST)
+
+
+def distribute_kernel(
+    rows_ref, query_ref, key_ref, value_ref, output_ref, gain_ref, gate_ref, up_ref, down_ref,
+    attention_ref, partner_ref, feed_ref,
+    stage, feed, zeros,
+    gather_send, gather_receive, local_sem, pair_rows_sem, send_sem, receive_sem, rest_send, rest_receive,
+    on_send, on_receive, rest_on_send, rest_on_receive,
+):
     z, x, c, t = place()
     own = fsdp_index(z, x, c)
     partner = (own, 1 - t)
     greet([(peer(z, x, c, k), t) for k in range(1, 16)] + [partner])
-    finish_own = stage_through(parts_ref.at[own], stage, out_ref.at[t, own], local_sem)
-    onward = [remote(parts_ref.at[own], out_ref.at[t, own], on_sem.at[0], pair_sem.at[0], partner)]
-    onward[0].start()
-    direct = []
-    for k in range(1, 16):
+    rows_copy = remote(rows_ref, partner_ref, pair_rows_sem.at[0], pair_rows_sem.at[1], partner)
+    rows_copy.start()
+    loads, start = [], 0
+    for i, ref in enumerate((query_ref, key_ref, value_ref, output_ref, gain_ref)):
+        loads.append(pltpu.make_async_copy(ref, stage.at[:, pl.ds(start, ref.shape[1])], local_sem.at[i]))
+        start += ref.shape[1]
+    feed_loads = [
+        pltpu.make_async_copy(ref, feed.at[i], local_sem.at[5 + i])
+        for i, ref in enumerate((gate_ref, up_ref, down_ref))
+    ]
+    for copy in loads + feed_loads:
+        copy.start()
+    for copy in loads:
+        copy.wait()
+    gather = Gather(stage, attention_ref, gather_send, gather_receive)
+    gather.start()
+    keep = pltpu.make_async_copy(stage, attention_ref.at[own], local_sem.at[8])
+    keep.start()
+    for copy in feed_loads:
+        copy.wait()
+
+    def main_at(half, source):
+        return feed_ref.at[:, source, :, pl.ds(pl.multiple_of(half * MAIN, MAIN), MAIN)]
+
+    def rest_at(source):
+        return feed_ref.at[:, source, :, pl.ds(2 * MAIN, REST)]
+
+    takes_rest = (c == 0) & (x == t)
+
+    def direct(k):
         to = peer(z, x, c, k)
-        copy = remote(parts_ref.at[to], out_ref.at[t, own], send_sem.at[k], receive_sem.at[k], (to, t))
-        copy.start()
-        direct.append(copy)
-    outward = finish_own()
-    for k in range(1, 16):
-        source = peer(z, x, c, k)
-        direct[k - 1].wait_recv()
-        copy = remote(out_ref.at[t, source], out_ref.at[t, source], on_sem.at[k], pair_sem.at[k], partner)
-        copy.start()
-        onward.append(copy)
-    outward.wait()
-    for copy in onward:
-        copy.wait_recv()
-    for copy in direct + onward:
-        copy.wait_send()
-
-
-def resplit(parts, collective_id):
-    size = parts.shape[0]
+        return remote(feed.at[:, :, main_of(to)], main_at(t, own), send_sem.at[k], receive_sem.at[k], (to, t))
+
+    def rest(dz):
+        to_z = peer(z, x, c, 4 * dz) // 4
+        slot = 4 * dz + 2 * ((x + t) % 2) + c
+        return remote(
+            feed.at[:, :, rest_of(to_z)], rest_at(own), rest_send.at[dz], rest_receive.at[slot], (fsdp_index(to_z, t, 0), t)
+        )
+
+    def onward(k):
+        at = main_at(t, peer(z, x, c, k))
+        return remote(at if k else feed.at[:, :, main_of(own)], at, on_send.at[k], on_receive.at[k], partner)
+
+    def rest_onward(k):
+        at = rest_at(peer(z, x, c, k))
+        return remote(at if k else feed.at[:, :, rest_of(z)], at, rest_on_send.at[k], rest_on_receive.at[k], partner)
+
+    def send(dz):
+        for k in range(4 * dz, 4 * dz + 4):
+            if k:
+                direct(k).start()
+        if dz:
+            rest(dz).start()
+        else:
+
+            @pl.when(jnp.logical_not(takes_rest))
+            def _():
+                rest(0).start()
+
+    def pass_on(dz):
+        for k in range(4 * dz, 4 * dz + 4):
+            if k:
+                direct(k).wait_recv()
+            onward(k).start()
+
+        @pl.when(takes_rest)
+        def _():
+            for k in range(4 * dz, 4 * dz + 4):
+                if k:
+                    remote(
+                        feed.at[:, :, rest_of(0)], rest_at(own), rest_send.at[0], rest_receive.at[k], partner
+                    ).wait_recv()
+                rest_onward(k).start()
+
+    send(0)
+    send(1)
+    keep_main = pltpu.make_async_copy(feed.at[:, :, main_of(own)], main_at(t, own), local_sem.at[9])
+    keep_main.start()
+    keep_rest = pltpu.make_async_copy(feed.at[:, :, rest_of(z)], rest_at(own), local_sem.at[10])
+
+    @pl.when(takes_rest)
+    def _():
+        keep_rest.start()
+
+    fills = [
+        pltpu.make_async_copy(zeros, feed_ref.at[i, :, :, pl.ds(2 * MAIN, REST)], local_sem.at[11 + i])
+        for i in range(3)
+    ]
+
+    @pl.when(c == 1)
+    def _():
+        zeros[...] = jnp.zeros_like(zeros)
+        for copy in fills:
+            copy.start()
+
+    pass_on(0)
+    gather.line(1)
+    gather.side(0)
+    send(2)
+    gather.line(2)
+    send(3)
+    gather.side(1)
+    pass_on(1)
+    gather.line(3)
+    gather.side(2)
+    pass_on(2)
+    gather.side(3)
+    pass_on(3)
+    gather.finish()
+    rows_copy.wait()
+    for k in range(16):
+        onward(k).wait_recv()
+        onward(k).wait_send()
+        if k:
+            direct(k).wait_send()
+
+    @pl.when(jnp.logical_not(takes_rest))
+    def _():
+        rest(0).wait_send()
+
+    for dz in (1, 2, 3):
+        rest(dz).wait_send()
+
+    @pl.when(takes_rest)
+    def _():
+        for k in range(16):
+            rest_onward(k).wait_send()
+        keep_rest.wait()
+
+    @pl.when((c == 0) & (x != t))
+    def _():
+        for k in range(16):
+            rest_onward(k).wait_recv()
+
+    @pl.when(c == 1)
+    def _():
+        for copy in fills:
+            copy.wait()
+
+    keep.wait()
+    keep_main.wait()
+
+
+def distribute(rows, attention, gain_columns, feed, collective_id):
+    size = lax.axis_size("fsdp")
+    shard_rows, feed_width = feed[0].shape
+    columns = sum(w.shape[1] for w in attention) + gain_columns.shape[1]
     if size != KERNEL_FSDP:
-        mine = lax.all_to_all(parts, "fsdp", split_axis=0, concat_axis=0, tiled=True)
-        return lax.all_gather(mine, "tp", axis=0)
-    return scratch_call(
-        resplit_kernel,
-        jax.ShapeDtypeStruct((2,) + parts.shape, parts.dtype),
+        halves = lax.all_to_all(pack_units(feed, size), "fsdp", split_axis=0, concat_axis=0, tiled=True)
+        halves = lax.all_gather(halves, "tp", axis=0)
+        halves = halves.reshape(halves.shape[0], size * shard_rows, halves.shape[-1])
+        return (
+            lax.all_gather(jnp.concatenate((*attention, gain_columns), axis=1), "fsdp", axis=0),
+            lax.ppermute(rows, "tp", [(0, 1), (1, 0)]),
+            jnp.stack(join_units(halves, feed_width, size, 3)),
+        )
+    kind = rows.dtype
+    attention_full, partner_rows, feed_full = scratch_call(
+        distribute_kernel,
+        (
+            jax.ShapeDtypeStruct((size, shard_rows, columns), kind),
+            jax.ShapeDtypeStruct(rows.shape, kind),
+            jax.ShapeDtypeStruct((3, size, shard_rows, UNITS), kind),
+        ),
         [
-            pltpu.VMEM(parts.shape[1:], parts.dtype),
-            pltpu.SemaphoreType.DMA((16,)),
-            pltpu.SemaphoreType.DMA((16,)),
-            pltpu.SemaphoreType.DMA((16,)),
-            pltpu.SemaphoreType.DMA((16,)),
+            pltpu.VMEM((shard_rows, columns), kind),
+            pltpu.VMEM((3, shard_rows, feed_width), kind),
+            pltpu.VMEM((size, shard_rows, REST), kind),
+            pltpu.SemaphoreType.DMA((Gather.slots,)),
+            pltpu.SemaphoreType.DMA((size,)),
+            pltpu.SemaphoreType.DMA((14,)),
             pltpu.SemaphoreType.DMA((2,)),
+            pltpu.SemaphoreType.DMA((size,)),
+            pltpu.SemaphoreType.DMA((size,)),
+            pltpu.SemaphoreType.DMA((4,)),
+            pltpu.SemaphoreType.DMA((size,)),
+            pltpu.SemaphoreType.DMA((size,)),
+            pltpu.SemaphoreType.DMA((size,)),
+            pltpu.SemaphoreType.DMA((size,)),
+            pltpu.SemaphoreType.DMA((size,)),
         ],
         collective_id,
-        parts,
-    )
-
-
-def unsplit_kernel(parts_ref, out_ref, held, received, send_sem, receive_sem, on_sem, pair_sem, local_sem):
+        rows,
+        *attention,
+        gain_columns,
+        *feed,
+    )
+    return attention_full, partner_rows, feed_full.reshape(3, size * shard_rows, UNITS)
+
+
+def collect_kernel(
+    gate_ref, up_ref, down_ref, out_ref,
+    held, received, rest_held, rest_received,
+    local_sem, pair_send, pair_receive, rest_pair_send, rest_pair_receive, send_sem, receive_sem, rest_send, rest_receive,
+):
     z, x, c, t = place()
     own = fsdp_index(z, x, c)
     rows = out_ref.shape[1]
     partner = (own, 1 - t)
-    order = list(range(15, -1, -1))
-    local = {}
-    for k in order:
-        copy = pltpu.make_async_copy(parts_ref.at[t, peer(z, x, c, k)], held.at[k], local_sem.at[k])
-        copy.start()
-        local[k] = copy
+    parts = (gate_ref, up_ref, down_ref)
+    order = (3, 2, 1, 0)
+    takes_rest = (c == 0) & (x == t)
+    gives_rest = (c == 0) & (x != t)
+
+    def plane(dz):
+        return pl.ds(peer(z, x, c, 4 * dz) // 4 * 4, 4)
+
+    def half(which):
+        return pl.ds(pl.multiple_of(which * MAIN, MAIN), MAIN)
+
+    rest_columns = pl.ds(2 * MAIN, REST)
+
+    def load(dz, i):
+        return pltpu.make_async_copy(parts[i].at[plane(dz), :, half(t)], held.at[dz, i], local_sem.at[3 * dz + i])
+
+    def rest_load(dz, i):
+        return pltpu.make_async_copy(
+            parts[i].at[plane(dz), :, rest_columns], rest_held.at[dz, i], local_sem.at[12 + 3 * dz + i]
+        )
+
+    def pair(dz, i):
+        slot = 3 * dz + i
+        return remote(
+            parts[i].at[plane(dz), :, half(1 - t)], received.at[dz, i], pair_send.at[slot], pair_receive.at[slot], partner
+        )
+
+    def rest_pair(dz, i):
+        slot = 3 * dz + i
+        return remote(
+            parts[i].at[plane(dz), :, rest_columns],
+            rest_received.at[dz, i],
+            rest_pair_send.at[slot],
+            rest_pair_receive.at[slot],
+            partner,
+        )
+
+    def spot(k):
+        return peer(z, x, c, k) % 4
+
+    def direct(k):
+        return remote(
+            held.at[k // 4, :, spot(k)], out_ref.at[:, :, main_of(own)], send_sem.at[k], receive_sem.at[k], (peer(z, x, c, k), t)
+        )
+
+    def rest_direct(k):
+        return remote(
+            rest_held.at[k // 4, :, spot(k)],
+            out_ref.at[:, :, rest_of(z)],
+            rest_send.at[k],
+            rest_receive.at[z],
+            (peer(z, x, c, k), t),
+        )
+
+    def add(target, source):
+        def body(j, carry):
+            i, at = j // 4, j % 4
+            total = target[i, at].astype(jnp.float32) + source[i, at].astype(jnp.float32)
+            target[i, at] = total.astype(target.dtype)
+            return carry
+
+        lax.fori_loop(0, 12, body, 0)
+
+    for dz in order:
+        for i in range(3):
+            load(dz, i).start()
+
+    @pl.when(takes_rest)
+    def _():
+        for dz in order:
+            for i in range(3):
+                rest_load(dz, i).start()
+
     greet([(peer(z, x, c, k), t) for k in range(1, 16)] + [partner])
-    pair = {}
-    for k in order:
-        copy = remote(
-            parts_ref.at[1 - t, peer(z, x, c, k)], received.at[k], on_sem.at[k], pair_sem.at[k], partner
-        )
-        copy.start()
-        pair[k] = copy
-    direct = []
-    for k in order:
-        local[k].wait()
-        pair[k].wait_recv()
-        add_rows(rows, 16, held.at[k], held.at[k], received.at[k])
-        if k:
-            copy = remote(held.at[k], out_ref.at[own], send_sem.at[k], receive_sem.at[k], (peer(z, x, c, k), t))
-            copy.start()
-            direct.append(copy)
-    keep = pltpu.make_async_copy(held.at[0], out_ref.at[own], local_sem.at[16])
+    for dz in order:
+        for i in range(3):
+            pair(dz, i).start()
+
+        @pl.when(gives_rest)
+        def _():
+            for i in range(3):
+                rest_pair(dz, i).start()
+
+    for dz in order:
+        for i in range(3):
+            load(dz, i).wait()
+            pair(dz, i).wait_recv()
+        add(held.at[dz], received.at[dz])
+        for k in range(4 * dz, 4 * dz + 4):
+            if k:
+                direct(k).start()
+
+        @pl.when(takes_rest)
+        def _():
+            for i in range(3):
+                rest_load(dz, i).wait()
+                rest_pair(dz, i).wait_recv()
+            add(rest_held.at[dz], rest_received.at[dz])
+            for k in range(4 * dz, 4 * dz + 4):
+                if k:
+                    rest_direct(k).start()
+
+    keep = pltpu.make_async_copy(held.at[0, :, spot(0)], out_ref.at[:, :, main_of(own)], local_sem.at[24])
     keep.start()
-    for copy in direct:
-        copy.wait_recv()
+    keep_rest = pltpu.make_async_copy(rest_held.at[0, :, spot(0)], out_ref.at[:, :, rest_of(z)], local_sem.at[25])
+
+    @pl.when(takes_rest)
+    def _():
+        keep_rest.start()
+
+    for k in range(1, 16):
+        direct(k).wait_recv()
+
+    for dz in range(4):
+        from_z = peer(z, x, c, 4 * dz) // 4
+
+        def arrived():
+            remote(
+                rest_held.at[0, :, 0], out_ref.at[:, :, rest_of(from_z)], rest_send.at[0], rest_receive.at[from_z], partner
+            ).wait_recv()
+
+        if dz:
+            arrived()
+        else:
+
+            @pl.when(jnp.logical_not(takes_rest))
+            def _():
+                arrived()
+
+    for k in range(1, 16):
+        direct(k).wait_send()
+    for dz in order:
+        for i in range(3):
+            pair(dz, i).wait_send()
+
+    @pl.when(gives_rest)
+    def _():
+        for dz in order:
+            for i in range(3):
+                rest_pair(dz, i).wait_send()
+
+    @pl.when(takes_rest)
+    def _():
+        for k in range(1, 16):
+            rest_direct(k).wait_send()
+        keep_rest.wait()
+
     keep.wait()
-    for copy in direct + list(pair.values()):
-        copy.wait_send()
-
-
-def unsplit(parts, collective_id):
-    pairs, size, rows, columns = parts.shape
+
+
+def collect(gradients, feed_width, collective_id):
+    size, pairs = lax.axis_size("fsdp"), lax.axis_size("tp")
+    shard_rows = gradients[0].shape[0] // size
     if size != KERNEL_FSDP:
-        mine = lax.psum_scatter(parts, "tp", scatter_dimension=0, tiled=False)
-        return lax.all_to_all(mine, "fsdp", split_axis=0, concat_axis=0, tiled=True)
-    return scratch_call(
-        unsplit_kernel,
-        jax.ShapeDtypeStruct((size, rows, columns), parts.dtype),
+        packed = part_units(gradients, feed_width, size, pairs)
+        mine = lax.psum_scatter(packed, "tp", scatter_dimension=0, tiled=False)
+        mine = mine.reshape(size, shard_rows, mine.shape[-1])
+        mine = lax.all_to_all(mine, "fsdp", split_axis=0, concat_axis=0, tiled=True)
+        return [g.astype(jnp.float32) for g in unpack_units(mine, feed_width, 3)]
+    kind = gradients[0].dtype
+    main, rest = (4, 3, 4, shard_rows, MAIN), (4, 3, 4, shard_rows, REST)
+    out = scratch_call(
+        collect_kernel,
+        jax.ShapeDtypeStruct((3, shard_rows, feed_width), kind),
         [
-            pltpu.VMEM((size, rows, columns), parts.dtype),
-            pltpu.VMEM((size, rows, columns), parts.dtype),
-            pltpu.SemaphoreType.DMA((16,)),
-            pltpu.SemaphoreType.DMA((16,)),
-            pltpu.SemaphoreType.DMA((16,)),
-            pltpu.SemaphoreType.DMA((16,)),
-            pltpu.SemaphoreType.DMA((17,)),
+            pltpu.VMEM(main, kind),
+            pltpu.VMEM(main, kind),
+            pltpu.VMEM(rest, kind),
+            pltpu.VMEM(rest, kind),
+            pltpu.SemaphoreType.DMA((26,)),
+            pltpu.SemaphoreType.DMA((12,)),
+            pltpu.SemaphoreType.DMA((12,)),
+            pltpu.SemaphoreType.DMA((12,)),
+            pltpu.SemaphoreType.DMA((12,)),
+            pltpu.SemaphoreType.DMA((size,)),
+            pltpu.SemaphoreType.DMA((size,)),
+            pltpu.SemaphoreType.DMA((size,)),
+            pltpu.SemaphoreType.DMA((4,)),
         ],
         collective_id,
-        parts,
-    )
+        *[g.reshape(size, shard_rows, UNITS) for g in gradients],
+    )
+    return [out[i].astype(jnp.float32) for i in range(3)]
 
 
 def contract_last(left_rows, right_rows):
@@ -683,25 +1029,17 @@
         [attention_norm_gain, attention_post_gain, feedforward_norm_gain, feedforward_post_gain],
         axis=1,
     )
-    attention_block = jnp.concatenate(
-        [
-            query_weight,
-            key_weight,
-            value_weight,
-            output_weight,
-            jnp.pad(gain_columns, ((0, 0), (0, LANES - 4))),
-        ],
-        axis=1,
-    )
-    attention_full = gather_fsdp(attention_block, 1).reshape(size * shard_rows, gain_start + LANES)
+    attention_full, other_input, feed_full = distribute(
+        block_input,
+        (query_weight, key_weight, value_weight, output_weight),
+        jnp.pad(gain_columns, ((0, 0), (0, LANES - 4))),
+        (gate_weight, up_weight, down_weight),
+        1,
+    )
+    attention_full = attention_full.reshape(size * shard_rows, gain_start + LANES)
     gains = jnp.transpose(attention_full[:, gain_start : gain_start + 4]).astype(jnp.float32)
     gain_one, gain_two, gain_three, gain_four = gains[0], gains[1], gains[2], gains[3]
-    other_input = exchange_tp(block_input, 2)
-
-    feed_halves = resplit(pack_units((gate_weight, up_weight, down_weight), size), 3)
-    feed_halves = feed_halves.reshape(pairs, size * shard_rows, feed_halves.shape[-1])
-    gate_full, up_full, down_full = join_units(feed_halves, feed_width, size, 3)
-    units = gate_full.shape[1]
+    gate_full, up_full, down_full = feed_full[0], feed_full[1], feed_full[2]
 
     row_index = (
         jnp.arange(grouped_rows, dtype=jnp.int32) + lax.axis_index("tp") * rows_local
@@ -754,7 +1092,7 @@
     up_value = jnp.dot(feed_input, up_full, preferred_element_type=jnp.float32)
     hidden = gelu_product(gate_value, up_value).astype(low)
     branch_two = scatter_fsdp(
-        contract_last(hidden, down_full).astype(low).reshape(size, rows_local, width), 6
+        (contract_last(hidden, down_full).astype(low).reshape(size, rows_local, width),), 6
     )
     unit_four, inverse_four = normalize_parts(branch_two)
     block_output = (middle + unit_four * gain_four).astype(low)
@@ -766,25 +1104,18 @@
     unused_out, pullback = jax.vjp(gelu_product, gate_value, up_value)
     gate_grad, up_grad = pullback(hidden_grad)
     gate_grad, up_grad = gate_grad.astype(low), up_grad.astype(low)
+    normed_three_parts = contract_last(gate_grad, gate_full) + contract_last(up_grad, up_full)
     normed_three_grad = scatter_fsdp(
-        (contract_last(gate_grad, gate_full) + contract_last(up_grad, up_full))
-        .astype(low)
-        .reshape(size, rows_local, width),
-        8,
-    )
-    feed_grads = part_units(
+        (normed_three_parts.astype(low).reshape(size, rows_local, width),), 8
+    )
+    gate_weight_grad, up_weight_grad, down_weight_grad = collect(
         (
-            contract_first(feed_input, gate_grad),
-            contract_first(feed_input, up_grad),
-            contract_first(feed_grad_rows, hidden),
+            contract_first(feed_input, gate_grad).astype(low),
+            contract_first(feed_input, up_grad).astype(low),
+            contract_first(feed_grad_rows, hidden).astype(low),
         ),
         feed_width,
-        size,
-        pairs,
-    ).astype(low)
-    feed_grads = feed_grads.reshape(pairs, size, shard_rows, feed_grads.shape[-1])
-    gate_weight_grad, up_weight_grad, down_weight_grad = unpack_units(
-        unsplit(feed_grads, 9).astype(jnp.float32), feed_width, 3
+        9,
     )
 
     gain_three_grad = jnp.sum(normed_three_grad * unit_three, axis=0)
@@ -844,16 +1175,16 @@
     gain_grads = gain_grads + received[rows_local : rows_local + 4]
     input_gradient = middle_grad + norm_backward(unit_one, inverse_one, gain_one, normed_one_grad)
 
-    attention_grads = jnp.concatenate(
+    attention_grads = scatter_fsdp(
         [
-            contract_first(normed, projected_grad).astype(low),
-            contract_first(attention_grad_rows, attended).astype(low),
-            jnp.pad(jnp.transpose(gain_grads), ((0, 0), (0, LANES - 4))).astype(low),
+            part.astype(low).reshape(size, shard_rows, part.shape[1])
+            for part in (
+                contract_first(normed, projected_grad),
+                contract_first(attention_grad_rows, attended),
+                jnp.pad(jnp.transpose(gain_grads), ((0, 0), (0, LANES - 4))),
+            )
         ],
-        axis=1,
-    )
-    attention_grads = scatter_fsdp(
-        attention_grads.reshape(size, shard_rows, gain_start + LANES), 12
+        12,
     )
     gain_shards = jnp.transpose(attention_grads[:, gain_start : gain_start + 4])
     return (

time: 947 us -> 836 us (0.88)
  local copies, waits for them, and re-layouts: 125 us -> 26.4 us
  other arithmetic: 69 us -> 31.2 us
  matrix products: 114 us -> 129 us
  Pallas kernels: 626 us -> 639 us
    concatenate x4 -> x0, other arithmetic: 33.8 us -> none  [the longest x1 27 us: shards(): jnp.concatenate([contract_first(normed, projected_grad).astype(low), cont...]
    concatenate x4 -> x0, local copies, waits for them, and re-layouts: 27.8 us -> none  [the longest x1 19.3 us: shards(): jnp.concatenate([contract_first(normed, projected_grad).astype(low), cont...]
    unnamed x185 -> x109, local copies, waits for them, and re-layouts: 30 us -> 5.04 us
    dot_general x5, matrix products: 19.8 us -> 34.6 us  [contract_first(): lax.dot_general(left_rows, right_rows, (((0,), (0,)), ((), ())), preferre...]
    pallas_call x12 -> x10, Pallas kernels: 626 us -> 639 us  [scratch_call(): pl.pallas_call(kernel, out_shape=outputs, in_specs=[ANY] * len(operands),...]
    pad x3 -> x2, local copies, waits for them, and re-layouts: 13.7 us -> 1.57 us  [the longest x1 0.93 us: shards(): jnp.pad(jnp.transpose(gain_grads), ((0, 0), (0, LANES - 4)))]
    transpose x5 -> x0, local copies, waits for them, and re-layouts: 11.6 us -> none  [the longest x4 10.4 us: unpack_units(): pieces.append(jnp.transpose(piece, (1, 0, 2)).reshape(rows, size * rest))]
    reshape x10 -> x0, local copies, waits for them, and re-layouts: 11.4 us -> none  [the longest x3 4.34 us: unpack_units(): pieces.append(jnp.transpose(piece, (1, 0, 2)).reshape(rows, size * rest))]
where the time goes in v2:
time: 836 us; the launch traced here: 828 us
  Pallas kernels  639 us (76%)
  matrix products  129 us (15%)
  other arithmetic  31.2 us (4%)
  local copies, waits for them, and re-layouts  26.4 us (3%)
    pallas_call x10, Pallas kernels, scratch_call(): pl.pallas_call(kernel, out_shape=outputs, in_specs=[ANY] * len(operands),...  639 us
    dot_general x5, matrix products, contract_last(): lax.dot_general(left_rows, right_rows, (((1,), (1,)), ((), ())), preferre...  39.8 us
    dot_general x5, matrix products, contract_first(): lax.dot_general(left_rows, right_rows, (((0,), (0,)), ((), ())), preferre...  34.6 us
    dot_general x1, matrix products, shards(): jnp.dot(feed_grad_rows, down_full, preferred_element_type=jnp.float32)  21.1 us

profile of v2, /device:TPU:0, one launch (start us, length us, event | category | flops | bytes accessed | tf_op | source)
XLA Modules:
  0.0 827.8 jit_solution(9941405850084423046)
XLA Ops:
  7.1 202.5 %shard_map.237 = (bf16[16,144,3200]{2,1,0:T(8,128)(2,1)}, bf16[96,2304]{1,0:T(8,128)(2,1)}, bf16[3,16,144,640]{3,2,1,0:T(8,128)(2,1)}) custom-call(bf16[96,2304]{1,0:T(8,128)(2,1)} %rows_ref.1, bf16[144,1024]{1,0:T(8,128)(2,1)} %query_ref.1, bf16[144,512]{1,0:T(8,128)(2,1)} %key_ref.1, bf16[144,512]{1,0:T(8,128)(2,1)} %value_ref.1, ...), custom_call_target="tpu_custom_call" | custom-call | tf_op jit(solution)/shard_map/pallas_call | solution.py:222
  209.7 1.3 multiply_reduce_fusion.1
  212.6 5.7 fusion.4
  219.6 1.2 slice.189
  222.0 1.2 fusion.23
  223.2 1.3 fusion.86
  226.0 4.2 fusion.8
  231.0 9.1 %shard_map.238 = bf16[96,2304]{1,0:T(8,128)(2,1)} custom-call(bf16[96,2304]{1,0:T(8,128)(2,1)} %slice.277.block_ref), custom_call_target="tpu_custom_call" | custom-call | tf_op jit(solution)/shard_map/pallas_call | solution.py:222
  240.1 1.3 multiply_reduce_fusion.9
  242.9 47.6 %shard_map.239 = bf16[16,96,2304]{2,1,0:T(8,128)(2,1)} custom-call(bf16[96,2304]{1,0:T(8,128)(2,1)} %multiply_convert_fusion.4.block_ref), custom_call_target="tpu_custom_call" | custom-call | tf_op jit(solution)/shard_map/pallas_call | solution.py:222
  290.5 4.1 fusion.81
  294.7 2.5 copy-done.1
  297.2 5.8 fusion.87
  303.0 8.3 %multiply_convert_fusion.1 = (bf16[1536,640]{1,0:T(8,128)(2,1)S(1)}, f32[1536,640]{1,0:T(8,128)}) fusion(f32[1536,640]{1,0:T(8,128)S(1)} %fusion.87, bf16[1536,2304]{1,0:T(8,128)(2,1)S(1)} %bitcast.139, bf16[2304,640]{1,0:T(8,128)(2,1)S(1)} %bitcast.148), kind=kOutput, calls=%fused_computation.27 | convolution fusion | flops 4539678720 | bytes 19857408 | tf_op jit(solution)/shard_map/dot_general | solution.py:1092
  311.3 7.7 convolution_convert_fusion.1
  319.0 48.4 %shard_map.240 = f32[96,2304]{1,0:T(8,128)} custom-call(bf16[16,96,2304]{2,1,0:T(8,128)(2,1)} %bitcast.146), custom_call_target="tpu_custom_call" | custom-call | tf_op jit(solution)/shard_map/pallas_call | solution.py:222
  367.4 1.3 multiply_reduce_fusion.7
  368.8 1.5 fusion.37
  370.9 2.4 fusion.36
  373.3 43.1 %shard_map.241 = bf16[16,96,2304]{2,1,0:T(8,128)(2,1)} custom-call(bf16[96,2304]{1,0:T(8,128)(2,1)} %get-tuple-element.54.block_ref), custom_call_target="tpu_custom_call" | custom-call | tf_op jit(solution)/shard_map/pallas_call | solution.py:222
  416.4 21.1 %multiply_convert_fusion = (bf16[1536,640]{1,0:T(8,128)(2,1)S(1)}, bf16[1536,640]{1,0:T(8,128)(2,1)S(1)}) fusion(f32[1536,640]{1,0:T(8,128)} %copy-done.43, f32[1536,640]{1,0:T(8,128)} %get-tuple-element.71, bf16[1536,2304]{1,0:T(8,128)(2,1)} %bitcast.143, bf16[2304,640]{1,0:T(8,128)(2,1)} %bitcast.153), kind=kOutput, calls=%fused_computation.26 | convolution fusion | flops 4553441280 | bytes 21823488 | tf_op jit(solution)/shard_map/dot_general | solution.py:1103
  437.6 7.2 convolution_convert_fusion.3
  444.8 10.2 %convolution_convert_fusion.4 = bf16[2304,640]{1,0:T(8,128)(2,1)} fusion(bf16[1536,2304]{1,0:T(8,128)(2,1)} %bitcast.137, bf16[1536,640]{1,0:T(8,128)(2,1)S(1)} %get-tuple-element.41), kind=kOutput, calls=%fused_computation.13 | convolution fusion | flops 4531322880 | bytes 11993088 | tf_op jit(solution)/shard_map/dot_general | solution.py:858
  455.1 7.2 convolution_convert_fusion.5
  462.2 120.4 %shard_map.246 = bf16[3,144,4608]{2,1,0:T(8,128)(2,1)} custom-call(bf16[16,144,640]{2,1,0:T(8,128)(2,1)} %bitcast.156, bf16[16,144,640]{2,1,0:T(8,128)(2,1)} %bitcast.155, bf16[16,144,640]{2,1,0:T(8,128)(2,1)} %bitcast.154), custom_call_target="tpu_custom_call" | custom-call | tf_op jit(solution)/shard_map/pallas_call | solution.py:222
  582.7 5.8 bitcast_convert_fusion
  588.5 8.7 %fusion.88 = f32[1536,2304]{1,0:T(8,128)} fusion(bf16[1536,640]{1,0:T(8,128)(2,1)S(1)} %copy-done.42, bf16[2304,640]{1,0:T(8,128)(2,1)S(1)} %bitcast.151), kind=kOutput, calls=%fused_computation.183 | convolution fusion | flops 4529848320 | bytes 19070976 | tf_op jit(solution)/shard_map/dot_general | solution.py:852
  597.3 10.9 %add_convert_fusion = bf16[1536,2304]{1,0:T(8,128)(2,1)} fusion(f32[1536,2304]{1,0:T(8,128)} %fusion.88, bf16[1536,640]{1,0:T(8,128)(2,1)S(1)} %copy-done.45, bf16[2304,640]{1,0:T(8,128)(2,1)S(1)} %bitcast.149), kind=kOutput, calls=%fused_computation.2 | convolution fusion | flops 4536926208 | bytes 26148864 | tf_op jit(solution)/shard_map/dot_general | solution.py:852
  608.1 51.5 %shard_map.242 = f32[96,2304]{1,0:T(8,128)} custom-call(bf16[16,96,2304]{2,1,0:T(8,128)(2,1)} %bitcast.145), custom_call_target="tpu_custom_call" | custom-call | tf_op jit(solution)/shard_map/pallas_call | solution.py:222
  659.6 1.5 multiply_reduce_fusion.3
  661.2 2.0 multiply_reduce_fusion.5
  664.3 10.5 %shard_map.243 = bf16[96,2304]{1,0:T(8,128)(2,1)} custom-call(bf16[96,2304]{1,0:T(8,128)(2,1)} %multiply_convert_fusion.3.block_ref), custom_call_target="tpu_custom_call" | custom-call | tf_op jit(solution)/shard_map/pallas_call | solution.py:222
  674.8 3.8 fusion.25
  678.9 1.5 fusion.30
  680.7 2.1 convolution_bitcast_fusion.2
  682.9 3.1 fusion.39
  686.1 1.2 fusion.84
  688.3 8.4 %multiply_reduce_fusion = (f32[2304]{0:T(1024)S(1)}, f32[192,2304]{1,0:T(8,128)}, f32[192,2304]{1,0:T(8,128)S(1)}) fusion(f32[192]{0:T(256)S(1)} %copy-done.37, bf16[96,2304]{1,0:T(8,128)(2,1)S(1)} %copy-done.7, bf16[96,2304]{1,0:T(8,128)(2,1)S(1)} %copy-done.4, bf16[192,2048]{1,0:T(8,128)(2,1)S(1)} %constant_dynamic-update-slice_fusion, ...), kind=kOutput, calls=%fused_computation.29 | convolution fusion | flops 1815033600 | bytes 14657280 | tf_op jit(solution)/shard_map/dot_general | solution.py:852
  696.7 1.2 copy-done.13
  698.8 11.2 %shard_map.244 = bf16[112,2304]{1,0:T(8,128)(2,1)} custom-call(bf16[112,2304]{1,0:T(8,128)(2,1)} %fusion.47.block_ref), custom_call_target="tpu_custom_call" | custom-call | tf_op jit(solution)/shard_map/pallas_call | solution.py:222
  709.9 1.2 convert_element_type.168
  711.2 1.7 multiply_reduce_fusion.2
  713.0 2.4 multiply_add_fusion
  716.8 4.6 convolution_convert_fusion.2
  721.4 5.3 convolution_convert_fusion
  726.7 94.6 %shard_map.245 = f32[144,3200]{1,0:T(8,128)} custom-call(bf16[16,144,2048]{2,1,0:T(8,128)(2,1)} %bitcast.136, bf16[16,144,1024]{2,1,0:T(8,128)(2,1)} %bitcast.147, bf16[16,144,128]{2,1,0:T(8,128)(2,1)} %bitcast.157), custom_call_target="tpu_custom_call" | custom-call | tf_op jit(solution)/shard_map/pallas_call | solution.py:222
  823.1 1.9 fusion.83
  825.0 2.4 fusion.82
  (176 shorter events, 21.4 us)
Async XLA Ops:
  0.6 209.0 %copy-start.3 = (bf16[96,2304]{1,0:T(8,128)(2,1)S(1)}, bf16[96,2304]{1,0:T(8,128)(2,1)}, u32[]{:S(2)}) copy-start(bf16[96,2304]{1,0:T(8,128)(2,1)} %rows_ref.1) | copy-start | bytes 1327108
  6.7 217.9 %copy-start.35 = (pred[192,192]{0,1:T(8,128)(4,1)}, pred[192,192]{0,1:T(8,128)(4,1)S(1)}, u32[]{:S(2)}) copy-start(pred[192,192]{0,1:T(8,128)(4,1)S(1)} %and_or_fusion) | copy-start | bytes 110596
  7.1 214.8 %copy-start.15 = (f32[192,128]{1,0:T(8,128)}, f32[192,128]{1,0:T(8,128)S(1)}, u32[]{:S(2)}) copy-start(f32[192,128]{1,0:T(8,128)S(1)} %get-tuple-element.67) | copy-start | bytes 294916
  209.6 3.0 copy-start.6
  211.0 7.4 copy-start.36
  219.6 1.9 slice-start.2
  221.5 3.1 copy-start.25
  221.9 2.7 copy-start.21
  222.0 3.3 copy-start.29
  222.0 3.3 copy-start.31
  222.0 3.3 copy-start.27
  226.0 4.2 copy-start.24
  242.0 417.7 %copy-start.38 = (f32[96]{0:T(128)}, f32[96]{0:T(128)S(1)}, u32[]{:S(2)}) copy-start(f32[96]{0:T(128)S(1)} %add_rsqrt_fusion.2) | copy-start | bytes 1156
  290.5 6.7 copy-start.1
  294.6 8.3 %copy-start.8 = (bf16[1,16,144,640]{3,2,1,0:T(8,128)(2,1)}, bf16[1,16,144,640]{3,2,1,0:T(8,128)(2,1)S(1)}, u32[]{:S(2)}) copy-start(bf16[1,16,144,640]{3,2,1,0:T(8,128)(2,1)S(1)} %get-tuple-element.39) | copy-start | bytes 8847364
  294.7 8.3 %copy-start.10 = (bf16[1,16,144,640]{3,2,1,0:T(8,128)(2,1)}, bf16[1,16,144,640]{3,2,1,0:T(8,128)(2,1)S(1)}, u32[]{:S(2)}) copy-start(bf16[1,16,144,640]{3,2,1,0:T(8,128)(2,1)S(1)} %get-tuple-element.40) | copy-start | bytes 8847364
  294.7 16.6 %copy-start.12 = (bf16[1,16,144,640]{3,2,1,0:T(8,128)(2,1)}, bf16[1,16,144,640]{3,2,1,0:T(8,128)(2,1)S(1)}, u32[]{:S(2)}) copy-start(bf16[1,16,144,640]{3,2,1,0:T(8,128)(2,1)S(1)} %get-tuple-element.38) | copy-start | bytes 8847364
  303.0 8.3 %copy-start.43 = (f32[1536,640]{1,0:T(8,128)}, f32[1536,640]{1,0:T(8,128)S(1)}, u32[]{:S(2)}) copy-start(f32[1536,640]{1,0:T(8,128)S(1)} %fusion.87) | copy-start | bytes 11796484
  311.3 7.7 copy-start.46
  319.0 49.7 %copy-start.5 = (bf16[96,2304]{1,0:T(8,128)(2,1)S(1)}, bf16[96,2304]{1,0:T(8,128)(2,1)}, u32[]{:S(2)}) copy-start(bf16[96,2304]{1,0:T(8,128)(2,1)} %param.27) | copy-start | bytes 1327108
  416.4 21.1 %copy-start.2 = (bf16[16,96,2304]{2,1,0:T(8,128)(2,1)S(1)}, bf16[16,96,2304]{2,1,0:T(8,128)(2,1)}, u32[]{:S(2)}) copy-start(bf16[16,96,2304]{2,1,0:T(8,128)(2,1)} %shard_map.241) | copy-start | bytes 21233668
  416.4 21.1 %copy-start.47 = (bf16[1536,640]{1,0:T(8,128)(2,1)S(1)}, bf16[1536,640]{1,0:T(8,128)(2,1)}, u32[]{:S(2)}) copy-start(bf16[1536,640]{1,0:T(8,128)(2,1)} %copy-done.46) | copy-start | bytes 5898244
  437.5 7.3 copy-start.44
  437.6 17.5 %copy-start.41 = (bf16[1536,640]{1,0:T(8,128)(2,1)}, bf16[1536,640]{1,0:T(8,128)(2,1)S(1)}, u32[]{:S(2)}) copy-start(bf16[1536,640]{1,0:T(8,128)(2,1)S(1)} %get-tuple-element.42) | copy-start | bytes 5898244
  437.6 17.5 %slice-start = ((s8[7077888]{0:T(1024)(128)(4,1)}), s8[4194304]{0:T(1024)(128)(4,1)S(1)}, s32[]{:S(2)}) async-start(s8[7077888]{0:T(1024)(128)(4,1)} %bitcast.140), calls=%async_computation | async-start | bytes 8388608
  444.8 10.2 %slice-start.1 = ((s8[7077888]{0:T(1024)(128)(4,1)}), s8[2883584]{0:T(1024)(128)(4,1)S(1)}, s32[]{:S(2)}) async-start(s8[7077888]{0:T(1024)(128)(4,1)} %bitcast.140), calls=%async_computation.1 | async-start | bytes 5767168
  582.7 5.8 copy-start.11
  582.7 5.8 copy-start.42
  588.5 8.8 %copy-start.9 = (bf16[1,16,144,640]{3,2,1,0:T(8,128)(2,1)S(1)}, bf16[1,16,144,640]{3,2,1,0:T(8,128)(2,1)}, u32[]{:S(2)}) copy-start(bf16[1,16,144,640]{3,2,1,0:T(8,128)(2,1)} %copy-done.8) | copy-start | bytes 8847364
  588.5 8.8 %copy-start.45 = (bf16[1536,640]{1,0:T(8,128)(2,1)S(1)}, bf16[1536,640]{1,0:T(8,128)(2,1)}, u32[]{:S(2)}) copy-start(bf16[1536,640]{1,0:T(8,128)(2,1)} %copy-done.44) | copy-start | bytes 5898244
  659.6 3.5 copy-start.40
  674.7 4.1 copy-start.26
  674.7 4.1 copy-start.28
  674.7 4.1 copy-start.30
  674.8 4.1 copy-start.32
  674.8 4.1 copy-start.49
  680.4 2.4 copy-start.33
  682.9 3.1 copy-start.16
  686.0 2.2 copy-start.4
  686.0 2.2 copy-start.7
  686.1 2.2 copy-start.37
  688.3 8.4 %copy-start.18 = (bf16[192,2048]{1,0:T(8,128)(2,1)}, bf16[192,2048]{1,0:T(8,128)(2,1)S(1)}, u32[]{:S(2)}) copy-start(bf16[192,2048]{1,0:T(8,128)(2,1)S(1)} %constant_dynamic-update-slice_fusion) | copy-start | bytes 2359300
  688.3 8.4 %copy-start.34 = (f32[1,2304]{1,0:T(1,128)S(1)}, f32[1,2304]{1,0:T(1,128)}, u32[]{:S(2)}) copy-start(f32[1,2304]{1,0:T(1,128)} %stack.38) | copy-start | bytes 27652
  697.9 15.1 %slice-start.3 = ((f32[192]{0:T(256)}), f32[96]{0:T(128)S(1)}, s32[]{:S(2)}) async-start(f32[192]{0:T(256)} %copy-done.36), calls=%async_computation.3 | async-start | bytes 1024 | tf_op jit(solution)/shard_map/slice | solution.py:1053
  709.9 3.1 copy-start.14
  713.0 3.8 copy-start.17
  713.0 3.7 copy-start.23
  716.8 4.6 copy-start.19
  (6 other events, 8.6 us)

commit v3 on v2

--- a/solution.py
+++ b/solution.py
@@ -261,120 +261,270 @@
     lax.fori_loop(0, rows // step, body, 0)
 
 
+class Scatter:
+    def __init__(self, buffers, semaphores):
+        self.held, self.from_core, self.from_across, self.from_below, self.from_above, self.total = buffers
+        self.send_sem, self.across_sem, self.below_sem, self.above_sem = semaphores
+        self.z, self.x, self.c, t = place()
+        z, x, c = self.z, self.x, self.c
+        self.rows = self.total.shape[0]
+        self.down, self.up = (fsdp_index(z - 1, x, c), t), (fsdp_index(z + 1, x, c), t)
+        self.across, self.other = (fsdp_index(z, 1 - x, c), t), (fsdp_index(z, x, 1 - c), t)
+
+    def target(self, i):
+        if i == 3:
+            return self.z
+        half = self.z // 2
+        mirrored = self.z + half * (3 - 2 * self.z)
+        base = 3 - i - (i + mirrored) // 3
+        return base + half * (3 - 2 * base)
+
+    def index(self, k, core):
+        return fsdp_index(self.target(k % 4), 1 - self.x if k < 4 else self.x, core)
+
+    def add(self, target, *sources):
+        add_rows(self.rows, 16, target, *sources)
+
+    def over(self, i):
+        return remote(
+            self.held.at[i], self.from_across.at[i], self.send_sem.at[3 + i], self.across_sem.at[i], self.across
+        )
+
+    def going_up(self, i, target):
+        return remote(
+            self.held.at[4 + i], self.from_below.at[target], self.send_sem.at[i], self.below_sem.at[target], self.up
+        )
+
+    def going_down(self, i, target):
+        return remote(
+            self.held.at[4 + i], self.from_above.at[target], self.send_sem.at[i], self.above_sem.at[target], self.down
+        )
+
+    def side(self, i):
+        self.add(self.held.at[i], self.held.at[i], self.from_core.at[i])
+        self.over(i).start()
+
+    def line(self, i):
+        z, target = self.z, self.target(i)
+        held = self.held.at[4 + i]
+        sources = (held, self.from_core.at[4 + i], self.from_across.at[i])
+        self.over(i).wait_recv()
+
+        @pl.when(target > z)
+        def _():
+            @pl.when(z > 0)
+            def _():
+                self.going_up(i, target).wait_recv()
+                self.add(held, *sources, self.from_below.at[target])
+
+            @pl.when(z == 0)
+            def _():
+                self.add(held, *sources)
+
+            self.going_up(i, target).start()
+
+        @pl.when(target < z)
+        def _():
+            @pl.when(z < 3)
+            def _():
+                self.going_down(i, target).wait_recv()
+                self.add(held, *sources, self.from_above.at[target])
+
+            @pl.when(z == 3)
+            def _():
+                self.add(held, *sources)
+
+            self.going_down(i, target).start()
+
+    def last(self):
+        z = self.z
+        self.over(3).wait_recv()
+        self.add(self.total, self.held.at[7], self.from_core.at[7], self.from_across.at[3])
+
+        @pl.when(z > 0)
+        def _():
+            self.going_up(0, z).wait_recv()
+            self.add(self.total, self.total, self.from_below.at[z])
+
+        @pl.when(z < 3)
+        def _():
+            self.going_down(0, z).wait_recv()
+            self.add(self.total, self.total, self.from_above.at[z])
+
+    def finish(self):
+        for i in range(4):
+            self.over(i).wait_send()
+        for i in range(3):
+            self.going_up(i, 0).wait_send()
+
+    @staticmethod
+    def scratch(block, kind):
+        return [
+            *[pltpu.VMEM((amount,) + block, kind) for amount in (8, 8, 4, 4, 4)],
+            pltpu.VMEM(block, jnp.float32),
+            *[pltpu.SemaphoreType.DMA((amount,)) for amount in (7, 4, 4, 4)],
+        ]
+
+
 def scatter_kernel(amount, *refs):
     parts_refs, out_ref = refs[:amount], refs[amount]
-    held, from_core, from_across, from_below, from_above, total = refs[amount + 1 : amount + 7]
-    send_sem, core_send_sem, core_sem, across_sem, below_sem, above_sem, local_sem = refs[amount + 7 :]
-    z, x, c, t = place()
-    rows = out_ref.shape[0]
-    down, up = (fsdp_index(z - 1, x, c), t), (fsdp_index(z + 1, x, c), t)
-    across, other = (fsdp_index(z, 1 - x, c), t), (fsdp_index(z, x, 1 - c), t)
-    half = z // 2
-    mirrored = z + half * (3 - 2 * z)
-
-    def target_of(i):
-        if i == 3:
-            return z
-        base = 3 - i - (i + mirrored) // 3
-        return base + half * (3 - 2 * base)
-
+    scatter = Scatter(refs[amount + 1 : amount + 7], refs[amount + 7 : amount + 11])
+    core_send_sem, core_sem, local_sem = refs[amount + 11 :]
     columns, start = [], 0
     for ref in parts_refs:
         columns.append(pl.ds(start, ref.shape[2]))
         start += ref.shape[2]
-    local = []
-    for k in range(8):
-        index = fsdp_index(target_of(k % 4), 1 - x if k < 4 else x, c)
-        copies = [
-            pltpu.make_async_copy(ref.at[index], held.at[k, :, at], local_sem.at[k * amount + i])
+
+    def local(k):
+        index = scatter.index(k, scatter.c)
+        return [
+            pltpu.make_async_copy(ref.at[index], scatter.held.at[k, :, at], local_sem.at[k * amount + i])
             for i, (ref, at) in enumerate(zip(parts_refs, columns))
         ]
-        for copy in copies:
-            copy.start()
-        local.append(copies)
-    greet_line(z, (across, other), down, up)
-    to_core = []
-    for k in range(8):
-        index = fsdp_index(target_of(k % 4), 1 - x if k < 4 else x, 1 - c)
-        copies = [
+
+    def to_core(k):
+        index = scatter.index(k, 1 - scatter.c)
+        return [
             remote(
                 ref.at[index],
-                from_core.at[k, :, at],
+                scatter.from_core.at[k, :, at],
                 core_send_sem.at[k * amount + i],
                 core_sem.at[k * amount + i],
-                other,
+                scatter.other,
             )
             for i, (ref, at) in enumerate(zip(parts_refs, columns))
         ]
-        for copy in copies:
+
+    for k in range(8):
+        for copy in local(k):
             copy.start()
-        to_core.append(copies)
+    greet_line(scatter.z, (scatter.across, scatter.other), scatter.down, scatter.up)
+    for k in range(8):
+        for copy in to_core(k):
+            copy.start()
 
     def both(k):
-        for copy in local[k]:
+        for copy in local(k):
             copy.wait()
-        for copy in to_core[k]:
+        for copy in to_core(k):
             copy.wait_recv()
 
-    to_across = []
     for i in range(4):
         both(i)
-        add_rows(rows, 16, held.at[i], held.at[i], from_core.at[i])
-        copy = remote(held.at[i], from_across.at[i], send_sem.at[3 + i], across_sem.at[i], across)
+        scatter.side(i)
+    for i in range(3):
+        both(4 + i)
+        scatter.line(i)
+    both(7)
+    scatter.last()
+    outward = pltpu.make_async_copy(scatter.total, out_ref, local_sem.at[8 * amount])
+    outward.start()
+    for k in range(8):
+        for copy in to_core(k):
+            copy.wait_send()
+    scatter.finish()
+    outward.wait()
+
+
+def contract(left, right, left_dim, right_dim):
+    return lax.dot_general(
+        left, right, (((left_dim,), (right_dim,)), ((), ())), preferred_element_type=jnp.float32
+    )
+
+
+def backward_kernel(
+    unit_grads_ref, weights_ref, rows_ref, hidden_ref, out_ref, weight_grads_ref,
+    held, from_core, from_across, from_below, from_above, total, send_sem, across_sem, below_sem, above_sem,
+    core_send_sem, core_sem, local_sem, for_core, unit_grads, weights, rows, tile, tile_sem,
+):
+    scatter = Scatter(
+        (held, from_core, from_across, from_below, from_above, total), (send_sem, across_sem, below_sem, above_sem)
+    )
+    block_rows, width = out_ref.shape
+    blocks = rows.shape[1] // block_rows
+    step = 3 * 256
+    loads = [
+        pltpu.make_async_copy(unit_grads_ref, unit_grads.at[pl.ds(0, 2)], local_sem.at[0]),
+        pltpu.make_async_copy(weights_ref.at[pl.ds(0, 2)], weights, local_sem.at[1]),
+        pltpu.make_async_copy(hidden_ref, unit_grads.at[2], local_sem.at[2]),
+        pltpu.make_async_copy(rows_ref[0], rows.at[0], local_sem.at[3]),
+        pltpu.make_async_copy(rows_ref[1], rows.at[1], local_sem.at[4]),
+    ]
+    for copy in loads:
         copy.start()
-        to_across.append(copy)
+    greet_line(scatter.z, (scatter.across, scatter.other), scatter.down, scatter.up)
+    loads[0].wait()
+    loads[1].wait()
+
+    def partial(j, core, target):
+        spots = [pl.ds(pl.multiple_of(scatter.index(k, core) * block_rows, block_rows), block_rows) for k in (j, 4 + j)]
+
+        def body(d, carry):
+            at = pl.ds(pl.multiple_of(d * step, step), step)
+            sums = None
+            for i in range(2):
+                left = jnp.concatenate([unit_grads[i, spot, :] for spot in spots], axis=0)
+                part = contract(left, weights[i, at, :], 1, 1)
+                sums = part if sums is None else sums + part
+            sums = sums.astype(target.dtype)
+            target[j, :, at] = sums[:block_rows]
+            target[4 + j, :, at] = sums[block_rows:]
+            return carry
+
+        lax.fori_loop(0, width // step, body, 0)
+
+    def to_core(k):
+        return remote(for_core.at[k], from_core.at[k], core_send_sem.at[k], core_sem.at[k], scatter.other)
+
+    tile_rows = tile.shape[2]
+
+    def tile_out(u, i):
+        return pltpu.make_async_copy(
+            tile.at[u % 2, i], weight_grads_ref.at[i, pl.ds(u * tile_rows, tile_rows), :], tile_sem.at[u % 2, i]
+        )
+
+    def weight_tile(u):
+        if u == 0:
+            for copy in loads[2:]:
+                copy.wait()
+        if u >= 2:
+            for i in range(3):
+                tile_out(u - 2, i).wait()
+
+        def body(i, carry):
+            left = rows[i // 2, :, pl.ds(u * tile_rows, tile_rows)]
+            tile[u % 2, i] = contract(left, unit_grads[i], 0, 0).astype(tile.dtype)
+            return carry
+
+        lax.fori_loop(0, 3, body, 0)
+        for i in range(3):
+            tile_out(u, i).start()
+
+    for j in range(4):
+        partial(j, 1 - scatter.c, for_core)
+        to_core(j).start()
+        to_core(4 + j).start()
+        partial(j, scatter.c, held)
+        to_core(j).wait_recv()
+        scatter.side(j)
+        if j == 1:
+            weight_tile(0)
+    weight_tile(1)
     for i in range(3):
-        k = 4 + i
-        target = target_of(i)
-        both(k)
-        to_across[i].wait_recv()
-
-        @pl.when(target > z)
-        def _():
-            @pl.when(z > 0)
-            def _():
-                remote(held.at[k], from_below.at[target], send_sem.at[i], below_sem.at[target], up).wait_recv()
-                add_rows(rows, 16, held.at[k], held.at[k], from_core.at[k], from_across.at[i], from_below.at[target])
-
-            @pl.when(z == 0)
-            def _():
-                add_rows(rows, 16, held.at[k], held.at[k], from_core.at[k], from_across.at[i])
-
-            remote(held.at[k], from_below.at[target], send_sem.at[i], below_sem.at[target], up).start()
-
-        @pl.when(target < z)
-        def _():
-            @pl.when(z < 3)
-            def _():
-                remote(held.at[k], from_above.at[target], send_sem.at[i], above_sem.at[target], down).wait_recv()
-                add_rows(rows, 16, held.at[k], held.at[k], from_core.at[k], from_across.at[i], from_above.at[target])
-
-            @pl.when(z == 3)
-            def _():
-                add_rows(rows, 16, held.at[k], held.at[k], from_core.at[k], from_across.at[i])
-
-            remote(held.at[k], from_above.at[target], send_sem.at[i], above_sem.at[target], down).start()
-
-    both(7)
-    to_across[3].wait_recv()
-    add_rows(rows, 16, total, held.at[7], from_core.at[7], from_across.at[3])
-
-    @pl.when(z > 0)
-    def _():
-        remote(held.at[7], from_below.at[z], send_sem.at[0], below_sem.at[z], up).wait_recv()
-        add_rows(rows, 16, total, total, from_below.at[z])
-
-    @pl.when(z < 3)
-    def _():
-        remote(held.at[7], from_above.at[z], send_sem.at[0], above_sem.at[z], down).wait_recv()
-        add_rows(rows, 16, total, total, from_above.at[z])
-
-    outward = pltpu.make_async_copy(total, out_ref, local_sem.at[8 * amount])
+        to_core(4 + i).wait_recv()
+        scatter.line(i)
+        weight_tile(2 + i)
+    weight_tile(5)
+    to_core(7).wait_recv()
+    scatter.last()
+    outward = pltpu.make_async_copy(total, out_ref, local_sem.at[5])
     outward.start()
-    for copy in sum(to_core, to_across):
-        copy.wait_send()
-    for i in range(3):
-        remote(held.at[4 + i], from_below.at[0], send_sem.at[i], below_sem.at[0], other).wait_send()
+    for k in range(8):
+        to_core(k).wait_send()
+    scatter.finish()
+    for u in (4, 5):
+        for i in range(3):
+            tile_out(u, i).wait()
     outward.wait()
 
 
@@ -385,28 +535,65 @@
         return lax.psum_scatter(
             jnp.concatenate(parts, axis=2), "fsdp", scatter_dimension=0, tiled=False
         ).astype(jnp.float32)
-    block, amount, kind = (rows, columns), len(parts), parts[0].dtype
+    block, amount = (rows, columns), len(parts)
     return scratch_call(
         functools.partial(scatter_kernel, amount),
         jax.ShapeDtypeStruct(block, jnp.float32),
         [
-            pltpu.VMEM((8,) + block, kind),
-            pltpu.VMEM((8,) + block, kind),
-            pltpu.VMEM((4,) + block, kind),
-            pltpu.VMEM((4,) + block, kind),
-            pltpu.VMEM((4,) + block, kind),
-            pltpu.VMEM(block, jnp.float32),
-            pltpu.SemaphoreType.DMA((7,)),
+            *Scatter.scratch(block, parts[0].dtype),
             pltpu.SemaphoreType.DMA((8 * amount,)),
             pltpu.SemaphoreType.DMA((8 * amount,)),
-            pltpu.SemaphoreType.DMA((4,)),
-            pltpu.SemaphoreType.DMA((4,)),
-            pltpu.SemaphoreType.DMA((4,)),
             pltpu.SemaphoreType.DMA((8 * amount + 1,)),
         ],
         collective_id,
         *parts,
     )
+
+
+def feed_backward(gate_grad, up_grad, feed_full, feed_input, feed_grad_rows, hidden, collective_id):
+    size = lax.axis_size("fsdp")
+    kind = hidden.dtype
+    tokens, width = feed_input.shape
+    if size != KERNEL_FSDP:
+        sums = contract(gate_grad, feed_full[0], 1, 1) + contract(up_grad, feed_full[1], 1, 1)
+        return (
+            scatter_fsdp((sums.astype(kind).reshape(size, tokens // size, width),), collective_id),
+            jnp.stack(
+                [
+                    contract(left, right, 0, 0).astype(kind)
+                    for left, right in ((feed_input, gate_grad), (feed_input, up_grad), (feed_grad_rows, hidden))
+                ]
+            ),
+        )
+    block, units = (tokens // size, width), hidden.shape[1]
+    tile_rows = width // 6
+
+    def kernel(unit_grads_ref, weights_ref, input_ref, grad_ref, hidden_ref, *refs):
+        backward_kernel(unit_grads_ref, weights_ref, (input_ref, grad_ref), hidden_ref, *refs)
+
+    rows_grad, weight_grads = scratch_call(
+        kernel,
+        (jax.ShapeDtypeStruct(block, jnp.float32), jax.ShapeDtypeStruct((3, width, units), kind)),
+        [
+            *Scatter.scratch(block, kind),
+            pltpu.SemaphoreType.DMA((8,)),
+            pltpu.SemaphoreType.DMA((8,)),
+            pltpu.SemaphoreType.DMA((6,)),
+            pltpu.VMEM((8,) + block, kind),
+            pltpu.VMEM((3, tokens, units), kind),
+            pltpu.VMEM((2, width, units), kind),
+            pltpu.VMEM((2, tokens, width), kind),
+            pltpu.VMEM((2, 3, tile_rows, units), kind),
+            pltpu.SemaphoreType.DMA((2, 3)),
+        ],
+        collective_id,
+        jnp.stack([gate_grad, up_grad]),
+        feed_full,
+        feed_input,
+        feed_grad_rows,
+        hidden,
+    )
+    return rows_grad, weight_grads
 
 
 def exchange_kernel(block_ref, out_ref, send_sem, receive_sem):
@@ -559,19 +746,19 @@
         for copy in fills:
             copy.start()
 
+    send(2)
     pass_on(0)
+    pass_on(1)
     gather.line(1)
     gather.side(0)
-    send(2)
+    send(3)
     gather.line(2)
-    send(3)
     gather.side(1)
-    pass_on(1)
+    pass_on(2)
     gather.line(3)
     gather.side(2)
-    pass_on(2)
+    pass_on(3)
     gather.side(3)
-    pass_on(3)
     gather.finish()
     rows_copy.wait()
     for k in range(16):
@@ -655,7 +842,7 @@
 
 
 def collect_kernel(
-    gate_ref, up_ref, down_ref, out_ref,
+    parts_ref, out_ref,
     held, received, rest_held, rest_received,
     local_sem, pair_send, pair_receive, rest_pair_send, rest_pair_receive, send_sem, receive_sem, rest_send, rest_receive,
 ):
@@ -663,7 +850,7 @@
     own = fsdp_index(z, x, c)
     rows = out_ref.shape[1]
     partner = (own, 1 - t)
-    parts = (gate_ref, up_ref, down_ref)
+    parts = [parts_ref.at[i] for i in range(3)]
     order = (3, 2, 1, 0)
     takes_rest = (c == 0) & (x == t)
     gives_rest = (c == 0) & (x != t)
@@ -815,14 +1002,14 @@
 
 def collect(gradients, feed_width, collective_id):
     size, pairs = lax.axis_size("fsdp"), lax.axis_size("tp")
-    shard_rows = gradients[0].shape[0] // size
+    shard_rows = gradients.shape[1] // size
     if size != KERNEL_FSDP:
-        packed = part_units(gradients, feed_width, size, pairs)
+        packed = part_units([gradients[i] for i in range(3)], feed_width, size, pairs)
         mine = lax.psum_scatter(packed, "tp", scatter_dimension=0, tiled=False)
         mine = mine.reshape(size, shard_rows, mine.shape[-1])
         mine = lax.all_to_all(mine, "fsdp", split_axis=0, concat_axis=0, tiled=True)
         return [g.astype(jnp.float32) for g in unpack_units(mine, feed_width, 3)]
-    kind = gradients[0].dtype
+    kind = gradients.dtype
     main, rest = (4, 3, 4, shard_rows, MAIN), (4, 3, 4, shard_rows, REST)
     out = scratch_call(
         collect_kernel,
@@ -843,7 +1030,7 @@
             pltpu.SemaphoreType.DMA((4,)),
         ],
         collective_id,
-        *[g.reshape(size, shard_rows, UNITS) for g in gradients],
+        gradients.reshape(3, size, shard_rows, UNITS),
     )
     return [out[i].astype(jnp.float32) for i in range(3)]
 
@@ -1104,19 +1291,10 @@
     unused_out, pullback = jax.vjp(gelu_product, gate_value, up_value)
     gate_grad, up_grad = pullback(hidden_grad)
     gate_grad, up_grad = gate_grad.astype(low), up_grad.astype(low)
-    normed_three_parts = contract_last(gate_grad, gate_full) + contract_last(up_grad, up_full)
-    normed_three_grad = scatter_fsdp(
-        (normed_three_parts.astype(low).reshape(size, rows_local, width),), 8
-    )
-    gate_weight_grad, up_weight_grad, down_weight_grad = collect(
-        (
-            contract_first(feed_input, gate_grad).astype(low),
-            contract_first(feed_input, up_grad).astype(low),
-            contract_first(feed_grad_rows, hidden).astype(low),
-        ),
-        feed_width,
-        9,
-    )
+    normed_three_grad, feed_grads = feed_backward(
+        gate_grad, up_grad, feed_full, feed_input, feed_grad_rows, hidden, 8
+    )
+    gate_weight_grad, up_weight_grad, down_weight_grad = collect(feed_grads, feed_width, 9)
 
     gain_three_grad = jnp.sum(normed_three_grad * unit_three, axis=0)
     middle_grad = upstream + norm_backward(unit_three, inverse_three, gain_three, normed_three_grad)

time: 836 us -> 766 us (0.916)
  matrix products: 129 us -> 75.7 us
  Pallas kernels: 639 us -> 624 us
    dot_general x5 -> x2, matrix products: 34.6 us -> 9.1 us  [contract_first(): lax.dot_general(left_rows, right_rows, (((0,), (0,)), ((), ())), preferre...]
    dot_general x5 -> x3, matrix products: 39.8 us -> 20.2 us  [contract_last(): lax.dot_general(left_rows, right_rows, (((1,), (1,)), ((), ())), preferre...]
    pallas_call x10, Pallas kernels: 639 us -> 624 us  [scratch_call(): pl.pallas_call(kernel, out_shape=outputs, in_specs=[ANY] * len(operands),...]
    dot_general x1, matrix products: 21.1 us -> 12.5 us  [shards(): jnp.dot(feed_grad_rows, down_full, preferred_element_type=jnp.float32)]
where the time goes in v3:
time: 766 us; the launch traced here: 756 us
  Pallas kernels  624 us (81%)
  matrix products  75.7 us (10%)
  other arithmetic  31.2 us (4%)
  local copies, waits for them, and re-layouts  23.7 us (3%)
    pallas_call x10, Pallas kernels, scratch_call(): pl.pallas_call(kernel, out_shape=outputs, in_specs=[ANY] * len(operands),...  624 us
    dot_general x3, matrix products, contract_last(): lax.dot_general(left_rows, right_rows, (((1,), (1,)), ((), ())), preferre...  20.2 us

profile of v3, /device:TPU:0, one launch (start us, length us, event | category | flops | bytes accessed | tf_op | source)
XLA Modules:
  0.0 756.4 jit_solution(2959417731820209513)
XLA Ops:
  4.1 161.6 %shard_map.237 = (bf16[16,144,3200]{2,1,0:T(8,128)(2,1)}, bf16[96,2304]{1,0:T(8,128)(2,1)}, bf16[3,16,144,640]{3,2,1,0:T(8,128)(2,1)}) custom-call(bf16[96,2304]{1,0:T(8,128)(2,1)} %rows_ref.1, bf16[144,1024]{1,0:T(8,128)(2,1)} %query_ref.1, bf16[144,512]{1,0:T(8,128)(2,1)} %key_ref.1, bf16[144,512]{1,0:T(8,128)(2,1)} %value_ref.1, ...), custom_call_target="tpu_custom_call" | custom-call | tf_op jit(solution)/shard_map/pallas_call | solution.py:222
  165.6 1.2 slice_convert_fusion.2
  167.6 5.7 fusion.4
  176.6 1.3 fusion.88
  179.2 1.0 convert_element_type.137
  180.2 4.2 fusion.8
  185.2 10.2 %shard_map.238 = bf16[96,2304]{1,0:T(8,128)(2,1)} custom-call(bf16[96,2304]{1,0:T(8,128)(2,1)} %slice.277.block_ref), custom_call_target="tpu_custom_call" | custom-call | tf_op jit(solution)/shard_map/pallas_call | solution.py:222
  195.4 1.3 multiply_reduce_fusion.9
  197.3 0.9 multiply_convert_fusion.4.block_ref
  198.2 57.1 %shard_map.239 = bf16[16,96,2304]{2,1,0:T(8,128)(2,1)} custom-call(bf16[96,2304]{1,0:T(8,128)(2,1)} %multiply_convert_fusion.4.block_ref), custom_call_target="tpu_custom_call" | custom-call | tf_op jit(solution)/shard_map/pallas_call | solution.py:222
  255.3 4.1 fusion.83
  259.4 2.5 copy-done
  262.0 5.8 fusion.89
  267.7 8.4 %multiply_convert_fusion.1 = (bf16[1536,640]{1,0:T(8,128)(2,1)S(1)}, f32[1536,640]{1,0:T(8,128)}) fusion(f32[1536,640]{1,0:T(8,128)S(1)} %fusion.89, bf16[1536,2304]{1,0:T(8,128)(2,1)S(1)} %bitcast.132, bf16[2304,640]{1,0:T(8,128)(2,1)S(1)} %bitcast.140), kind=kOutput, calls=%fused_computation.24 | convolution fusion | flops 4539678720 | bytes 19857408 | tf_op jit(solution)/shard_map/dot_general | solution.py:1279
  276.2 8.0 %convolution_convert_fusion.1 = bf16[1536,2304]{1,0:T(8,128)(2,1)} fusion(bf16[1536,640]{1,0:T(8,128)(2,1)S(1)} %get-tuple-element.74.hidden_ref, bf16[2304,640]{1,0:T(8,128)(2,1)S(1)} %bitcast.138), kind=kOutput, calls=%fused_computation.3 | convolution fusion | flops 4533387264 | bytes 11993088 | tf_op jit(solution)/shard_map/dot_general | solution.py:1039
  284.2 47.6 %shard_map.240 = f32[96,2304]{1,0:T(8,128)} custom-call(bf16[16,96,2304]{2,1,0:T(8,128)(2,1)} %bitcast.136), custom_call_target="tpu_custom_call" | custom-call | tf_op jit(solution)/shard_map/pallas_call | solution.py:222
  331.8 1.3 multiply_reduce_fusion.7
  333.1 2.0 fusion.39
  335.2 2.4 fusion.38
  337.6 42.8 %shard_map.241 = bf16[16,96,2304]{2,1,0:T(8,128)(2,1)} custom-call(bf16[96,2304]{1,0:T(8,128)(2,1)} %get-tuple-element.58.block_ref), custom_call_target="tpu_custom_call" | custom-call | tf_op jit(solution)/shard_map/pallas_call | solution.py:222
  380.4 12.5 %fusion.18 = (bf16[1,1536,640]{2,1,0:T(8,128)(2,1)S(1)}, bf16[1,1536,640]{2,1,0:T(8,128)(2,1)S(1)}) fusion(f32[1536,640]{1,0:T(8,128)} %copy-done.37, f32[1536,640]{1,0:T(8,128)} %get-tuple-element.75, bf16[1536,2304]{1,0:T(8,128)(2,1)} %bitcast.133, bf16[2304,640]{1,0:T(8,128)(2,1)} %bitcast.139), kind=kOutput, calls=%fused_computation.27 | convolution fusion | flops 4553441280 | bytes 21823488 | tf_op jit(solution)/shard_map/dot_general | solution.py:1290
  392.9 2.3 pad_maximum_fusion.unit_grads_ref
  395.1 67.7 %shard_map.242 = (f32[96,2304]{1,0:T(8,128)}, bf16[3,2304,640]{2,1,0:T(8,128)(2,1)}) custom-call(bf16[2,1536,640]{2,1,0:T(8,128)(2,1)} %pad_maximum_fusion.unit_grads_ref, bf16[3,2304,640]{2,1,0:T(8,128)(2,1)} %bitcast.129, bf16[1536,2304]{1,0:T(8,128)(2,1)} %bitcast.130, bf16[1536,2304]{1,0:T(8,128)(2,1)} %bitcast.134, bf16[1536,640]{1,0:T(8,128)(2,1)} %copy-done.12), custom_call_target="tpu_custom_call" | custom-call | tf_op jit(solution)/shard_map/pallas_call | solution.py:222
  462.9 1.5 multiply_reduce_fusion.3
  464.4 2.5 multiply_reduce_fusion.5
  466.9 1.1 multiply_convert_fusion.3.block_ref
  468.0 12.2 %shard_map.243 = bf16[96,2304]{1,0:T(8,128)(2,1)} custom-call(bf16[96,2304]{1,0:T(8,128)(2,1)} %multiply_convert_fusion.3.block_ref), custom_call_target="tpu_custom_call" | custom-call | tf_op jit(solution)/shard_map/pallas_call | solution.py:222
  480.2 3.8 fusion.27
  484.6 1.2 fusion.25
  485.8 2.2 fusion.41
  488.9 2.7 convolution_bitcast_fusion.2
  491.9 1.9 fusion.32
  493.8 8.1 %multiply_reduce_fusion = (f32[2304]{0:T(1024)S(1)}, f32[192,2304]{1,0:T(8,128)}, f32[192,2304]{1,0:T(8,128)S(1)}) fusion(f32[192]{0:T(256)S(1)} %copy-done.32, bf16[96,2304]{1,0:T(8,128)(2,1)S(1)} %copy-done.6, bf16[96,2304]{1,0:T(8,128)(2,1)S(1)} %copy-done.3, bf16[192,2048]{1,0:T(8,128)(2,1)S(1)} %constant_dynamic-update-slice_fusion, ...), kind=kOutput, calls=%fused_computation.28 | convolution fusion | flops 1815033600 | bytes 14657280 | tf_op jit(solution)/shard_map/dot_general | solution.py:1039
  502.0 1.1 copy-done.8
  504.0 12.3 %shard_map.244 = bf16[112,2304]{1,0:T(8,128)(2,1)} custom-call(bf16[112,2304]{1,0:T(8,128)(2,1)} %fusion.49.block_ref), custom_call_target="tpu_custom_call" | custom-call | tf_op jit(solution)/shard_map/pallas_call | solution.py:222
  516.4 1.2 convert_element_type.155
  517.6 1.7 multiply_reduce_fusion.2
  519.3 2.3 multiply_add_fusion
  521.6 5.4 convolution_convert_fusion
  527.1 3.7 convolution_convert_fusion.2
  531.1 0.9 pad.16.clone
  532.1 91.3 %shard_map.245 = f32[144,3200]{1,0:T(8,128)} custom-call(bf16[16,144,2048]{2,1,0:T(8,128)(2,1)} %bitcast.128, bf16[16,144,1024]{2,1,0:T(8,128)(2,1)} %bitcast.137, bf16[16,144,128]{2,1,0:T(8,128)(2,1)} %bitcast.142), custom_call_target="tpu_custom_call" | custom-call | tf_op jit(solution)/shard_map/pallas_call | solution.py:222
  623.4 0.9 slice_bitcast_fusion
  624.3 0.9 slice_reduce_fusion
  625.2 2.4 fusion.84
  627.5 1.9 fusion.85
  629.4 121.0 %shard_map.246 = bf16[3,144,4608]{2,1,0:T(8,128)(2,1)} custom-call(bf16[3,16,144,640]{3,2,1,0:T(8,128)(2,1)} %bitcast.135), custom_call_target="tpu_custom_call" | custom-call | tf_op jit(solution)/shard_map/pallas_call | solution.py:222
  750.5 5.6 bitcast_convert_fusion
  (147 shorter events, 12.7 us)
Async XLA Ops:
  4.1 163.3 %copy-start.2 = (bf16[96,2304]{1,0:T(8,128)(2,1)S(1)}, bf16[96,2304]{1,0:T(8,128)(2,1)}, u32[]{:S(2)}) copy-start(bf16[96,2304]{1,0:T(8,128)(2,1)} %rows_ref.1) | copy-start | bytes 1327108
  165.6 1.7 copy-start.5
  167.6 5.8 copy-start.31
  167.6 6.7 copy-start.36
  173.4 1.5 copy-start.14
  174.9 3.1 copy-start.30
  175.0 1.2 slice-start
  175.8 2.2 copy-start.10
  176.1 1.9 copy-start.20
  176.1 1.9 copy-start.22
  176.1 1.9 copy-start.16
  176.6 1.4 copy-start.26
  176.6 2.1 copy-start.24
  178.0 1.2 copy-start.38
  195.4 1.5 copy-start.1
  196.7 0.5 copy-start.34
  197.3 265.6 %copy-start.33 = (f32[96]{0:T(128)}, f32[96]{0:T(128)S(1)}, u32[]{:S(2)}) copy-start(f32[96]{0:T(128)S(1)} %add_rsqrt_fusion.2) | copy-start | bytes 1156
  255.3 6.7 copy-start
  259.4 16.7 %copy-start.7 = (bf16[1,16,144,640]{3,2,1,0:T(8,128)(2,1)}, bf16[1,16,144,640]{3,2,1,0:T(8,128)(2,1)S(1)}, u32[]{:S(2)}) copy-start(bf16[1,16,144,640]{3,2,1,0:T(8,128)(2,1)S(1)} %get-tuple-element.42) | copy-start | bytes 8847364
  267.7 8.4 %copy-start.37 = (f32[1536,640]{1,0:T(8,128)}, f32[1536,640]{1,0:T(8,128)S(1)}, u32[]{:S(2)}) copy-start(f32[1536,640]{1,0:T(8,128)S(1)} %fusion.89) | copy-start | bytes 11796484
  276.2 8.0 %copy-start.12 = (bf16[1536,640]{1,0:T(8,128)(2,1)}, bf16[1536,640]{1,0:T(8,128)(2,1)S(1)}, u32[]{:S(2)}) copy-start(bf16[1536,640]{1,0:T(8,128)(2,1)S(1)} %get-tuple-element.74.hidden_ref) | copy-start | bytes 5898244
  284.2 48.9 %copy-start.4 = (bf16[96,2304]{1,0:T(8,128)(2,1)S(1)}, bf16[96,2304]{1,0:T(8,128)(2,1)}, u32[]{:S(2)}) copy-start(bf16[96,2304]{1,0:T(8,128)(2,1)} %param.27) | copy-start | bytes 1327108
  462.9 4.0 copy-start.35
  480.2 4.1 copy-start.17
  480.2 4.4 copy-start.21
  480.2 4.4 copy-start.23
  480.2 4.4 copy-start.25
  480.2 4.4 copy-start.27
  484.0 1.8 copy-start.39
  484.6 3.3 copy-start.15
  485.8 2.2 copy-start.11
  491.8 2.0 copy-start.3
  491.8 2.0 copy-start.6
  491.8 2.0 copy-start.32
  493.8 8.1 %copy-start.28 = (f32[2304]{0:T(1024)S(1)}, f32[2304]{0:T(1024)}, u32[]{:S(2)}) copy-start(f32[2304]{0:T(1024)} %get-tuple-element.27) | copy-start | bytes 27652
  493.8 8.1 %copy-start.29 = (f32[2304]{0:T(1024)S(1)}, f32[2304]{0:T(1024)}, u32[]{:S(2)}) copy-start(f32[2304]{0:T(1024)} %get-tuple-element.24) | copy-start | bytes 27652
  501.9 1.2 copy-start.8
  503.2 16.1 %slice-start.1 = ((f32[192]{0:T(256)}), f32[96]{0:T(128)S(1)}, s32[]{:S(2)}) async-start(f32[192]{0:T(256)} %copy-done.31), calls=%async_computation.1 | async-start | bytes 1024 | tf_op jit(solution)/shard_map/slice | solution.py:1240
  516.3 2.9 copy-start.9
  521.6 5.4 copy-start.13
  521.6 5.4 copy-start.18
  521.6 5.4 copy-start.19

commit v4 on v3

--- a/solution.py
+++ b/solution.py
@@ -366,62 +366,78 @@
         ]
 
 
-def scatter_kernel(amount, *refs):
-    parts_refs, out_ref = refs[:amount], refs[amount]
-    scatter = Scatter(refs[amount + 1 : amount + 7], refs[amount + 7 : amount + 11])
-    core_send_sem, core_sem, local_sem = refs[amount + 11 :]
-    columns, start = [], 0
-    for ref in parts_refs:
-        columns.append(pl.ds(start, ref.shape[2]))
-        start += ref.shape[2]
-
-    def local(k):
-        index = scatter.index(k, scatter.c)
+class Blocks:
+    def __init__(self, scatter, parts_refs, core_send_sem, core_sem, local_sem):
+        self.scatter, self.parts = scatter, []
+        self.core_send_sem, self.core_sem, self.local_sem = core_send_sem, core_sem, local_sem
+        start = 0
+        for ref in parts_refs:
+            self.parts.append((ref, pl.ds(start, ref.shape[2])))
+            start += ref.shape[2]
+
+    def local(self, k):
+        index = self.scatter.index(k, self.scatter.c)
         return [
-            pltpu.make_async_copy(ref.at[index], scatter.held.at[k, :, at], local_sem.at[k * amount + i])
-            for i, (ref, at) in enumerate(zip(parts_refs, columns))
+            pltpu.make_async_copy(
+                ref.at[index], self.scatter.held.at[k, :, at], self.local_sem.at[k * len(self.parts) + i]
+            )
+            for i, (ref, at) in enumerate(self.parts)
         ]
 
-    def to_core(k):
-        index = scatter.index(k, 1 - scatter.c)
+    def to_core(self, k):
+        index = self.scatter.index(k, 1 - self.scatter.c)
         return [
             remote(
                 ref.at[index],
-                scatter.from_core.at[k, :, at],
-                core_send_sem.at[k * amount + i],
-                core_sem.at[k * amount + i],
-                scatter.other,
+                self.scatter.from_core.at[k, :, at],
+                self.core_send_sem.at[k * len(self.parts) + i],
+                self.core_sem.at[k * len(self.parts) + i],
+                self.scatter.other,
             )
-            for i, (ref, at) in enumerate(zip(parts_refs, columns))
+            for i, (ref, at) in enumerate(self.parts)
         ]
 
-    for k in range(8):
-        for copy in local(k):
-            copy.start()
+    def load(self):
+        for k in range(8):
+            for copy in self.local(k):
+                copy.start()
+
+    def send(self):
+        for k in range(8):
+            for copy in self.to_core(k):
+                copy.start()
+
+    def both(self, k):
+        for copy in self.local(k):
+            copy.wait()
+        for copy in self.to_core(k):
+            copy.wait_recv()
+
+    def finish(self):
+        for k in range(8):
+            for copy in self.to_core(k):
+                copy.wait_send()
+
+
+def scatter_kernel(amount, *refs):
+    out_ref = refs[amount]
+    scatter = Scatter(refs[amount + 1 : amount + 7], refs[amount + 7 : amount + 11])
+    blocks = Blocks(scatter, refs[:amount], *refs[amount + 11 : amount + 14])
+    (out_sem,) = refs[amount + 14 :]
+    blocks.load()
     greet_line(scatter.z, (scatter.across, scatter.other), scatter.down, scatter.up)
-    for k in range(8):
-        for copy in to_core(k):
-            copy.start()
-
-    def both(k):
-        for copy in local(k):
-            copy.wait()
-        for copy in to_core(k):
-            copy.wait_recv()
-
+    blocks.send()
     for i in range(4):
-        both(i)
+        blocks.both(i)
         scatter.side(i)
     for i in range(3):
-        both(4 + i)
+        blocks.both(4 + i)
         scatter.line(i)
-    both(7)
+    blocks.both(7)
     scatter.last()
-    outward = pltpu.make_async_copy(scatter.total, out_ref, local_sem.at[8 * amount])
+    outward = pltpu.make_async_copy(scatter.total, out_ref, out_sem.at[0])
     outward.start()
-    for k in range(8):
-        for copy in to_core(k):
-            copy.wait_send()
+    blocks.finish()
     scatter.finish()
     outward.wait()
 
@@ -541,9 +557,8 @@
         jax.ShapeDtypeStruct(block, jnp.float32),
         [
             *Scatter.scratch(block, parts[0].dtype),
-            pltpu.SemaphoreType.DMA((8 * amount,)),
-            pltpu.SemaphoreType.DMA((8 * amount,)),
-            pltpu.SemaphoreType.DMA((8 * amount + 1,)),
+            *[pltpu.SemaphoreType.DMA((8 * amount,)) for _ in range(3)],
+            pltpu.SemaphoreType.DMA((1,)),
         ],
         collective_id,
         *parts,
@@ -842,10 +857,14 @@
 
 
 def collect_kernel(
-    parts_ref, out_ref,
+    parts_ref, projected_ref, output_ref, gain_ref, out_ref, attention_ref,
     held, received, rest_held, rest_received,
     local_sem, pair_send, pair_receive, rest_pair_send, rest_pair_receive, send_sem, receive_sem, rest_send, rest_receive,
+    *scatter_refs,
 ):
+    scatter = Scatter(scatter_refs[:6], scatter_refs[6:10])
+    blocks = Blocks(scatter, (projected_ref, output_ref, gain_ref), *scatter_refs[10:13])
+    blocks.load()
     z, x, c, t = place()
     own = fsdp_index(z, x, c)
     rows = out_ref.shape[1]
@@ -924,6 +943,7 @@
                 rest_load(dz, i).start()
 
     greet([(peer(z, x, c, k), t) for k in range(1, 16)] + [partner])
+    blocks.send()
     for dz in order:
         for i in range(3):
             pair(dz, i).start()
@@ -933,7 +953,7 @@
             for i in range(3):
                 rest_pair(dz, i).start()
 
-    for dz in order:
+    def pass_on(dz):
         for i in range(3):
             load(dz, i).wait()
             pair(dz, i).wait_recv()
@@ -952,6 +972,24 @@
                 if k:
                     rest_direct(k).start()
 
+    def line(i):
+        blocks.both(4 + i)
+        scatter.line(i)
+
+    for i in range(4):
+        blocks.both(i)
+        scatter.side(i)
+    pass_on(3)
+    line(0)
+    pass_on(2)
+    line(1)
+    pass_on(1)
+    line(2)
+    pass_on(0)
+    blocks.both(7)
+    scatter.last()
+    outward = pltpu.make_async_copy(scatter.total, attention_ref, local_sem.at[26])
+    outward.start()
     keep = pltpu.make_async_copy(held.at[0, :, spot(0)], out_ref.at[:, :, main_of(own)], local_sem.at[24])
     keep.start()
     keep_rest = pltpu.make_async_copy(rest_held.at[0, :, spot(0)], out_ref.at[:, :, rest_of(z)], local_sem.at[25])
@@ -997,10 +1035,13 @@
             rest_direct(k).wait_send()
         keep_rest.wait()
 
+    blocks.finish()
+    scatter.finish()
     keep.wait()
-
-
-def collect(gradients, feed_width, collective_id):
+    outward.wait()
+
+
+def collect(gradients, feed_width, attention_parts, collective_id):
     size, pairs = lax.axis_size("fsdp"), lax.axis_size("tp")
     shard_rows = gradients.shape[1] // size
     if size != KERNEL_FSDP:
@@ -1008,18 +1049,23 @@
         mine = lax.psum_scatter(packed, "tp", scatter_dimension=0, tiled=False)
         mine = mine.reshape(size, shard_rows, mine.shape[-1])
         mine = lax.all_to_all(mine, "fsdp", split_axis=0, concat_axis=0, tiled=True)
-        return [g.astype(jnp.float32) for g in unpack_units(mine, feed_width, 3)]
+        feed = [g.astype(jnp.float32) for g in unpack_units(mine, feed_width, 3)]
+        return feed, scatter_fsdp(attention_parts, collective_id)
     kind = gradients.dtype
     main, rest = (4, 3, 4, shard_rows, MAIN), (4, 3, 4, shard_rows, REST)
-    out = scratch_call(
+    block = (shard_rows, sum(part.shape[2] for part in attention_parts))
+    out, attention = scratch_call(
         collect_kernel,
-        jax.ShapeDtypeStruct((3, shard_rows, feed_width), kind),
+        (
+            jax.ShapeDtypeStruct((3, shard_rows, feed_width), kind),
+            jax.ShapeDtypeStruct(block, jnp.float32),
+        ),
         [
             pltpu.VMEM(main, kind),
             pltpu.VMEM(main, kind),
             pltpu.VMEM(rest, kind),
             pltpu.VMEM(rest, kind),
-            pltpu.SemaphoreType.DMA((26,)),
+            pltpu.SemaphoreType.DMA((27,)),
             pltpu.SemaphoreType.DMA((12,)),
             pltpu.SemaphoreType.DMA((12,)),
             pltpu.SemaphoreType.DMA((12,)),
@@ -1028,11 +1074,14 @@
             pltpu.SemaphoreType.DMA((size,)),
             pltpu.SemaphoreType.DMA((size,)),
             pltpu.SemaphoreType.DMA((4,)),
+            *Scatter.scratch(block, kind),
+            *[pltpu.SemaphoreType.DMA((24,)) for _ in range(3)],
         ],
         collective_id,
         gradients.reshape(3, size, shard_rows, UNITS),
-    )
-    return [out[i].astype(jnp.float32) for i in range(3)]
+        *attention_parts,
+    )
+    return [out[i].astype(jnp.float32) for i in range(3)], attention
 
 
 def contract_last(left_rows, right_rows):
@@ -1294,8 +1343,6 @@
     normed_three_grad, feed_grads = feed_backward(
         gate_grad, up_grad, feed_full, feed_input, feed_grad_rows, hidden, 8
     )
-    gate_weight_grad, up_weight_grad, down_weight_grad = collect(feed_grads, feed_width, 9)
-
     gain_three_grad = jnp.sum(normed_three_grad * unit_three, axis=0)
     middle_grad = upstream + norm_backward(unit_three, inverse_three, gain_three, normed_three_grad)
     gain_two_grad = jnp.sum(middle_grad * unit_two, axis=0)
@@ -1353,7 +1400,9 @@
     gain_grads = gain_grads + received[rows_local : rows_local + 4]
     input_gradient = middle_grad + norm_backward(unit_one, inverse_one, gain_one, normed_one_grad)
 
-    attention_grads = scatter_fsdp(
+    (gate_weight_grad, up_weight_grad, down_weight_grad), attention_grads = collect(
+        feed_grads,
+        feed_width,
         [
             part.astype(low).reshape(size, shard_rows, part.shape[1])
             for part in (
@@ -1362,7 +1411,7 @@
                 jnp.pad(jnp.transpose(gain_grads), ((0, 0), (0, LANES - 4))),
             )
         ],
-        12,
+        9,
     )
     gain_shards = jnp.transpose(attention_grads[:, gain_start : gain_start + 4])
     return (

time: 766 us -> 727 us (0.949)
  Pallas kernels: 624 us -> 589 us
    pallas_call x10 -> x9, Pallas kernels: 624 us -> 589 us  [scratch_call(): pl.pallas_call(kernel, out_shape=outputs, in_specs=[ANY] * len(operands),...]
where the time goes in v4:
time: 727 us; the launch traced here: 719 us
  Pallas kernels  589 us (81%)
  matrix products  75.7 us (10%)
  other arithmetic  29.1 us (4%)
  local copies, waits for them, and re-layouts  23.9 us (3%)
    pallas_call x9, Pallas kernels, scratch_call(): pl.pallas_call(kernel, out_shape=outputs, in_specs=[ANY] * len(operands),...  589 us
    dot_general x3, matrix products, contract_last(): lax.dot_general(left_rows, right_rows, (((1,), (1,)), ((), ())), preferre...  20.2 us

profile of v4, /device:TPU:0, one launch (start us, length us, event | category | flops | bytes accessed | tf_op | source)
XLA Modules:
  0.0 719.4 jit_solution(8431165849056856892)
XLA Ops:
  4.1 161.6 %shard_map.237 = (bf16[16,144,3200]{2,1,0:T(8,128)(2,1)}, bf16[96,2304]{1,0:T(8,128)(2,1)}, bf16[3,16,144,640]{3,2,1,0:T(8,128)(2,1)}) custom-call(bf16[96,2304]{1,0:T(8,128)(2,1)} %rows_ref.1, bf16[144,1024]{1,0:T(8,128)(2,1)} %query_ref.1, bf16[144,512]{1,0:T(8,128)(2,1)} %key_ref.1, bf16[144,512]{1,0:T(8,128)(2,1)} %value_ref.1, ...), custom_call_target="tpu_custom_call" | custom-call | tf_op jit(solution)/shard_map/pallas_call | solution.py:222
  165.6 1.2 slice_convert_fusion.2
  167.6 5.7 fusion.4
  173.4 0.8 reshape.345
  176.6 1.3 fusion.88
  179.2 1.0 convert_element_type.137
  180.2 4.2 fusion.8
  185.2 10.2 %shard_map.238 = bf16[96,2304]{1,0:T(8,128)(2,1)} custom-call(bf16[96,2304]{1,0:T(8,128)(2,1)} %slice.277.block_ref), custom_call_target="tpu_custom_call" | custom-call | tf_op jit(solution)/shard_map/pallas_call | solution.py:222
  195.4 1.3 multiply_reduce_fusion.9
  197.3 0.9 multiply_convert_fusion.4.block_ref
  198.2 57.1 %shard_map.239 = bf16[16,96,2304]{2,1,0:T(8,128)(2,1)} custom-call(bf16[96,2304]{1,0:T(8,128)(2,1)} %multiply_convert_fusion.4.block_ref), custom_call_target="tpu_custom_call" | custom-call | tf_op jit(solution)/shard_map/pallas_call | solution.py:222
  255.3 4.1 fusion.83
  259.4 2.5 copy-done
  262.0 5.8 fusion.89
  267.7 8.4 %multiply_convert_fusion.1 = (bf16[1536,640]{1,0:T(8,128)(2,1)S(1)}, f32[1536,640]{1,0:T(8,128)}) fusion(f32[1536,640]{1,0:T(8,128)S(1)} %fusion.89, bf16[1536,2304]{1,0:T(8,128)(2,1)S(1)} %bitcast.132, bf16[2304,640]{1,0:T(8,128)(2,1)S(1)} %bitcast.140), kind=kOutput, calls=%fused_computation.24 | convolution fusion | flops 4539678720 | bytes 19857408 | tf_op jit(solution)/shard_map/dot_general | solution.py:1328
  276.2 8.0 %convolution_convert_fusion.1 = bf16[1536,2304]{1,0:T(8,128)(2,1)} fusion(bf16[1536,640]{1,0:T(8,128)(2,1)S(1)} %get-tuple-element.78.hidden_ref, bf16[2304,640]{1,0:T(8,128)(2,1)S(1)} %bitcast.138), kind=kOutput, calls=%fused_computation.3 | convolution fusion | flops 4533387264 | bytes 11993088 | tf_op jit(solution)/shard_map/dot_general | solution.py:1088
  284.2 47.7 %shard_map.240 = f32[96,2304]{1,0:T(8,128)} custom-call(bf16[16,96,2304]{2,1,0:T(8,128)(2,1)} %bitcast.136), custom_call_target="tpu_custom_call" | custom-call | tf_op jit(solution)/shard_map/pallas_call | solution.py:222
  331.9 1.3 multiply_reduce_fusion.7
  333.2 2.0 fusion.39
  335.3 2.4 fusion.38
  337.6 42.7 %shard_map.241 = bf16[16,96,2304]{2,1,0:T(8,128)(2,1)} custom-call(bf16[96,2304]{1,0:T(8,128)(2,1)} %get-tuple-element.62.block_ref), custom_call_target="tpu_custom_call" | custom-call | tf_op jit(solution)/shard_map/pallas_call | solution.py:222
  380.3 12.5 %fusion.18 = (bf16[1,1536,640]{2,1,0:T(8,128)(2,1)S(1)}, bf16[1,1536,640]{2,1,0:T(8,128)(2,1)S(1)}) fusion(f32[1536,640]{1,0:T(8,128)} %copy-done.38, f32[1536,640]{1,0:T(8,128)} %get-tuple-element.79, bf16[1536,2304]{1,0:T(8,128)(2,1)} %bitcast.133, bf16[2304,640]{1,0:T(8,128)(2,1)} %bitcast.139), kind=kOutput, calls=%fused_computation.27 | convolution fusion | flops 4553441280 | bytes 21823488 | tf_op jit(solution)/shard_map/dot_general | solution.py:1339
  392.8 2.3 pad_maximum_fusion.unit_grads_ref
  395.1 67.5 %shard_map.242 = (f32[96,2304]{1,0:T(8,128)}, bf16[3,2304,640]{2,1,0:T(8,128)(2,1)}) custom-call(bf16[2,1536,640]{2,1,0:T(8,128)(2,1)} %pad_maximum_fusion.unit_grads_ref, bf16[3,2304,640]{2,1,0:T(8,128)(2,1)} %bitcast.129, bf16[1536,2304]{1,0:T(8,128)(2,1)} %bitcast.130, bf16[1536,2304]{1,0:T(8,128)(2,1)} %bitcast.134, bf16[1536,640]{1,0:T(8,128)(2,1)} %copy-done.13), custom_call_target="tpu_custom_call" | custom-call | tf_op jit(solution)/shard_map/pallas_call | solution.py:222
  462.6 1.5 multiply_reduce_fusion.3
  464.1 2.5 multiply_reduce_fusion.5
  466.6 1.1 multiply_convert_fusion.3.block_ref
  467.7 12.6 %shard_map.243 = bf16[96,2304]{1,0:T(8,128)(2,1)} custom-call(bf16[96,2304]{1,0:T(8,128)(2,1)} %multiply_convert_fusion.3.block_ref), custom_call_target="tpu_custom_call" | custom-call | tf_op jit(solution)/shard_map/pallas_call | solution.py:222
  480.4 3.8 fusion.27
  484.8 1.2 fusion.25
  485.9 2.2 fusion.41
  489.1 2.7 convolution_bitcast_fusion.2
  492.0 1.9 fusion.32
  494.0 8.1 %multiply_reduce_fusion = (f32[2304]{0:T(1024)S(1)}, f32[192,2304]{1,0:T(8,128)}, f32[192,2304]{1,0:T(8,128)S(1)}) fusion(f32[192]{0:T(256)S(1)} %copy-done.33, bf16[96,2304]{1,0:T(8,128)(2,1)S(1)} %copy-done.7, bf16[96,2304]{1,0:T(8,128)(2,1)S(1)} %copy-done.3, bf16[192,2048]{1,0:T(8,128)(2,1)S(1)} %constant_dynamic-update-slice_fusion, ...), kind=kOutput, calls=%fused_computation.28 | convolution fusion | flops 1815033600 | bytes 14657280 | tf_op jit(solution)/shard_map/dot_general | solution.py:1088
  502.1 1.1 copy-done.9
  504.1 12.3 %shard_map.244 = bf16[112,2304]{1,0:T(8,128)(2,1)} custom-call(bf16[112,2304]{1,0:T(8,128)(2,1)} %fusion.49.block_ref), custom_call_target="tpu_custom_call" | custom-call | tf_op jit(solution)/shard_map/pallas_call | solution.py:222
  516.5 1.2 convert_element_type.155
  517.7 1.7 multiply_reduce_fusion.2
  519.4 2.3 multiply_add_fusion
  521.8 5.4 convolution_convert_fusion
  527.2 3.7 convolution_convert_fusion.2
  531.3 0.9 pad.16.clone
  532.2 177.2 %shard_map.245 = (bf16[3,144,4608]{2,1,0:T(8,128)(2,1)}, f32[144,3200]{1,0:T(8,128)}) custom-call(bf16[3,16,144,640]{3,2,1,0:T(8,128)(2,1)} %bitcast.135, bf16[16,144,2048]{2,1,0:T(8,128)(2,1)} %bitcast.128, bf16[16,144,1024]{2,1,0:T(8,128)(2,1)} %bitcast.137, bf16[16,144,128]{2,1,0:T(8,128)(2,1)} %bitcast.142), custom_call_target="tpu_custom_call" | custom-call | tf_op jit(solution)/shard_map/pallas_call | solution.py:222
  709.4 1.0 slice_bitcast_fusion
  710.4 0.9 slice_reduce_fusion
  711.3 2.4 fusion.84
  713.7 1.9 fusion.85
  715.6 3.5 bitcast_convert_fusion
  (148 shorter events, 11.9 us)
Async XLA Ops:
  4.1 163.3 %copy-start.2 = (bf16[96,2304]{1,0:T(8,128)(2,1)S(1)}, bf16[96,2304]{1,0:T(8,128)(2,1)}, u32[]{:S(2)}) copy-start(bf16[96,2304]{1,0:T(8,128)(2,1)} %rows_ref.1) | copy-start | bytes 1327108
  165.6 1.7 copy-start.6
  167.6 5.8 copy-start.32
  167.6 6.7 copy-start.37
  173.4 1.5 copy-start.15
  174.9 3.1 copy-start.31
  175.0 1.2 slice-start
  175.8 2.2 copy-start.11
  176.1 1.9 copy-start.21
  176.1 1.9 copy-start.23
  176.1 1.9 copy-start.17
  176.6 1.4 copy-start.27
  176.6 2.1 copy-start.25
  178.0 1.2 copy-start.39
  195.4 1.5 copy-start.1
  196.7 0.5 copy-start.35
  197.3 265.3 %copy-start.34 = (f32[96]{0:T(128)}, f32[96]{0:T(128)S(1)}, u32[]{:S(2)}) copy-start(f32[96]{0:T(128)S(1)} %add_rsqrt_fusion.2) | copy-start | bytes 1156
  255.3 6.7 copy-start
  259.4 16.7 %copy-start.8 = (bf16[1,16,144,640]{3,2,1,0:T(8,128)(2,1)}, bf16[1,16,144,640]{3,2,1,0:T(8,128)(2,1)S(1)}, u32[]{:S(2)}) copy-start(bf16[1,16,144,640]{3,2,1,0:T(8,128)(2,1)S(1)} %get-tuple-element.46) | copy-start | bytes 8847364
  267.7 8.4 %copy-start.38 = (f32[1536,640]{1,0:T(8,128)}, f32[1536,640]{1,0:T(8,128)S(1)}, u32[]{:S(2)}) copy-start(f32[1536,640]{1,0:T(8,128)S(1)} %fusion.89) | copy-start | bytes 11796484
  276.2 8.0 %copy-start.13 = (bf16[1536,640]{1,0:T(8,128)(2,1)}, bf16[1536,640]{1,0:T(8,128)(2,1)S(1)}, u32[]{:S(2)}) copy-start(bf16[1536,640]{1,0:T(8,128)(2,1)S(1)} %get-tuple-element.78.hidden_ref) | copy-start | bytes 5898244
  284.2 49.0 %copy-start.4 = (bf16[96,2304]{1,0:T(8,128)(2,1)S(1)}, bf16[96,2304]{1,0:T(8,128)(2,1)}, u32[]{:S(2)}) copy-start(bf16[96,2304]{1,0:T(8,128)(2,1)} %param.27) | copy-start | bytes 1327108
  462.6 4.0 copy-start.36
  480.3 4.1 copy-start.18
  480.3 4.4 copy-start.22
  480.3 4.4 copy-start.24
  480.3 4.4 copy-start.26
  480.3 4.4 copy-start.28
  484.1 1.8 copy-start.40
  484.7 3.3 copy-start.16
  485.9 2.2 copy-start.12
  491.9 2.0 copy-start.3
  491.9 2.0 copy-start.7
  491.9 2.0 copy-start.33
  493.9 8.1 %copy-start.29 = (f32[2304]{0:T(1024)S(1)}, f32[2304]{0:T(1024)}, u32[]{:S(2)}) copy-start(f32[2304]{0:T(1024)} %get-tuple-element.31) | copy-start | bytes 27652
  493.9 8.1 %copy-start.30 = (f32[2304]{0:T(1024)S(1)}, f32[2304]{0:T(1024)}, u32[]{:S(2)}) copy-start(f32[2304]{0:T(1024)} %get-tuple-element.28) | copy-start | bytes 27652
  502.0 1.2 copy-start.9
  503.3 16.1 %slice-start.1 = ((f32[192]{0:T(256)}), f32[96]{0:T(128)S(1)}, s32[]{:S(2)}) async-start(f32[192]{0:T(256)} %copy-done.32), calls=%async_computation.1 | async-start | bytes 1024 | tf_op jit(solution)/shard_map/slice | solution.py:1289
  516.5 2.9 copy-start.10
  521.8 5.4 copy-start.14
  521.8 5.4 copy-start.19
  521.8 5.4 copy-start.20
  709.4 6.2 copy-start.5

commit v5 on v4

--- a/solution.py
+++ b/solution.py
@@ -160,11 +160,12 @@
             self.arrived(index)
             self.relay(index, 25 + d, self.other)
 
-    def finish(self):
+    def finish(self, waits=True):
         z = self.z
-        for zi in range(4):
-            for xi in range(2):
-                self.arrived(fsdp_index(zi, xi, 1 - self.c))
+        if waits:
+            for zi in range(4):
+                for xi in range(2):
+                    self.arrived(fsdp_index(zi, xi, 1 - self.c))
 
         @pl.when(z < 3)
         def _():
@@ -457,8 +458,6 @@
         (held, from_core, from_across, from_below, from_above, total), (send_sem, across_sem, below_sem, above_sem)
     )
     block_rows, width = out_ref.shape
-    blocks = rows.shape[1] // block_rows
-    step = 3 * 256
     loads = [
         pltpu.make_async_copy(unit_grads_ref, unit_grads.at[pl.ds(0, 2)], local_sem.at[0]),
         pltpu.make_async_copy(weights_ref.at[pl.ds(0, 2)], weights, local_sem.at[1]),
@@ -472,23 +471,6 @@
     loads[0].wait()
     loads[1].wait()
 
-    def partial(j, core, target):
-        spots = [pl.ds(pl.multiple_of(scatter.index(k, core) * block_rows, block_rows), block_rows) for k in (j, 4 + j)]
-
-        def body(d, carry):
-            at = pl.ds(pl.multiple_of(d * step, step), step)
-            sums = None
-            for i in range(2):
-                left = jnp.concatenate([unit_grads[i, spot, :] for spot in spots], axis=0)
-                part = contract(left, weights[i, at, :], 1, 1)
-                sums = part if sums is None else sums + part
-            sums = sums.astype(target.dtype)
-            target[j, :, at] = sums[:block_rows]
-            target[4 + j, :, at] = sums[block_rows:]
-            return carry
-
-        lax.fori_loop(0, width // step, body, 0)
-
     def to_core(k):
         return remote(for_core.at[k], from_core.at[k], core_send_sem.at[k], core_sem.at[k], scatter.other)
 
@@ -517,10 +499,10 @@
             tile_out(u, i).start()
 
     for j in range(4):
-        partial(j, 1 - scatter.c, for_core)
+        partial_pair(scatter, unit_grads, weights, block_rows, j, 1 - scatter.c, for_core)
         to_core(j).start()
         to_core(4 + j).start()
-        partial(j, scatter.c, held)
+        partial_pair(scatter, unit_grads, weights, block_rows, j, scatter.c, held)
         to_core(j).wait_recv()
         scatter.side(j)
         if j == 1:
@@ -565,11 +547,281 @@
     )
 
 
-def feed_backward(gate_grad, up_grad, feed_full, feed_input, feed_grad_rows, hidden, collective_id):
+def gather_through(block_ref, gathered, gathered_ref, send_sem, receive_sem, out_sem, prepare, compute):
+    gather = Gather(block_ref, gathered, send_sem, receive_sem)
+    z, x, c = gather.z, gather.x, gather.c
+    _, block_rows, width = gathered.shape
+    own = pltpu.make_async_copy(block_ref, gathered.at[gather.own], out_sem.at[8])
+    own.start()
+    greet_line(z, (gather.across, gather.other), gather.down, gather.up)
+    gather.start()
+
+    def out(number):
+        at = pl.ds(number * 2, 2)
+        return pltpu.make_async_copy(gathered.at[at], gathered_ref.at[at], out_sem.at[number])
+
+    def pairs(first, side):
+        def body(i, carry):
+            dz = first + i
+            zi = (z // 2 + dz // 2) % 2 * 2 + (z + dz) % 2
+            number = zi * 2 + side
+            gather.arrived(fsdp_index(zi, side, 1 - c))
+            out(number).start()
+            left = gathered[pl.ds(number * 2, 2)].reshape(2 * block_rows, width)
+            compute(number, pl.ds(pl.multiple_of(number * 2 * block_rows, 2 * block_rows), 2 * block_rows), left)
+            return carry
+
+        lax.fori_loop(0, 2, body, 0)
+
+    gather.line(1)
+    gather.side(0)
+    own.wait()
+    prepare()
+    pairs(0, x)
+    gather.line(2)
+    gather.side(1)
+    pairs(0, 1 - x)
+    gather.line(3)
+    gather.side(2)
+    pairs(2, x)
+    gather.side(3)
+    pairs(2, 1 - x)
+    gather.finish(waits=False)
+    for number in range(8):
+        out(number).wait()
+
+
+GELU_SCALE = math.sqrt(2.0 / math.pi)
+GELU_CUBE = 0.044715
+
+
+def feed_first_kernel(
+    block_ref, weights_ref, gathered_ref, gate_up_ref, hidden_ref,
+    gathered, send_sem, receive_sem, out_sem, weights, gate_up, hidden, load_sem, gate_up_sem, hidden_sem,
+):
+    load = pltpu.make_async_copy(weights_ref.at[pl.ds(0, 2)], weights, load_sem.at[0])
+    load.start()
+
+    def outs(number, rows):
+        return (
+            pltpu.make_async_copy(gate_up.at[:, rows, :], gate_up_ref.at[:, rows, :], gate_up_sem.at[number]),
+            pltpu.make_async_copy(hidden.at[rows, :], hidden_ref.at[rows, :], hidden_sem.at[number]),
+        )
+
+    def compute(number, rows, left):
+        gate = contract(left, weights[0], 1, 0)
+        gate_up[0, rows, :] = gate
+        up = contract(left, weights[1], 1, 0)
+        gate_up[1, rows, :] = up
+        gate = gate_up[0, rows, :]
+        curve = jnp.tanh(GELU_SCALE * (gate + GELU_CUBE * (gate * gate * gate)))
+        hidden[rows, :] = (0.5 * gate * (1.0 + curve) * up).astype(hidden.dtype)
+        for copy in outs(number, rows):
+            copy.start()
+
+    gather_through(block_ref, gathered, gathered_ref, send_sem, receive_sem, out_sem, load.wait, compute)
+    pair_rows = hidden.shape[0] // 8
+    for number in range(8):
+        for copy in outs(number, pl.ds(number * pair_rows, pair_rows)):
+            copy.wait()
+
+
+def hidden_back_kernel(
+    block_ref, weights_ref, gate_up_ref, gathered_ref, unit_grads_ref,
+    gathered, send_sem, receive_sem, out_sem, weights, gate_up, unit_grads, load_sem, grads_sem,
+):
+    loads = [
+        pltpu.make_async_copy(weights_ref.at[2], weights, load_sem.at[0]),
+        pltpu.make_async_copy(gate_up_ref, gate_up, load_sem.at[1]),
+    ]
+    for copy in loads:
+        copy.start()
+
+    def prepare():
+        for copy in loads:
+            copy.wait()
+
+    def out(number, rows):
+        return pltpu.make_async_copy(unit_grads.at[:, rows, :], unit_grads_ref.at[:, rows, :], grads_sem.at[number])
+
+    def compute(number, rows, left):
+        hidden_grad = contract(left, weights[...], 1, 0)
+        gate, up = gate_up[0, rows, :], gate_up[1, rows, :]
+        square = gate * gate
+        curve = jnp.tanh(GELU_SCALE * (gate + GELU_CUBE * (square * gate)))
+        inner = GELU_SCALE * (1.0 + 3.0 * GELU_CUBE * square)
+        slope = 0.5 * (1.0 + curve) + 0.5 * gate * (1.0 - curve * curve) * inner
+        unit_grads[0, rows, :] = (hidden_grad * up * slope).astype(unit_grads.dtype)
+        unit_grads[1, rows, :] = (hidden_grad * (0.5 * gate * (1.0 + curve))).astype(unit_grads.dtype)
+        out(number, rows).start()
+
+    gather_through(block_ref, gathered, gathered_ref, send_sem, receive_sem, out_sem, prepare, compute)
+    pair_rows = unit_grads.shape[1] // 8
+    for number in range(8):
+        out(number, pl.ds(number * pair_rows, pair_rows)).wait()
+
+
+def gather_scratch(size, block, kind):
+    return [
+        pltpu.VMEM((size,) + block, kind),
+        pltpu.SemaphoreType.DMA((Gather.slots,)),
+        pltpu.SemaphoreType.DMA((size,)),
+        pltpu.SemaphoreType.DMA((9,)),
+    ]
+
+
+def feed_first(block, feed_full, collective_id):
+    size = lax.axis_size("fsdp")
+    tokens, width, units, kind = size * block.shape[0], block.shape[1], feed_full.shape[2], block.dtype
+    if size != KERNEL_FSDP:
+        rows = lax.all_gather(block, "fsdp", axis=0, tiled=True)
+        gate, up = contract(rows, feed_full[0], 1, 0), contract(rows, feed_full[1], 1, 0)
+        return rows, jnp.stack([gate, up]), gelu_product(gate, up).astype(kind)
+    rows, gate_up, hidden = scratch_call(
+        feed_first_kernel,
+        (
+            jax.ShapeDtypeStruct((size,) + block.shape, kind),
+            jax.ShapeDtypeStruct((2, tokens, units), jnp.float32),
+            jax.ShapeDtypeStruct((tokens, units), kind),
+        ),
+        [
+            *gather_scratch(size, block.shape, kind),
+            pltpu.VMEM((2, width, units), kind),
+            pltpu.VMEM((2, tokens, units), jnp.float32),
+            pltpu.VMEM((tokens, units), kind),
+            pltpu.SemaphoreType.DMA((1,)),
+            pltpu.SemaphoreType.DMA((8,)),
+            pltpu.SemaphoreType.DMA((8,)),
+        ],
+        collective_id,
+        block,
+        feed_full,
+    )
+    return rows.reshape(tokens, width), gate_up, hidden
+
+
+def hidden_back(block, feed_full, gate_up, collective_id):
+    size = lax.axis_size("fsdp")
+    tokens, width, units, kind = size * block.shape[0], block.shape[1], feed_full.shape[2], block.dtype
+    if size != KERNEL_FSDP:
+        rows = lax.all_gather(block, "fsdp", axis=0, tiled=True)
+        unused_out, pullback = jax.vjp(gelu_product, gate_up[0], gate_up[1])
+        gradients = pullback(contract(rows, feed_full[2], 1, 0))
+        return rows, jnp.stack(gradients).astype(kind)
+    rows, unit_grads = scratch_call(
+        hidden_back_kernel,
+        (
+            jax.ShapeDtypeStruct((size,) + block.shape, kind),
+            jax.ShapeDtypeStruct((2, tokens, units), kind),
+        ),
+        [
+            *gather_scratch(size, block.shape, kind),
+            pltpu.VMEM((width, units), kind),
+            pltpu.VMEM((2, tokens, units), jnp.float32),
+            pltpu.VMEM((2, tokens, units), kind),
+            pltpu.SemaphoreType.DMA((2,)),
+            pltpu.SemaphoreType.DMA((8,)),
+        ],
+        collective_id,
+        block,
+        feed_full,
+        gate_up,
+    )
+    return rows.reshape(tokens, width), unit_grads
+
+
+def partial_pair(scatter, units, weights, block_rows, j, core, target):
+    amount, width, _ = weights.shape
+    step = 3 * 256
+    spots = [pl.ds(pl.multiple_of(scatter.index(k, core) * block_rows, block_rows), block_rows) for k in (j, 4 + j)]
+
+    def body(d, carry):
+        at = pl.ds(pl.multiple_of(d * step, step), step)
+        sums = None
+        for i in range(amount):
+            left = jnp.concatenate([units[i, spot, :] for spot in spots], axis=0)
+            part = contract(left, weights[i, at, :], 1, 1)
+            sums = part if sums is None else sums + part
+        sums = sums.astype(target.dtype)
+        target[j, :, at] = sums[:block_rows]
+        target[4 + j, :, at] = sums[block_rows:]
+        return carry
+
+    lax.fori_loop(0, width // step, body, 0)
+
+
+def feed_last_kernel(
+    hidden_ref, weights_ref, out_ref,
+    held, from_core, from_across, from_below, from_above, total, send_sem, across_sem, below_sem, above_sem,
+    core_send_sem, core_sem, local_sem, for_core, hidden, weights,
+):
+    scatter = Scatter(
+        (held, from_core, from_across, from_below, from_above, total), (send_sem, across_sem, below_sem, above_sem)
+    )
+    loads = [
+        pltpu.make_async_copy(hidden_ref, hidden.at[0], local_sem.at[0]),
+        pltpu.make_async_copy(weights_ref.at[pl.ds(2, 1)], weights, local_sem.at[1]),
+    ]
+    for copy in loads:
+        copy.start()
+    greet_line(scatter.z, (scatter.across, scatter.other), scatter.down, scatter.up)
+    for copy in loads:
+        copy.wait()
+
+    def to_core(k):
+        return remote(for_core.at[k], from_core.at[k], core_send_sem.at[k], core_sem.at[k], scatter.other)
+
+    for j in range(4):
+        partial_pair(scatter, hidden, weights, out_ref.shape[0], j, 1 - scatter.c, for_core)
+        to_core(j).start()
+        to_core(4 + j).start()
+        partial_pair(scatter, hidden, weights, out_ref.shape[0], j, scatter.c, held)
+        to_core(j).wait_recv()
+        scatter.side(j)
+    for i in range(3):
+        to_core(4 + i).wait_recv()
+        scatter.line(i)
+    to_core(7).wait_recv()
+    scatter.last()
+    outward = pltpu.make_async_copy(total, out_ref, local_sem.at[2])
+    outward.start()
+    for k in range(8):
+        to_core(k).wait_send()
+    scatter.finish()
+    outward.wait()
+
+
+def feed_last(hidden, feed_full, collective_id):
+    size = lax.axis_size("fsdp")
+    tokens, width, kind = hidden.shape[0], feed_full.shape[1], hidden.dtype
+    block = (tokens // size, width)
+    if size != KERNEL_FSDP:
+        sums = contract(hidden, feed_full[2], 1, 1).astype(kind)
+        return scatter_fsdp((sums.reshape((size,) + block),), collective_id)
+    return scratch_call(
+        feed_last_kernel,
+        jax.ShapeDtypeStruct(block, jnp.float32),
+        [
+            *Scatter.scratch(block, kind),
+            pltpu.SemaphoreType.DMA((8,)),
+            pltpu.SemaphoreType.DMA((8,)),
+            pltpu.SemaphoreType.DMA((3,)),
+            pltpu.VMEM((8,) + block, kind),
+            pltpu.VMEM((1,) + hidden.shape, kind),
+            pltpu.VMEM((1,) + feed_full.shape[1:], kind),
+        ],
+        collective_id,
+        hidden,
+        feed_full,
+    )
+
+
+def feed_backward(unit_grads, feed_full, feed_input, feed_grad_rows, hidden, collective_id):
     size = lax.axis_size("fsdp")
     kind = hidden.dtype
     tokens, width = feed_input.shape
     if size != KERNEL_FSDP:
+        gate_grad, up_grad = unit_grads[0], unit_grads[1]
         sums = contract(gate_grad, feed_full[0], 1, 1) + contract(up_grad, feed_full[1], 1, 1)
         return (
             scatter_fsdp((sums.astype(kind).reshape(size, tokens // size, width),), collective_id),
@@ -602,7 +854,7 @@
             pltpu.SemaphoreType.DMA((2, 3)),
         ],
         collective_id,
-        jnp.stack([gate_grad, up_grad]),
+        unit_grads,
         feed_full,
         feed_input,
         feed_grad_rows,
@@ -1275,7 +1527,6 @@
     attention_full = attention_full.reshape(size * shard_rows, gain_start + LANES)
     gains = jnp.transpose(attention_full[:, gain_start : gain_start + 4]).astype(jnp.float32)
     gain_one, gain_two, gain_three, gain_four = gains[0], gains[1], gains[2], gains[3]
-    gate_full, up_full, down_full = feed_full[0], feed_full[1], feed_full[2]
 
     row_index = (
         jnp.arange(grouped_rows, dtype=jnp.int32) + lax.axis_index("tp") * rows_local
@@ -1323,25 +1574,16 @@
     middle = residual + unit_two * gain_two
     unit_three, inverse_three = normalize_parts(middle)
 
-    feed_input = gather_fsdp((unit_three * gain_three).astype(low), 5).reshape(-1, width)
-    gate_value = jnp.dot(feed_input, gate_full, preferred_element_type=jnp.float32)
-    up_value = jnp.dot(feed_input, up_full, preferred_element_type=jnp.float32)
-    hidden = gelu_product(gate_value, up_value).astype(low)
-    branch_two = scatter_fsdp(
-        (contract_last(hidden, down_full).astype(low).reshape(size, rows_local, width),), 6
-    )
+    feed_input, gate_up, hidden = feed_first((unit_three * gain_three).astype(low), feed_full, 5)
+    branch_two = feed_last(hidden, feed_full, 6)
     unit_four, inverse_four = normalize_parts(branch_two)
     block_output = (middle + unit_four * gain_four).astype(low)
     upstream = output_cotangent.astype(jnp.float32)
     gain_four_grad = jnp.sum(upstream * unit_four, axis=0)
     branch_two_grad = norm_backward(unit_four, inverse_four, gain_four, upstream).astype(low)
-    feed_grad_rows = gather_fsdp(branch_two_grad, 7).reshape(-1, width)
-    hidden_grad = jnp.dot(feed_grad_rows, down_full, preferred_element_type=jnp.float32)
-    unused_out, pullback = jax.vjp(gelu_product, gate_value, up_value)
-    gate_grad, up_grad = pullback(hidden_grad)
-    gate_grad, up_grad = gate_grad.astype(low), up_grad.astype(low)
+    feed_grad_rows, unit_grads = hidden_back(branch_two_grad, feed_full, gate_up, 7)
     normed_three_grad, feed_grads = feed_backward(
-        gate_grad, up_grad, feed_full, feed_input, feed_grad_rows, hidden, 8
+        unit_grads, feed_full, feed_input, feed_grad_rows, hidden, 8
     )
     gain_three_grad = jnp.sum(normed_three_grad * unit_three, axis=0)
     middle_grad = upstream + norm_backward(unit_three, inverse_three, gain_three, normed_three_grad)

time: 727 us -> 691 us (0.950)
  matrix products: 75.7 us -> 43.3 us
    dot_general x3 -> x0, matrix products: 26.6 us -> none  [the longest x1 12.5 us: shards(): jnp.dot(feed_grad_rows, down_full, preferred_element_type=jnp.float32)]
    dot_general x3 -> x2, matrix products: 20.2 us -> 12.5 us  [contract_last(): lax.dot_general(left_rows, right_rows, (((1,), (1,)), ((), ())), preferre...]
where the time goes in v5:
time: 691 us; the launch traced here: 683 us
  Pallas kernels  593 us (86%)
  matrix products  43.3 us (6%)
  other arithmetic  24.3 us (4%)
  local copies, waits for them, and re-layouts  20.7 us (3%)
    pallas_call x9, Pallas kernels, scratch_call(): pl.pallas_call(kernel, out_shape=outputs, in_specs=[ANY] * len(operands),...  593 us

profile of v5, /device:TPU:0, one launch (start us, length us, event | category | flops | bytes accessed | tf_op | source)
XLA Modules:
  0.0 683.0 jit_solution(3152917135104062512)
XLA Ops:
  4.1 161.6 %shard_map.237 = (bf16[16,144,3200]{2,1,0:T(8,128)(2,1)}, bf16[96,2304]{1,0:T(8,128)(2,1)}, bf16[3,16,144,640]{3,2,1,0:T(8,128)(2,1)}) custom-call(bf16[96,2304]{1,0:T(8,128)(2,1)} %rows_ref.1, bf16[144,1024]{1,0:T(8,128)(2,1)} %query_ref.1, bf16[144,512]{1,0:T(8,128)(2,1)} %key_ref.1, bf16[144,512]{1,0:T(8,128)(2,1)} %value_ref.1, ...), custom_call_target="tpu_custom_call" | custom-call | tf_op jit(solution)/shard_map/pallas_call | solution.py:223
  165.7 1.2 slice_convert_fusion.2
  167.2 0.7 slice_reduce_fusion.4
  168.2 5.7 fusion.4
  174.0 1.1 copy-done.16
  175.8 1.2 slice.174
  178.9 1.3 fusion.78
  180.9 0.7 fusion.21
  182.3 4.2 fusion.8
  186.4 0.8 slice.262.block_ref
  187.2 10.2 %shard_map.238 = bf16[96,2304]{1,0:T(8,128)(2,1)} custom-call(bf16[96,2304]{1,0:T(8,128)(2,1)} %slice.262.block_ref), custom_call_target="tpu_custom_call" | custom-call | tf_op jit(solution)/shard_map/pallas_call | solution.py:223
  197.4 1.3 multiply_reduce_fusion.9
  199.6 0.9 multiply_convert_fusion.2.block_ref
  200.5 58.2 %shard_map.239 = (bf16[16,96,2304]{2,1,0:T(8,128)(2,1)}, f32[2,1536,640]{2,1,0:T(8,128)}, bf16[1536,640]{1,0:T(8,128)(2,1)}) custom-call(bf16[96,2304]{1,0:T(8,128)(2,1)} %multiply_convert_fusion.2.block_ref, bf16[3,2304,640]{2,1,0:T(8,128)(2,1)} %bitcast.112), custom_call_target="tpu_custom_call" | custom-call | tf_op jit(solution)/shard_map/pallas_call | solution.py:223
  258.8 49.2 %shard_map.240 = f32[96,2304]{1,0:T(8,128)} custom-call(bf16[1536,640]{1,0:T(8,128)(2,1)} %get-tuple-element.28.hidden_ref, bf16[3,2304,640]{2,1,0:T(8,128)(2,1)} %bitcast.113), custom_call_target="tpu_custom_call" | custom-call | tf_op jit(solution)/shard_map/pallas_call | solution.py:223
  308.0 1.4 multiply_reduce_fusion.7
  309.4 2.1 fusion.30
  311.5 1.2 fusion.29
  312.7 48.5 %shard_map.241 = (bf16[16,96,2304]{2,1,0:T(8,128)(2,1)}, bf16[2,1536,640]{2,1,0:T(8,128)(2,1)}) custom-call(bf16[96,2304]{1,0:T(8,128)(2,1)} %get-tuple-element.67.block_ref, bf16[3,2304,640]{2,1,0:T(8,128)(2,1)} %bitcast.114, f32[2,1536,640]{2,1,0:T(8,128)} %get-tuple-element.29.gate_up_ref), custom_call_target="tpu_custom_call" | custom-call | tf_op jit(solution)/shard_map/pallas_call | solution.py:223
  361.3 67.8 %shard_map.242 = (f32[96,2304]{1,0:T(8,128)}, bf16[3,2304,640]{2,1,0:T(8,128)(2,1)}) custom-call(bf16[2,1536,640]{2,1,0:T(8,128)(2,1)} %get-tuple-element.30.unit_grads_ref, bf16[3,2304,640]{2,1,0:T(8,128)(2,1)} %bitcast.115, bf16[1536,2304]{1,0:T(8,128)(2,1)} %bitcast.118, bf16[1536,2304]{1,0:T(8,128)(2,1)} %bitcast.119, ...), custom_call_target="tpu_custom_call" | custom-call | tf_op jit(solution)/shard_map/pallas_call | solution.py:223
  429.1 2.1 multiply_reduce_fusion.3
  431.3 1.9 multiply_reduce_fusion.5
  433.1 1.1 multiply_convert_fusion.1.block_ref
  434.2 12.1 %shard_map.243 = bf16[96,2304]{1,0:T(8,128)(2,1)} custom-call(bf16[96,2304]{1,0:T(8,128)(2,1)} %multiply_convert_fusion.1.block_ref), custom_call_target="tpu_custom_call" | custom-call | tf_op jit(solution)/shard_map/pallas_call | solution.py:223
  446.3 3.7 fusion.18
  450.4 1.2 convolution_bitcast_fusion
  451.6 1.2 fusion.16
  452.7 2.6 fusion.32
  456.3 0.8 constant_dynamic-update-slice_fusion.2
  457.1 2.3 convolution_bitcast_fusion.2
  459.6 0.7 constant_dynamic-update-slice_fusion.1
  460.4 1.6 fusion.23
  462.0 0.7 constant_dynamic-update-slice_fusion
  462.7 8.3 %multiply_reduce_fusion = (f32[2304]{0:T(1024)S(1)}, f32[192,2304]{1,0:T(8,128)}, f32[192,2304]{1,0:T(8,128)S(1)}) fusion(f32[192]{0:T(256)S(1)} %add_rsqrt_fusion, bf16[96,2304]{1,0:T(8,128)(2,1)S(1)} %copy-done.8, bf16[96,2304]{1,0:T(8,128)(2,1)S(1)} %copy-done.3, bf16[192,2048]{1,0:T(8,128)(2,1)} %constant_dynamic-update-slice_fusion, ...), kind=kOutput, calls=%fused_computation.12 | convolution fusion | flops 1815033600 | bytes 14657280 | tf_op jit(solution)/shard_map/dot_general | solution.py:1340
  471.2 0.8 fusion.40.block_ref
  472.0 12.8 %shard_map.244 = bf16[112,2304]{1,0:T(8,128)(2,1)} custom-call(bf16[112,2304]{1,0:T(8,128)(2,1)} %fusion.40.block_ref), custom_call_target="tpu_custom_call" | custom-call | tf_op jit(solution)/shard_map/pallas_call | solution.py:223
  484.8 1.2 convert_element_type.139
  486.1 1.4 multiply_reduce_fusion.2
  487.5 1.2 multiply_add_fusion
  488.7 6.7 convolution_convert_fusion
  495.4 3.7 convolution_convert_fusion.1
  499.5 0.9 pad.16.clone
  500.4 172.4 %shard_map.245 = (bf16[3,144,4608]{2,1,0:T(8,128)(2,1)}, f32[144,3200]{1,0:T(8,128)}) custom-call(bf16[3,16,144,640]{3,2,1,0:T(8,128)(2,1)} %bitcast.117, bf16[16,144,2048]{2,1,0:T(8,128)(2,1)} %bitcast.116, bf16[16,144,1024]{2,1,0:T(8,128)(2,1)} %bitcast.120, bf16[16,144,128]{2,1,0:T(8,128)(2,1)} %bitcast.121), custom_call_target="tpu_custom_call" | custom-call | tf_op jit(solution)/shard_map/pallas_call | solution.py:223
  672.9 1.0 slice_bitcast_fusion
  673.9 0.9 slice_reduce_fusion
  674.8 2.4 fusion.74
  677.2 1.9 fusion.75
  679.1 3.5 bitcast_convert_fusion
  (157 shorter events, 10.6 us)
Async XLA Ops:
  165.6 2.3 copy-start.2
  165.6 2.3 copy-start.7
  168.2 7.0 %copy-start.44 = (s32[1,9]{1,0:T(1,128)S(1)}, s32[1,9]{1,0:T(1,128)}, u32[]{:S(2)}) copy-start(s32[1,9]{1,0:T(1,128)} %param.15) | copy-start | bytes 112
  174.0 1.1 copy-start.16
  175.2 5.1 copy-start.17
  175.8 4.5 copy-start.40
  177.4 1.0 slice-start
  177.9 0.9 copy-start.10
  177.9 0.9 copy-start.12
  178.1 2.1 copy-start.26
  178.2 2.1 copy-start.28
  178.9 1.4 copy-start.31
  178.9 1.4 copy-start.34
  182.2 4.2 copy-start.20
  197.4 1.5 copy-start.1
  197.4 1.5 copy-start.22
  198.9 0.7 copy-start.24
  199.6 229.5 %copy-start.41 = (f32[96]{0:T(128)}, f32[96]{0:T(128)S(1)}, u32[]{:S(2)}) copy-start(f32[96]{0:T(128)S(1)} %add_rsqrt_fusion.2) | copy-start | bytes 1156
  258.8 50.7 %copy-start.4 = (bf16[96,2304]{1,0:T(8,128)(2,1)S(1)}, bf16[96,2304]{1,0:T(8,128)(2,1)}, u32[]{:S(2)}) copy-start(bf16[96,2304]{1,0:T(8,128)(2,1)} %param.27) | copy-start | bytes 1327108
  258.8 50.7 %copy-start.30 = (f32[2304]{0:T(1024)S(1)}, f32[2304]{0:T(1024)}, u32[]{:S(2)}) copy-start(f32[2304]{0:T(1024)} %get-tuple-element.47) | copy-start | bytes 27652
  308.0 3.5 copy-start
  429.1 2.2 copy-start.5
  429.1 2.2 copy-start.9
  429.1 2.2 copy-start.23
  429.1 2.2 copy-start.25
  429.1 2.2 copy-start.43
  446.3 4.1 copy-start.18
  450.0 1.5 copy-start.27
  450.0 1.5 copy-start.29
  450.0 1.5 copy-start.32
  450.1 1.5 copy-start.35
  450.1 2.6 copy-start.47
  452.7 2.7 copy-start.11
  452.7 2.7 copy-start.13
  455.4 1.6 copy-start.45
  459.4 0.9 copy-start.33
  459.4 0.9 copy-start.36
  459.4 0.9 copy-start.48
  460.4 2.3 copy-start.3
  460.4 2.3 copy-start.8
  462.7 8.4 %copy-start.37 = (f32[2304]{0:T(1024)S(1)}, f32[2304]{0:T(1024)}, u32[]{:S(2)}) copy-start(f32[2304]{0:T(1024)} %get-tuple-element.41) | copy-start | bytes 27652
  462.7 8.4 %copy-start.38 = (f32[2304]{0:T(1024)S(1)}, f32[2304]{0:T(1024)}, u32[]{:S(2)}) copy-start(f32[2304]{0:T(1024)} %get-tuple-element.39) | copy-start | bytes 27652
  462.7 8.4 %copy-start.39 = (f32[2304]{0:T(1024)S(1)}, f32[2304]{0:T(1024)}, u32[]{:S(2)}) copy-start(f32[2304]{0:T(1024)} %get-tuple-element.38) | copy-start | bytes 27652
  484.8 2.7 copy-start.15
  488.7 6.7 copy-start.14
  488.7 6.7 copy-start.19
  488.7 6.7 copy-start.21
  672.9 6.2 copy-start.6
  (2 other events, 1.2 us)

commit v6 on v5

--- a/solution.py
+++ b/solution.py
@@ -63,19 +63,6 @@
     pl.semaphore_wait(barrier, len(devices) + (z + 2) // 3 + (5 - z) // 3)
 
 
-def stage_through(source, stage, target, sems):
-    inward = pltpu.make_async_copy(source, stage, sems.at[0])
-    inward.start()
-
-    def finish():
-        inward.wait()
-        outward = pltpu.make_async_copy(stage, target, sems.at[1])
-        outward.start()
-        return outward
-
-    return finish
-
-
 class Gather:
     slots = 29
 
@@ -200,23 +187,6 @@
 
                 for slot in (base + 1, base + 2, 25 + d):
                     self.sent(slot)
-
-
-def gather_kernel(block_ref, out_ref, stage, send_sem, receive_sem, local_sem):
-    gather = Gather(block_ref, out_ref, send_sem, receive_sem)
-    greet_line(gather.z, (gather.across, gather.other), gather.down, gather.up)
-    finish_own = stage_through(block_ref, stage, out_ref.at[gather.own], local_sem)
-    gather.start()
-    outward = finish_own()
-    gather.line(1)
-    gather.side(0)
-    gather.line(2)
-    gather.side(1)
-    gather.line(3)
-    gather.side(2)
-    gather.side(3)
-    gather.finish()
-    outward.wait()
 
 
 def scratch_call(kernel, outputs, scratch, collective_id, *operands):
@@ -232,24 +202,6 @@
     )(*operands)
 
 
-def gather_fsdp(block, collective_id):
-    size = lax.axis_size("fsdp")
-    if size != KERNEL_FSDP:
-        return lax.all_gather(block, "fsdp", axis=0)
-    return scratch_call(
-        gather_kernel,
-        jax.ShapeDtypeStruct((size,) + block.shape, block.dtype),
-        [
-            pltpu.VMEM(block.shape, block.dtype),
-            pltpu.SemaphoreType.DMA((29,)),
-            pltpu.SemaphoreType.DMA((size,)),
-            pltpu.SemaphoreType.DMA((2,)),
-        ],
-        collective_id,
-        block,
-    )
-
-
 def add_rows(rows, step, target, *sources):
     def body(i, carry):
         at = pl.ds(pl.multiple_of(i * step, step), step)
@@ -273,15 +225,13 @@
         self.across, self.other = (fsdp_index(z, 1 - x, c), t), (fsdp_index(z, x, 1 - c), t)
 
     def target(self, i):
-        if i == 3:
-            return self.z
         half = self.z // 2
         mirrored = self.z + half * (3 - 2 * self.z)
-        base = 3 - i - (i + mirrored) // 3
+        base = 3 - i + mirrored * (i // 2) * (2 * (i % 2) - 1)
         return base + half * (3 - 2 * base)
 
     def index(self, k, core):
-        return fsdp_index(self.target(k % 4), 1 - self.x if k < 4 else self.x, core)
+        return fsdp_index(self.target(k % 4), (self.x + 1 - k // 4) % 2, core)
 
     def add(self, target, *sources):
         add_rows(self.rows, 16, target, *sources)
@@ -418,29 +368,6 @@
         for k in range(8):
             for copy in self.to_core(k):
                 copy.wait_send()
-
-
-def scatter_kernel(amount, *refs):
-    out_ref = refs[amount]
-    scatter = Scatter(refs[amount + 1 : amount + 7], refs[amount + 7 : amount + 11])
-    blocks = Blocks(scatter, refs[:amount], *refs[amount + 11 : amount + 14])
-    (out_sem,) = refs[amount + 14 :]
-    blocks.load()
-    greet_line(scatter.z, (scatter.across, scatter.other), scatter.down, scatter.up)
-    blocks.send()
-    for i in range(4):
-        blocks.both(i)
-        scatter.side(i)
-    for i in range(3):
-        blocks.both(4 + i)
-        scatter.line(i)
-    blocks.both(7)
-    scatter.last()
-    outward = pltpu.make_async_copy(scatter.total, out_ref, out_sem.at[0])
-    outward.start()
-    blocks.finish()
-    scatter.finish()
-    outward.wait()
 
 
 def contract(left, right, left_dim, right_dim):
@@ -477,20 +404,22 @@
     tile_rows = tile.shape[2]
 
     def tile_out(u, i):
-        return pltpu.make_async_copy(
-            tile.at[u % 2, i], weight_grads_ref.at[i, pl.ds(u * tile_rows, tile_rows), :], tile_sem.at[u % 2, i]
-        )
+        at = pl.ds(pl.multiple_of(u * tile_rows, tile_rows), tile_rows)
+        return pltpu.make_async_copy(tile.at[u % 2, i], weight_grads_ref.at[i, at, :], tile_sem.at[u % 2, i])
 
     def weight_tile(u):
-        if u == 0:
+        @pl.when(u == 0)
+        def _():
             for copy in loads[2:]:
                 copy.wait()
-        if u >= 2:
+
+        @pl.when(u >= 2)
+        def _():
             for i in range(3):
                 tile_out(u - 2, i).wait()
 
         def body(i, carry):
-            left = rows[i // 2, :, pl.ds(u * tile_rows, tile_rows)]
+            left = rows[i // 2, :, pl.ds(pl.multiple_of(u * tile_rows, tile_rows), tile_rows)]
             tile[u % 2, i] = contract(left, unit_grads[i], 0, 0).astype(tile.dtype)
             return carry
 
@@ -498,21 +427,30 @@
         for i in range(3):
             tile_out(u, i).start()
 
-    for j in range(4):
-        partial_pair(scatter, unit_grads, weights, block_rows, j, 1 - scatter.c, for_core)
-        to_core(j).start()
-        to_core(4 + j).start()
-        partial_pair(scatter, unit_grads, weights, block_rows, j, scatter.c, held)
-        to_core(j).wait_recv()
-        scatter.side(j)
-        if j == 1:
-            weight_tile(0)
-    weight_tile(1)
-    for i in range(3):
-        to_core(4 + i).wait_recv()
-        scatter.line(i)
-        weight_tile(2 + i)
-    weight_tile(5)
+    def step(n, carry):
+        @pl.when(n < 4)
+        def _():
+            partial_pair(scatter, unit_grads, weights, block_rows, n, 1 - scatter.c, for_core)
+            to_core(n).start()
+            to_core(4 + n).start()
+            partial_pair(scatter, unit_grads, weights, block_rows, n, scatter.c, held)
+            to_core(n).wait_recv()
+            scatter.side(n)
+
+        @pl.when((n >= 4) & (n < 7))
+        def _():
+            to_core(n).wait_recv()
+            scatter.line(n - 4)
+
+        late = n // 4
+
+        @pl.when((n % 2 == 1) | (n >= 4))
+        def _():
+            weight_tile((1 - late) * (n // 2) + late * (n - 2))
+
+        return carry
+
+    lax.fori_loop(0, 8, step, 0)
     to_core(7).wait_recv()
     scatter.last()
     outward = pltpu.make_async_copy(total, out_ref, local_sem.at[5])
@@ -526,25 +464,8 @@
     outward.wait()
 
 
-def scatter_fsdp(parts, collective_id):
-    size, rows, _ = parts[0].shape
-    columns = sum(part.shape[2] for part in parts)
-    if size != KERNEL_FSDP:
-        return lax.psum_scatter(
-            jnp.concatenate(parts, axis=2), "fsdp", scatter_dimension=0, tiled=False
-        ).astype(jnp.float32)
-    block, amount = (rows, columns), len(parts)
-    return scratch_call(
-        functools.partial(scatter_kernel, amount),
-        jax.ShapeDtypeStruct(block, jnp.float32),
-        [
-            *Scatter.scratch(block, parts[0].dtype),
-            *[pltpu.SemaphoreType.DMA((8 * amount,)) for _ in range(3)],
-            pltpu.SemaphoreType.DMA((1,)),
-        ],
-        collective_id,
-        *parts,
-    )
+def scatter_fsdp(parts):
+    return lax.psum_scatter(jnp.concatenate(parts, axis=2), "fsdp", scatter_dimension=0, tiled=False).astype(jnp.float32)
 
 
 def gather_through(block_ref, gathered, gathered_ref, send_sem, receive_sem, out_sem, prepare, compute):
@@ -560,32 +481,36 @@
         at = pl.ds(number * 2, 2)
         return pltpu.make_async_copy(gathered.at[at], gathered_ref.at[at], out_sem.at[number])
 
-    def pairs(first, side):
-        def body(i, carry):
-            dz = first + i
-            zi = (z // 2 + dz // 2) % 2 * 2 + (z + dz) % 2
-            number = zi * 2 + side
-            gather.arrived(fsdp_index(zi, side, 1 - c))
-            out(number).start()
-            left = gathered[pl.ds(number * 2, 2)].reshape(2 * block_rows, width)
-            compute(number, pl.ds(pl.multiple_of(number * 2 * block_rows, 2 * block_rows), 2 * block_rows), left)
-            return carry
-
-        lax.fori_loop(0, 2, body, 0)
+    def step(n, carry):
+        @pl.when(n == 2)
+        def _():
+            gather.line(2)
+            gather.side(1)
+
+        @pl.when(n == 4)
+        def _():
+            gather.line(3)
+            gather.side(2)
+
+        @pl.when(n == 6)
+        def _():
+            gather.side(3)
+
+        dz = n // 4 * 2 + n % 2
+        side = (x + n // 2) % 2
+        zi = (z // 2 + dz // 2) % 2 * 2 + (z + dz) % 2
+        number = zi * 2 + side
+        gather.arrived(fsdp_index(zi, side, 1 - c))
+        out(number).start()
+        left = gathered[pl.ds(number * 2, 2)].reshape(2 * block_rows, width)
+        compute(number, pl.ds(pl.multiple_of(number * 2 * block_rows, 2 * block_rows), 2 * block_rows), left)
+        return carry
 
     gather.line(1)
     gather.side(0)
     own.wait()
     prepare()
-    pairs(0, x)
-    gather.line(2)
-    gather.side(1)
-    pairs(0, 1 - x)
-    gather.line(3)
-    gather.side(2)
-    pairs(2, x)
-    gather.side(3)
-    pairs(2, 1 - x)
+    lax.fori_loop(0, 8, step, 0)
     gather.finish(waits=False)
     for number in range(8):
         out(number).wait()
@@ -771,16 +696,22 @@
     def to_core(k):
         return remote(for_core.at[k], from_core.at[k], core_send_sem.at[k], core_sem.at[k], scatter.other)
 
-    for j in range(4):
+    def share(j, carry):
         partial_pair(scatter, hidden, weights, out_ref.shape[0], j, 1 - scatter.c, for_core)
         to_core(j).start()
         to_core(4 + j).start()
         partial_pair(scatter, hidden, weights, out_ref.shape[0], j, scatter.c, held)
         to_core(j).wait_recv()
         scatter.side(j)
-    for i in range(3):
+        return carry
+
+    def along(i, carry):
         to_core(4 + i).wait_recv()
         scatter.line(i)
+        return carry
+
+    lax.fori_loop(0, 4, share, 0)
+    lax.fori_loop(0, 3, along, 0)
     to_core(7).wait_recv()
     scatter.last()
     outward = pltpu.make_async_copy(total, out_ref, local_sem.at[2])
@@ -797,7 +728,7 @@
     block = (tokens // size, width)
     if size != KERNEL_FSDP:
         sums = contract(hidden, feed_full[2], 1, 1).astype(kind)
-        return scatter_fsdp((sums.reshape((size,) + block),), collective_id)
+        return scatter_fsdp((sums.reshape((size,) + block),))
     return scratch_call(
         feed_last_kernel,
         jax.ShapeDtypeStruct(block, jnp.float32),
@@ -824,7 +755,7 @@
         gate_grad, up_grad = unit_grads[0], unit_grads[1]
         sums = contract(gate_grad, feed_full[0], 1, 1) + contract(up_grad, feed_full[1], 1, 1)
         return (
-            scatter_fsdp((sums.astype(kind).reshape(size, tokens // size, width),), collective_id),
+            scatter_fsdp((sums.astype(kind).reshape(size, tokens // size, width),)),
             jnp.stack(
                 [
                     contract(left, right, 0, 0).astype(kind)
@@ -1228,9 +1159,12 @@
         blocks.both(4 + i)
         scatter.line(i)
 
-    for i in range(4):
+    def share(i, carry):
         blocks.both(i)
         scatter.side(i)
+        return carry
+
+    lax.fori_loop(0, 4, share, 0)
     pass_on(3)
     line(0)
     pass_on(2)
@@ -1302,7 +1236,7 @@
         mine = mine.reshape(size, shard_rows, mine.shape[-1])
         mine = lax.all_to_all(mine, "fsdp", split_axis=0, concat_axis=0, tiled=True)
         feed = [g.astype(jnp.float32) for g in unpack_units(mine, feed_width, 3)]
-        return feed, scatter_fsdp(attention_parts, collective_id)
+        return feed, scatter_fsdp(attention_parts)
     kind = gradients.dtype
     main, rest = (4, 3, 4, shard_rows, MAIN), (4, 3, 4, shard_rows, REST)
     block = (shard_rows, sum(part.shape[2] for part in attention_parts))

time: 691 us -> 686 us (level); the launches traced: 683 us -> 686 us
  no operation moved by 1% of the time
where the time goes in v6:
time: 686 us
  Pallas kernels  596 us (87%)
  matrix products  43.3 us (6%)
  other arithmetic  24.3 us (4%)
  local copies, waits for them, and re-layouts  20.7 us (3%)
    pallas_call x9, Pallas kernels, scratch_call(): pl.pallas_call(kernel, out_shape=outputs, in_specs=[ANY] * len(operands),...  596 us

profile of v6, /device:TPU:0, one launch (start us, length us, event | category | flops | bytes accessed | tf_op | source)
XLA Modules:
  0.0 685.7 jit_solution(17847895214874019227)
XLA Ops:
  4.1 161.6 %shard_map.237 = (bf16[16,144,3200]{2,1,0:T(8,128)(2,1)}, bf16[96,2304]{1,0:T(8,128)(2,1)}, bf16[3,16,144,640]{3,2,1,0:T(8,128)(2,1)}) custom-call(bf16[96,2304]{1,0:T(8,128)(2,1)} %rows_ref.1, bf16[144,1024]{1,0:T(8,128)(2,1)} %query_ref.1, bf16[144,512]{1,0:T(8,128)(2,1)} %key_ref.1, bf16[144,512]{1,0:T(8,128)(2,1)} %value_ref.1, ...), custom_call_target="tpu_custom_call" | custom-call | tf_op jit(solution)/shard_map/pallas_call | solution.py:193
  165.7 1.2 slice_convert_fusion.2
  167.2 0.7 slice_reduce_fusion.4
  168.2 5.7 fusion.4
  174.0 1.1 copy-done.16
  175.8 1.2 slice.174
  178.9 1.3 fusion.78
  180.9 0.7 fusion.21
  182.2 4.2 fusion.8
  186.4 0.8 slice.262.block_ref
  187.2 10.2 %shard_map.238 = bf16[96,2304]{1,0:T(8,128)(2,1)} custom-call(bf16[96,2304]{1,0:T(8,128)(2,1)} %slice.262.block_ref), custom_call_target="tpu_custom_call" | custom-call | tf_op jit(solution)/shard_map/pallas_call | solution.py:193
  197.4 1.3 multiply_reduce_fusion.9
  199.6 0.9 multiply_convert_fusion.2.block_ref
  200.5 59.6 %shard_map.239 = (bf16[16,96,2304]{2,1,0:T(8,128)(2,1)}, f32[2,1536,640]{2,1,0:T(8,128)}, bf16[1536,640]{1,0:T(8,128)(2,1)}) custom-call(bf16[96,2304]{1,0:T(8,128)(2,1)} %multiply_convert_fusion.2.block_ref, bf16[3,2304,640]{2,1,0:T(8,128)(2,1)} %bitcast.112), custom_call_target="tpu_custom_call" | custom-call | tf_op jit(solution)/shard_map/pallas_call | solution.py:193
  260.1 48.7 %shard_map.240 = f32[96,2304]{1,0:T(8,128)} custom-call(bf16[1536,640]{1,0:T(8,128)(2,1)} %get-tuple-element.28.hidden_ref, bf16[3,2304,640]{2,1,0:T(8,128)(2,1)} %bitcast.113), custom_call_target="tpu_custom_call" | custom-call | tf_op jit(solution)/shard_map/pallas_call | solution.py:193
  308.9 1.4 multiply_reduce_fusion.7
  310.3 2.1 fusion.30
  312.4 1.2 fusion.29
  313.6 48.3 %shard_map.241 = (bf16[16,96,2304]{2,1,0:T(8,128)(2,1)}, bf16[2,1536,640]{2,1,0:T(8,128)(2,1)}) custom-call(bf16[96,2304]{1,0:T(8,128)(2,1)} %get-tuple-element.67.block_ref, bf16[3,2304,640]{2,1,0:T(8,128)(2,1)} %bitcast.114, f32[2,1536,640]{2,1,0:T(8,128)} %get-tuple-element.29.gate_up_ref), custom_call_target="tpu_custom_call" | custom-call | tf_op jit(solution)/shard_map/pallas_call | solution.py:193
  361.9 68.1 %shard_map.242 = (f32[96,2304]{1,0:T(8,128)}, bf16[3,2304,640]{2,1,0:T(8,128)(2,1)}) custom-call(bf16[2,1536,640]{2,1,0:T(8,128)(2,1)} %get-tuple-element.30.unit_grads_ref, bf16[3,2304,640]{2,1,0:T(8,128)(2,1)} %bitcast.115, bf16[1536,2304]{1,0:T(8,128)(2,1)} %bitcast.118, bf16[1536,2304]{1,0:T(8,128)(2,1)} %bitcast.119, ...), custom_call_target="tpu_custom_call" | custom-call | tf_op jit(solution)/shard_map/pallas_call | solution.py:193
  430.1 2.1 multiply_reduce_fusion.3
  432.2 1.9 multiply_reduce_fusion.5
  434.1 1.1 multiply_convert_fusion.1.block_ref
  435.1 12.0 %shard_map.243 = bf16[96,2304]{1,0:T(8,128)(2,1)} custom-call(bf16[96,2304]{1,0:T(8,128)(2,1)} %multiply_convert_fusion.1.block_ref), custom_call_target="tpu_custom_call" | custom-call | tf_op jit(solution)/shard_map/pallas_call | solution.py:193
  447.1 3.7 fusion.18
  451.2 1.2 convolution_bitcast_fusion
  452.4 1.2 fusion.16
  453.5 2.6 fusion.32
  457.1 0.8 constant_dynamic-update-slice_fusion.2
  457.9 2.4 convolution_bitcast_fusion.2
  460.5 0.7 constant_dynamic-update-slice_fusion.1
  461.3 1.6 fusion.23
  462.9 0.7 constant_dynamic-update-slice_fusion
  463.6 8.3 %multiply_reduce_fusion = (f32[2304]{0:T(1024)S(1)}, f32[192,2304]{1,0:T(8,128)}, f32[192,2304]{1,0:T(8,128)S(1)}) fusion(f32[192]{0:T(256)S(1)} %add_rsqrt_fusion, bf16[96,2304]{1,0:T(8,128)(2,1)S(1)} %copy-done.8, bf16[96,2304]{1,0:T(8,128)(2,1)S(1)} %copy-done.3, bf16[192,2048]{1,0:T(8,128)(2,1)} %constant_dynamic-update-slice_fusion, ...), kind=kOutput, calls=%fused_computation.12 | convolution fusion | flops 1815033600 | bytes 14657280 | tf_op jit(solution)/shard_map/dot_general | solution.py:1274
  472.1 0.8 fusion.40.block_ref
  472.9 12.7 %shard_map.244 = bf16[112,2304]{1,0:T(8,128)(2,1)} custom-call(bf16[112,2304]{1,0:T(8,128)(2,1)} %fusion.40.block_ref), custom_call_target="tpu_custom_call" | custom-call | tf_op jit(solution)/shard_map/pallas_call | solution.py:193
  485.6 1.2 convert_element_type.139
  486.9 1.4 multiply_reduce_fusion.2
  488.3 1.2 multiply_add_fusion
  489.5 6.7 convolution_convert_fusion
  496.2 3.7 convolution_convert_fusion.1
  500.2 0.9 pad.16.clone
  501.2 174.8 %shard_map.245 = (bf16[3,144,4608]{2,1,0:T(8,128)(2,1)}, f32[144,3200]{1,0:T(8,128)}) custom-call(bf16[3,16,144,640]{3,2,1,0:T(8,128)(2,1)} %bitcast.117, bf16[16,144,2048]{2,1,0:T(8,128)(2,1)} %bitcast.116, bf16[16,144,1024]{2,1,0:T(8,128)(2,1)} %bitcast.120, bf16[16,144,128]{2,1,0:T(8,128)(2,1)} %bitcast.121), custom_call_target="tpu_custom_call" | custom-call | tf_op jit(solution)/shard_map/pallas_call | solution.py:193
  676.0 1.0 slice_bitcast_fusion
  677.0 0.9 slice_reduce_fusion
  677.9 2.4 fusion.74
  680.3 1.9 fusion.75
  682.2 3.5 bitcast_convert_fusion
  (157 shorter events, 10.6 us)
Async XLA Ops:
  165.6 2.3 copy-start.2
  165.6 2.3 copy-start.7
  168.2 7.0 %copy-start.44 = (s32[1,9]{1,0:T(1,128)S(1)}, s32[1,9]{1,0:T(1,128)}, u32[]{:S(2)}) copy-start(s32[1,9]{1,0:T(1,128)} %param.15) | copy-start | bytes 112
  174.0 1.1 copy-start.16
  175.2 5.1 copy-start.17
  175.8 4.5 copy-start.40
  177.4 1.0 slice-start
  177.9 0.9 copy-start.10
  177.9 0.9 copy-start.12
  178.1 2.1 copy-start.26
  178.2 2.1 copy-start.28
  178.9 1.4 copy-start.31
  178.9 1.4 copy-start.34
  182.2 4.2 copy-start.20
  197.4 1.5 copy-start.1
  197.4 1.5 copy-start.22
  198.9 0.7 copy-start.24
  199.6 230.5 %copy-start.41 = (f32[96]{0:T(128)}, f32[96]{0:T(128)S(1)}, u32[]{:S(2)}) copy-start(f32[96]{0:T(128)S(1)} %add_rsqrt_fusion.2) | copy-start | bytes 1156
  260.1 50.2 %copy-start.4 = (bf16[96,2304]{1,0:T(8,128)(2,1)S(1)}, bf16[96,2304]{1,0:T(8,128)(2,1)}, u32[]{:S(2)}) copy-start(bf16[96,2304]{1,0:T(8,128)(2,1)} %param.27) | copy-start | bytes 1327108
  260.1 50.2 %copy-start.30 = (f32[2304]{0:T(1024)S(1)}, f32[2304]{0:T(1024)}, u32[]{:S(2)}) copy-start(f32[2304]{0:T(1024)} %get-tuple-element.47) | copy-start | bytes 27652
  308.9 3.5 copy-start
  430.0 2.2 copy-start.5
  430.0 2.2 copy-start.9
  430.0 2.2 copy-start.23
  430.0 2.2 copy-start.25
  430.0 2.2 copy-start.43
  447.1 4.1 copy-start.18
  450.8 1.5 copy-start.27
  450.8 1.5 copy-start.29
  450.9 1.5 copy-start.32
  450.9 1.5 copy-start.35
  450.9 2.6 copy-start.47
  453.5 2.7 copy-start.11
  453.5 2.7 copy-start.13
  456.3 1.6 copy-start.45
  460.3 0.9 copy-start.33
  460.3 0.9 copy-start.36
  460.3 0.9 copy-start.48
  461.3 2.3 copy-start.3
  461.3 2.3 copy-start.8
  463.6 8.4 %copy-start.37 = (f32[2304]{0:T(1024)S(1)}, f32[2304]{0:T(1024)}, u32[]{:S(2)}) copy-start(f32[2304]{0:T(1024)} %get-tuple-element.41) | copy-start | bytes 27652
  463.6 8.4 %copy-start.38 = (f32[2304]{0:T(1024)S(1)}, f32[2304]{0:T(1024)}, u32[]{:S(2)}) copy-start(f32[2304]{0:T(1024)} %get-tuple-element.39) | copy-start | bytes 27652
  463.6 8.4 %copy-start.39 = (f32[2304]{0:T(1024)S(1)}, f32[2304]{0:T(1024)}, u32[]{:S(2)}) copy-start(f32[2304]{0:T(1024)} %get-tuple-element.38) | copy-start | bytes 27652
  485.6 2.7 copy-start.15
  489.5 6.7 copy-start.14
  489.5 6.7 copy-start.19
  489.5 6.7 copy-start.21
  675.9 6.2 copy-start.6
  (2 other events, 1.2 us)

commit v7 on v6

--- a/solution.py
+++ b/solution.py
@@ -954,8 +954,8 @@
     gather.side(1)
     pass_on(2)
     gather.line(3)
+    pass_on(3)
     gather.side(2)
-    pass_on(3)
     gather.side(3)
     gather.finish()
     rows_copy.wait()
@@ -1053,7 +1053,7 @@
     rows = out_ref.shape[1]
     partner = (own, 1 - t)
     parts = [parts_ref.at[i] for i in range(3)]
-    order = (3, 2, 1, 0)
+    order = (2, 3, 1, 0)
     takes_rest = (c == 0) & (x == t)
     gives_rest = (c == 0) & (x != t)
 
@@ -1165,9 +1165,9 @@
         return carry
 
     lax.fori_loop(0, 4, share, 0)
+    pass_on(2)
+    line(0)
     pass_on(3)
-    line(0)
-    pass_on(2)
     line(1)
     pass_on(1)
     line(2)

time: 686 us -> 663 us (0.966)
  Pallas kernels: 596 us -> 568 us
    pallas_call x9, Pallas kernels: 596 us -> 568 us  [scratch_call(): pl.pallas_call(kernel, out_shape=outputs, in_specs=[ANY] * len(operands),...]
where the time goes in v7:
time: 663 us; the launch traced here: 658 us
  Pallas kernels  568 us (86%)
  matrix products  43.3 us (7%)
  other arithmetic  24.3 us (4%)
  local copies, waits for them, and re-layouts  20.7 us (3%)
    pallas_call x9, Pallas kernels, scratch_call(): pl.pallas_call(kernel, out_shape=outputs, in_specs=[ANY] * len(operands),...  568 us

profile of v7, /device:TPU:0, one launch (start us, length us, event | category | flops | bytes accessed | tf_op | source)
XLA Modules:
  0.0 658.4 jit_solution(6635284816607489328)
XLA Ops:
  4.1 161.6 %shard_map.237 = (bf16[16,144,3200]{2,1,0:T(8,128)(2,1)}, bf16[96,2304]{1,0:T(8,128)(2,1)}, bf16[3,16,144,640]{3,2,1,0:T(8,128)(2,1)}) custom-call(bf16[96,2304]{1,0:T(8,128)(2,1)} %rows_ref.1, bf16[144,1024]{1,0:T(8,128)(2,1)} %query_ref.1, bf16[144,512]{1,0:T(8,128)(2,1)} %key_ref.1, bf16[144,512]{1,0:T(8,128)(2,1)} %value_ref.1, ...), custom_call_target="tpu_custom_call" | custom-call | tf_op jit(solution)/shard_map/pallas_call | solution.py:193
  165.7 1.2 slice_convert_fusion.2
  167.2 0.7 slice_reduce_fusion.4
  168.2 5.7 fusion.4
  174.0 1.1 copy-done.16
  175.8 1.2 slice.174
  178.9 1.3 fusion.78
  180.9 0.7 fusion.21
  182.2 4.2 fusion.8
  186.4 0.8 slice.262.block_ref
  187.2 10.2 %shard_map.238 = bf16[96,2304]{1,0:T(8,128)(2,1)} custom-call(bf16[96,2304]{1,0:T(8,128)(2,1)} %slice.262.block_ref), custom_call_target="tpu_custom_call" | custom-call | tf_op jit(solution)/shard_map/pallas_call | solution.py:193
  197.4 1.3 multiply_reduce_fusion.9
  199.6 0.9 multiply_convert_fusion.2.block_ref
  200.5 47.2 %shard_map.239 = (bf16[16,96,2304]{2,1,0:T(8,128)(2,1)}, f32[2,1536,640]{2,1,0:T(8,128)}, bf16[1536,640]{1,0:T(8,128)(2,1)}) custom-call(bf16[96,2304]{1,0:T(8,128)(2,1)} %multiply_convert_fusion.2.block_ref, bf16[3,2304,640]{2,1,0:T(8,128)(2,1)} %bitcast.112), custom_call_target="tpu_custom_call" | custom-call | tf_op jit(solution)/shard_map/pallas_call | solution.py:193
  247.8 51.5 %shard_map.240 = f32[96,2304]{1,0:T(8,128)} custom-call(bf16[1536,640]{1,0:T(8,128)(2,1)} %get-tuple-element.28.hidden_ref, bf16[3,2304,640]{2,1,0:T(8,128)(2,1)} %bitcast.113), custom_call_target="tpu_custom_call" | custom-call | tf_op jit(solution)/shard_map/pallas_call | solution.py:193
  299.2 1.4 multiply_reduce_fusion.7
  300.7 2.1 fusion.30
  302.7 1.2 fusion.29
  304.0 46.3 %shard_map.241 = (bf16[16,96,2304]{2,1,0:T(8,128)(2,1)}, bf16[2,1536,640]{2,1,0:T(8,128)(2,1)}) custom-call(bf16[96,2304]{1,0:T(8,128)(2,1)} %get-tuple-element.67.block_ref, bf16[3,2304,640]{2,1,0:T(8,128)(2,1)} %bitcast.114, f32[2,1536,640]{2,1,0:T(8,128)} %get-tuple-element.29.gate_up_ref), custom_call_target="tpu_custom_call" | custom-call | tf_op jit(solution)/shard_map/pallas_call | solution.py:193
  350.2 68.1 %shard_map.242 = (f32[96,2304]{1,0:T(8,128)}, bf16[3,2304,640]{2,1,0:T(8,128)(2,1)}) custom-call(bf16[2,1536,640]{2,1,0:T(8,128)(2,1)} %get-tuple-element.30.unit_grads_ref, bf16[3,2304,640]{2,1,0:T(8,128)(2,1)} %bitcast.115, bf16[1536,2304]{1,0:T(8,128)(2,1)} %bitcast.118, bf16[1536,2304]{1,0:T(8,128)(2,1)} %bitcast.119, ...), custom_call_target="tpu_custom_call" | custom-call | tf_op jit(solution)/shard_map/pallas_call | solution.py:193
  418.4 2.1 multiply_reduce_fusion.3
  420.6 1.9 multiply_reduce_fusion.5
  422.4 1.1 multiply_convert_fusion.1.block_ref
  423.5 13.4 %shard_map.243 = bf16[96,2304]{1,0:T(8,128)(2,1)} custom-call(bf16[96,2304]{1,0:T(8,128)(2,1)} %multiply_convert_fusion.1.block_ref), custom_call_target="tpu_custom_call" | custom-call | tf_op jit(solution)/shard_map/pallas_call | solution.py:193
  436.9 3.7 fusion.18
  441.0 1.2 convolution_bitcast_fusion
  442.2 1.2 fusion.16
  443.3 2.6 fusion.32
  446.9 0.8 constant_dynamic-update-slice_fusion.2
  447.7 2.4 convolution_bitcast_fusion.2
  450.3 0.7 constant_dynamic-update-slice_fusion.1
  451.1 1.6 fusion.23
  452.7 0.7 constant_dynamic-update-slice_fusion
  453.4 8.3 %multiply_reduce_fusion = (f32[2304]{0:T(1024)S(1)}, f32[192,2304]{1,0:T(8,128)}, f32[192,2304]{1,0:T(8,128)S(1)}) fusion(f32[192]{0:T(256)S(1)} %add_rsqrt_fusion, bf16[96,2304]{1,0:T(8,128)(2,1)S(1)} %copy-done.8, bf16[96,2304]{1,0:T(8,128)(2,1)S(1)} %copy-done.3, bf16[192,2048]{1,0:T(8,128)(2,1)} %constant_dynamic-update-slice_fusion, ...), kind=kOutput, calls=%fused_computation.12 | convolution fusion | flops 1815033600 | bytes 14657280 | tf_op jit(solution)/shard_map/dot_general | solution.py:1274
  461.9 0.8 fusion.40.block_ref
  462.7 13.0 %shard_map.244 = bf16[112,2304]{1,0:T(8,128)(2,1)} custom-call(bf16[112,2304]{1,0:T(8,128)(2,1)} %fusion.40.block_ref), custom_call_target="tpu_custom_call" | custom-call | tf_op jit(solution)/shard_map/pallas_call | solution.py:193
  475.7 1.2 convert_element_type.139
  477.0 1.4 multiply_reduce_fusion.2
  478.4 1.2 multiply_add_fusion
  479.6 6.7 %convolution_convert_fusion = bf16[2304,2048]{1,0:T(8,128)(2,1)} fusion(bf16[192,2048]{1,0:T(8,128)(2,1)} %constant_dynamic-update-slice_fusion, f32[2304]{0:T(1024)S(1)} %get-tuple-element.50, f32[192]{0:T(256)S(1)} %add_rsqrt_fusion, bf16[96,2304]{1,0:T(8,128)(2,1)S(1)} %copy-done.8, bf16[96,2304]{1,0:T(8,128)(2,1)S(1)} %copy-done.3), kind=kOutput, calls=%fused_computation.2 | convolution fusion | flops 1819754496 | bytes 11118336 | tf_op jit(solution)/shard_map/dot_general | solution.py:1280
  486.3 3.7 convolution_convert_fusion.1
  490.3 0.9 pad.16.clone
  491.3 157.3 %shard_map.245 = (bf16[3,144,4608]{2,1,0:T(8,128)(2,1)}, f32[144,3200]{1,0:T(8,128)}) custom-call(bf16[3,16,144,640]{3,2,1,0:T(8,128)(2,1)} %bitcast.117, bf16[16,144,2048]{2,1,0:T(8,128)(2,1)} %bitcast.116, bf16[16,144,1024]{2,1,0:T(8,128)(2,1)} %bitcast.120, bf16[16,144,128]{2,1,0:T(8,128)(2,1)} %bitcast.121), custom_call_target="tpu_custom_call" | custom-call | tf_op jit(solution)/shard_map/pallas_call | solution.py:193
  648.6 1.0 slice_bitcast_fusion
  649.7 0.9 slice_reduce_fusion
  650.6 2.4 fusion.74
  652.9 1.9 fusion.75
  654.9 3.5 bitcast_convert_fusion
  (157 shorter events, 10.6 us)
Async XLA Ops:
  165.6 2.3 copy-start.2
  165.6 2.3 copy-start.7
  168.2 7.0 %copy-start.44 = (s32[1,9]{1,0:T(1,128)S(1)}, s32[1,9]{1,0:T(1,128)}, u32[]{:S(2)}) copy-start(s32[1,9]{1,0:T(1,128)} %param.15) | copy-start | bytes 112
  174.0 1.1 copy-start.16
  175.2 5.1 copy-start.17
  175.8 4.5 copy-start.40
  177.4 1.0 slice-start
  177.9 0.9 copy-start.10
  177.9 0.9 copy-start.12
  178.1 2.1 copy-start.26
  178.2 2.1 copy-start.28
  178.9 1.4 copy-start.31
  178.9 1.4 copy-start.34
  182.2 4.2 copy-start.20
  197.4 1.5 copy-start.1
  197.4 1.5 copy-start.22
  198.9 0.7 copy-start.24
  199.6 218.8 %copy-start.41 = (f32[96]{0:T(128)}, f32[96]{0:T(128)S(1)}, u32[]{:S(2)}) copy-start(f32[96]{0:T(128)S(1)} %add_rsqrt_fusion.2) | copy-start | bytes 1156
  247.8 52.9 %copy-start.4 = (bf16[96,2304]{1,0:T(8,128)(2,1)S(1)}, bf16[96,2304]{1,0:T(8,128)(2,1)}, u32[]{:S(2)}) copy-start(bf16[96,2304]{1,0:T(8,128)(2,1)} %param.27) | copy-start | bytes 1327108
  247.8 52.9 %copy-start.30 = (f32[2304]{0:T(1024)S(1)}, f32[2304]{0:T(1024)}, u32[]{:S(2)}) copy-start(f32[2304]{0:T(1024)} %get-tuple-element.47) | copy-start | bytes 27652
  299.2 3.5 copy-start
  418.4 2.2 copy-start.5
  418.4 2.2 copy-start.9
  418.4 2.2 copy-start.23
  418.4 2.2 copy-start.25
  418.4 2.2 copy-start.43
  436.9 4.1 copy-start.18
  440.6 1.5 copy-start.27
  440.6 1.5 copy-start.29
  440.7 1.5 copy-start.32
  440.7 1.5 copy-start.35
  440.7 2.6 copy-start.47
  443.3 2.7 copy-start.11
  443.3 2.7 copy-start.13
  446.1 1.6 copy-start.45
  450.1 0.9 copy-start.33
  450.1 0.9 copy-start.36
  450.1 0.9 copy-start.48
  451.0 2.3 copy-start.3
  451.1 2.3 copy-start.8
  453.4 8.4 %copy-start.37 = (f32[2304]{0:T(1024)S(1)}, f32[2304]{0:T(1024)}, u32[]{:S(2)}) copy-start(f32[2304]{0:T(1024)} %get-tuple-element.41) | copy-start | bytes 27652
  453.4 8.4 %copy-start.38 = (f32[2304]{0:T(1024)S(1)}, f32[2304]{0:T(1024)}, u32[]{:S(2)}) copy-start(f32[2304]{0:T(1024)} %get-tuple-element.39) | copy-start | bytes 27652
  453.4 8.4 %copy-start.39 = (f32[2304]{0:T(1024)S(1)}, f32[2304]{0:T(1024)}, u32[]{:S(2)}) copy-start(f32[2304]{0:T(1024)} %get-tuple-element.38) | copy-start | bytes 27652
  475.7 2.7 copy-start.15
  479.6 6.7 %copy-start.14 = (bf16[96,2304]{1,0:T(8,128)(2,1)S(1)}, bf16[96,2304]{1,0:T(8,128)(2,1)}, u32[]{:S(2)}) copy-start(bf16[96,2304]{1,0:T(8,128)(2,1)} %multiply_convert_fusion.1.block_ref) | copy-start | bytes 1327108
  479.6 6.7 %copy-start.19 = (bf16[96,2304]{1,0:T(8,128)(2,1)S(1)}, bf16[96,2304]{1,0:T(8,128)(2,1)}, u32[]{:S(2)}) copy-start(bf16[96,2304]{1,0:T(8,128)(2,1)} %shard_map.243) | copy-start | bytes 1327108
  479.6 6.7 %copy-start.21 = (bf16[192,1024]{1,0:T(8,128)(2,1)S(1)}, bf16[192,1024]{1,0:T(8,128)(2,1)}, u32[]{:S(2)}) copy-start(bf16[192,1024]{1,0:T(8,128)(2,1)} %copy-done.20) | copy-start | bytes 1179652
  648.6 6.2 copy-start.6
  (2 other events, 1.2 us)

commit v8 on v7

--- a/solution.py
+++ b/solution.py
@@ -437,20 +437,19 @@
             to_core(n).wait_recv()
             scatter.side(n)
 
-        @pl.when((n >= 4) & (n < 7))
+        @pl.when(n >= 4)
         def _():
             to_core(n).wait_recv()
             scatter.line(n - 4)
 
-        late = n // 4
-
-        @pl.when((n % 2 == 1) | (n >= 4))
-        def _():
-            weight_tile((1 - late) * (n // 2) + late * (n - 2))
+        @pl.when(n >= 4)
+        def _():
+            weight_tile(2 * n - 8)
+            weight_tile(2 * n - 7)
 
         return carry
 
-    lax.fori_loop(0, 8, step, 0)
+    lax.fori_loop(0, 7, step, 0)
     to_core(7).wait_recv()
     scatter.last()
     outward = pltpu.make_async_copy(total, out_ref, local_sem.at[5])
@@ -1558,7 +1557,9 @@
         ],
         axis=1,
     )
-    input_parts = contract_last(projected_grad, attention_full[:, :output_start])
+    input_parts = lax.optimization_barrier(
+        contract_last(projected_grad, attention_full[:, :output_start])
+    )
 
     gain_grads = jnp.stack(
         [

time: 663 us -> 654 us (0.986)
  no operation moved by 1% of the time
where the time goes in v8:
time: 654 us; the launch traced here: 649 us
  Pallas kernels  565 us (86%)
  matrix products  39.1 us (6%)
  other arithmetic  23.3 us (4%)
  local copies, waits for them, and re-layouts  20.1 us (3%)
    pallas_call x9, Pallas kernels, scratch_call(): pl.pallas_call(kernel, out_shape=outputs, in_specs=[ANY] * len(operands),...  565 us

profile of v8, /device:TPU:0, one launch (start us, length us, event | category | flops | bytes accessed | tf_op | source)
XLA Modules:
  0.0 649.3 jit_solution(9768928500641366107)
XLA Ops:
  0.6 0.7 stack.33
  1.3 0.7 stack.32
  2.0 0.7 stack.31
  4.1 161.6 %shard_map.237 = (bf16[16,144,3200]{2,1,0:T(8,128)(2,1)}, bf16[96,2304]{1,0:T(8,128)(2,1)}, bf16[3,16,144,640]{3,2,1,0:T(8,128)(2,1)}) custom-call(bf16[96,2304]{1,0:T(8,128)(2,1)} %rows_ref.1, bf16[144,1024]{1,0:T(8,128)(2,1)} %query_ref.1, bf16[144,512]{1,0:T(8,128)(2,1)} %key_ref.1, bf16[144,512]{1,0:T(8,128)(2,1)} %value_ref.1, ...), custom_call_target="tpu_custom_call" | custom-call | tf_op jit(solution)/shard_map/pallas_call | solution.py:193
  165.7 1.2 slice_convert_fusion.2
  167.2 0.7 slice_reduce_fusion.4
  168.2 5.7 fusion.4
  174.5 0.8 and_or_fusion
  177.4 1.3 fusion.78
  179.3 0.7 fusion.21
  180.7 4.2 fusion.8
  184.9 0.8 slice.262.block_ref
  185.7 10.1 %shard_map.238 = bf16[96,2304]{1,0:T(8,128)(2,1)} custom-call(bf16[96,2304]{1,0:T(8,128)(2,1)} %slice.262.block_ref), custom_call_target="tpu_custom_call" | custom-call | tf_op jit(solution)/shard_map/pallas_call | solution.py:193
  195.9 1.3 multiply_reduce_fusion.9
  198.1 0.9 multiply_convert_fusion.2.block_ref
  199.0 47.3 %shard_map.239 = (bf16[16,96,2304]{2,1,0:T(8,128)(2,1)}, f32[2,1536,640]{2,1,0:T(8,128)}, bf16[1536,640]{1,0:T(8,128)(2,1)}) custom-call(bf16[96,2304]{1,0:T(8,128)(2,1)} %multiply_convert_fusion.2.block_ref, bf16[3,2304,640]{2,1,0:T(8,128)(2,1)} %bitcast.112), custom_call_target="tpu_custom_call" | custom-call | tf_op jit(solution)/shard_map/pallas_call | solution.py:193
  246.2 51.5 %shard_map.240 = f32[96,2304]{1,0:T(8,128)} custom-call(bf16[1536,640]{1,0:T(8,128)(2,1)} %get-tuple-element.28.hidden_ref, bf16[3,2304,640]{2,1,0:T(8,128)(2,1)} %bitcast.113), custom_call_target="tpu_custom_call" | custom-call | tf_op jit(solution)/shard_map/pallas_call | solution.py:193
  297.8 1.4 multiply_reduce_fusion.7
  299.2 2.0 fusion.30
  301.2 1.2 fusion.29
  302.5 46.1 %shard_map.241 = (bf16[16,96,2304]{2,1,0:T(8,128)(2,1)}, bf16[2,1536,640]{2,1,0:T(8,128)(2,1)}) custom-call(bf16[96,2304]{1,0:T(8,128)(2,1)} %get-tuple-element.67.block_ref, bf16[3,2304,640]{2,1,0:T(8,128)(2,1)} %bitcast.114, f32[2,1536,640]{2,1,0:T(8,128)} %get-tuple-element.29.gate_up_ref), custom_call_target="tpu_custom_call" | custom-call | tf_op jit(solution)/shard_map/pallas_call | solution.py:193
  348.6 64.9 %shard_map.242 = (f32[96,2304]{1,0:T(8,128)}, bf16[3,2304,640]{2,1,0:T(8,128)(2,1)}) custom-call(bf16[2,1536,640]{2,1,0:T(8,128)(2,1)} %get-tuple-element.30.unit_grads_ref, bf16[3,2304,640]{2,1,0:T(8,128)(2,1)} %bitcast.115, bf16[1536,2304]{1,0:T(8,128)(2,1)} %bitcast.118, bf16[1536,2304]{1,0:T(8,128)(2,1)} %bitcast.119, ...), custom_call_target="tpu_custom_call" | custom-call | tf_op jit(solution)/shard_map/pallas_call | solution.py:193
  413.5 2.1 multiply_reduce_fusion.3
  415.6 1.1 multiply_reduce_fusion.5
  416.7 0.9 copy-done.3
  417.6 1.1 multiply_convert_fusion.1.block_ref
  418.7 13.5 %shard_map.243 = bf16[96,2304]{1,0:T(8,128)(2,1)} custom-call(bf16[96,2304]{1,0:T(8,128)(2,1)} %multiply_convert_fusion.1.block_ref), custom_call_target="tpu_custom_call" | custom-call | tf_op jit(solution)/shard_map/pallas_call | solution.py:193
  432.3 3.7 fusion.18
  437.2 1.2 fusion.16
  438.3 2.2 fusion.32
  441.5 2.2 convolution_bitcast_fusion.2
  443.9 0.8 copy-done.31
  444.8 1.5 fusion.23
  446.3 0.9 copy-done.16
  447.2 7.0 %fusion.2 = f32[192,2304]{1,0:T(8,128)S(1)} fusion(bf16[192,2048]{1,0:T(8,128)(2,1)S(1)} %constant_dynamic-update-slice_fusion, bf16[2304,3200]{1,0:T(8,128)(2,1)} %bitcast.144), kind=kOutput, calls=%fused_computation.3 | convolution fusion | flops 1811939328 | bytes 11993088 | tf_op jit(solution)/shard_map/dot_general | solution.py:1273
  455.1 0.8 fusion.40.block_ref
  455.9 13.0 %shard_map.244 = bf16[112,2304]{1,0:T(8,128)(2,1)} custom-call(bf16[112,2304]{1,0:T(8,128)(2,1)} %fusion.40.block_ref), custom_call_target="tpu_custom_call" | custom-call | tf_op jit(solution)/shard_map/pallas_call | solution.py:193
  469.0 1.2 convert_element_type.139
  470.4 1.2 multiply_add_fusion
  471.8 5.4 convolution_convert_fusion
  477.3 3.7 convolution_convert_fusion.1
  481.3 0.9 pad.16.clone
  482.3 157.3 %shard_map.245 = (bf16[3,144,4608]{2,1,0:T(8,128)(2,1)}, f32[144,3200]{1,0:T(8,128)}) custom-call(bf16[3,16,144,640]{3,2,1,0:T(8,128)(2,1)} %bitcast.117, bf16[16,144,2048]{2,1,0:T(8,128)(2,1)} %bitcast.116, bf16[16,144,1024]{2,1,0:T(8,128)(2,1)} %bitcast.120, bf16[16,144,128]{2,1,0:T(8,128)(2,1)} %bitcast.121), custom_call_target="tpu_custom_call" | custom-call | tf_op jit(solution)/shard_map/pallas_call | solution.py:193
  639.5 1.0 slice_bitcast_fusion
  640.6 0.9 slice_reduce_fusion
  641.5 2.4 fusion.74
  643.9 1.9 fusion.75
  645.8 3.5 bitcast_convert_fusion
  (154 shorter events, 10.6 us)
Async XLA Ops:
  165.6 2.3 copy-start.2
  165.6 2.3 copy-start.5
  168.2 5.9 copy-start.44
  174.0 1.4 copy-start.18
  174.1 4.7 copy-start.19
  175.8 1.0 slice-start
  176.2 0.9 copy-start.11
  176.2 0.9 copy-start.13
  176.5 2.2 copy-start.27
  176.5 0.9 copy-start.41
  176.5 2.2 copy-start.29
  177.2 1.5 copy-start.35
  177.3 2.7 copy-start.33
  178.7 0.6 copy-start.45
  180.7 4.2 copy-start.22
  195.9 1.5 copy-start.1
  195.9 1.5 copy-start.24
  197.2 0.6 copy-start.42
  197.3 0.7 copy-start.26
  246.2 53.0 %copy-start.8 = (bf16[96,2304]{1,0:T(8,128)(2,1)S(1)}, bf16[96,2304]{1,0:T(8,128)(2,1)}, u32[]{:S(2)}) copy-start(bf16[96,2304]{1,0:T(8,128)(2,1)} %param.27) | copy-start | bytes 1327108
  246.2 53.0 %copy-start.32 = (f32[2304]{0:T(1024)S(1)}, f32[2304]{0:T(1024)}, u32[]{:S(2)}) copy-start(f32[2304]{0:T(1024)} %get-tuple-element.47) | copy-start | bytes 27652
  297.8 3.5 copy-start
  413.5 2.1 copy-start.10
  413.5 2.1 copy-start.25
  413.5 2.1 copy-start.43
  416.7 0.9 copy-start.3
  432.3 4.1 copy-start.20
  436.0 0.9 copy-start.28
  436.0 1.0 copy-start.30
  436.1 1.1 copy-start.34
  436.1 1.1 copy-start.36
  436.1 2.3 copy-start.46
  438.3 2.3 copy-start.12
  438.3 2.3 copy-start.14
  443.8 0.9 copy-start.31
  443.8 1.0 copy-start.37
  446.3 0.9 copy-start.16
  447.2 7.0 %copy-start.6 = (bf16[96,2304]{1,0:T(8,128)(2,1)S(1)}, bf16[96,2304]{1,0:T(8,128)(2,1)}, u32[]{:S(2)}) copy-start(bf16[96,2304]{1,0:T(8,128)(2,1)} %get-tuple-element.25) | copy-start | bytes 1327108
  454.2 0.7 copy-start.38
  454.2 0.7 copy-start.39
  454.2 0.7 copy-start.40
  468.9 1.4 copy-start.4
  470.4 1.2 copy-start.7
  470.4 1.4 copy-start.17
  471.8 5.4 copy-start.15
  471.8 5.4 copy-start.21
  471.8 5.4 copy-start.23
  639.5 6.2 copy-start.9

commit v9 on v8

--- a/solution.py
+++ b/solution.py
@@ -315,59 +315,6 @@
             pltpu.VMEM(block, jnp.float32),
             *[pltpu.SemaphoreType.DMA((amount,)) for amount in (7, 4, 4, 4)],
         ]
-
-
-class Blocks:
-    def __init__(self, scatter, parts_refs, core_send_sem, core_sem, local_sem):
-        self.scatter, self.parts = scatter, []
-        self.core_send_sem, self.core_sem, self.local_sem = core_send_sem, core_sem, local_sem
-        start = 0
-        for ref in parts_refs:
-            self.parts.append((ref, pl.ds(start, ref.shape[2])))
-            start += ref.shape[2]
-
-    def local(self, k):
-        index = self.scatter.index(k, self.scatter.c)
-        return [
-            pltpu.make_async_copy(
-                ref.at[index], self.scatter.held.at[k, :, at], self.local_sem.at[k * len(self.parts) + i]
-            )
-            for i, (ref, at) in enumerate(self.parts)
-        ]
-
-    def to_core(self, k):
-        index = self.scatter.index(k, 1 - self.scatter.c)
-        return [
-            remote(
-                ref.at[index],
-                self.scatter.from_core.at[k, :, at],
-                self.core_send_sem.at[k * len(self.parts) + i],
-                self.core_sem.at[k * len(self.parts) + i],
-                self.scatter.other,
-            )
-            for i, (ref, at) in enumerate(self.parts)
-        ]
-
-    def load(self):
-        for k in range(8):
-            for copy in self.local(k):
-                copy.start()
-
-    def send(self):
-        for k in range(8):
-            for copy in self.to_core(k):
-                copy.start()
-
-    def both(self, k):
-        for copy in self.local(k):
-            copy.wait()
-        for copy in self.to_core(k):
-            copy.wait_recv()
-
-    def finish(self):
-        for k in range(8):
-            for copy in self.to_core(k):
-                copy.wait_send()
 
 
 def contract(left, right, left_dim, right_dim):
@@ -1039,14 +986,57 @@
 
 
 def collect_kernel(
-    parts_ref, projected_ref, output_ref, gain_ref, out_ref, attention_ref,
+    parts_ref, rows_ref, grad_rows_ref, projected_ref, attended_ref, gain_ref, out_ref, attention_ref,
     held, received, rest_held, rest_received,
     local_sem, pair_send, pair_receive, rest_pair_send, rest_pair_receive, send_sem, receive_sem, rest_send, rest_receive,
     *scatter_refs,
 ):
     scatter = Scatter(scatter_refs[:6], scatter_refs[6:10])
-    blocks = Blocks(scatter, (projected_ref, output_ref, gain_ref), *scatter_refs[10:13])
-    blocks.load()
+    for_core, left, projected, attended, core_send_sem, core_sem, operand_sem, gain_sem = scatter_refs[10:]
+    operands = [
+        pltpu.make_async_copy(source, target, operand_sem.at[i])
+        for i, (source, target) in enumerate(
+            ((rows_ref, left.at[0]), (grad_rows_ref, left.at[1]), (projected_ref, projected), (attended_ref, attended))
+        )
+    ]
+    for copy in operands:
+        copy.start()
+    split, gain_start = projected.shape[1], projected.shape[1] + attended.shape[1]
+
+    def gains(k, core, target, slot):
+        return pltpu.make_async_copy(
+            gain_ref.at[scatter.index(k, core)],
+            target.at[k, :, pl.ds(gain_start, gain_ref.shape[2])],
+            gain_sem.at[slot],
+        )
+
+    def weight_block(k, core, target):
+        index = scatter.index(k, core)
+        target[k, :, :split] = contract(left[0, index], projected[...], 1, 0).astype(target.dtype)
+        target[k, :, split:gain_start] = contract(left[1, index], attended[...], 1, 0).astype(target.dtype)
+
+    def to_core(k):
+        return remote(
+            for_core.at[k], scatter.from_core.at[k], core_send_sem.at[k], core_sem.at[k], scatter.other
+        )
+
+    def share(k, carry):
+        weight_block(k, 1 - scatter.c, for_core)
+        gains(k, 1 - scatter.c, for_core, k).wait()
+        to_core(k).start()
+        weight_block(k, scatter.c, scatter.held)
+        gains(k, scatter.c, scatter.held, 8 + k).wait()
+
+        @pl.when(k < 4)
+        def _():
+            to_core(k).wait_recv()
+            scatter.side(k)
+
+        return carry
+
+    for k in range(8):
+        gains(k, 1 - scatter.c, for_core, k).start()
+        gains(k, scatter.c, scatter.held, 8 + k).start()
     z, x, c, t = place()
     own = fsdp_index(z, x, c)
     rows = out_ref.shape[1]
@@ -1125,7 +1115,6 @@
                 rest_load(dz, i).start()
 
     greet([(peer(z, x, c, k), t) for k in range(1, 16)] + [partner])
-    blocks.send()
     for dz in order:
         for i in range(3):
             pair(dz, i).start()
@@ -1155,15 +1144,12 @@
                     rest_direct(k).start()
 
     def line(i):
-        blocks.both(4 + i)
+        to_core(4 + i).wait_recv()
         scatter.line(i)
 
-    def share(i, carry):
-        blocks.both(i)
-        scatter.side(i)
-        return carry
-
-    lax.fori_loop(0, 4, share, 0)
+    for copy in operands:
+        copy.wait()
+    lax.fori_loop(0, 8, share, 0)
     pass_on(2)
     line(0)
     pass_on(3)
@@ -1171,7 +1157,7 @@
     pass_on(1)
     line(2)
     pass_on(0)
-    blocks.both(7)
+    to_core(7).wait_recv()
     scatter.last()
     outward = pltpu.make_async_copy(scatter.total, attention_ref, local_sem.at[26])
     outward.start()
@@ -1220,13 +1206,14 @@
             rest_direct(k).wait_send()
         keep_rest.wait()
 
-    blocks.finish()
+    for k in range(8):
+        to_core(k).wait_send()
     scatter.finish()
     keep.wait()
     outward.wait()
 
 
-def collect(gradients, feed_width, attention_parts, collective_id):
+def collect(gradients, feed_width, rows, projected, grad_rows, attended, gain_parts, collective_id):
     size, pairs = lax.axis_size("fsdp"), lax.axis_size("tp")
     shard_rows = gradients.shape[1] // size
     if size != KERNEL_FSDP:
@@ -1235,10 +1222,12 @@
         mine = mine.reshape(size, shard_rows, mine.shape[-1])
         mine = lax.all_to_all(mine, "fsdp", split_axis=0, concat_axis=0, tiled=True)
         feed = [g.astype(jnp.float32) for g in unpack_units(mine, feed_width, 3)]
-        return feed, scatter_fsdp(attention_parts)
+        parts = (contract(rows, projected, 0, 0), contract(grad_rows, attended, 0, 0), gain_parts)
+        return feed, scatter_fsdp([part.astype(rows.dtype).reshape(size, shard_rows, -1) for part in parts])
     kind = gradients.dtype
     main, rest = (4, 3, 4, shard_rows, MAIN), (4, 3, 4, shard_rows, REST)
-    block = (shard_rows, sum(part.shape[2] for part in attention_parts))
+    columns = projected.shape[1] + attended.shape[1] + gain_parts.shape[1]
+    block, by_block = (shard_rows, columns), (size, shard_rows, rows.shape[0])
     out, attention = scratch_call(
         collect_kernel,
         (
@@ -1260,11 +1249,22 @@
             pltpu.SemaphoreType.DMA((size,)),
             pltpu.SemaphoreType.DMA((4,)),
             *Scatter.scratch(block, kind),
-            *[pltpu.SemaphoreType.DMA((24,)) for _ in range(3)],
+            pltpu.VMEM((8,) + block, kind),
+            pltpu.VMEM((2,) + by_block, kind),
+            pltpu.VMEM(projected.shape, kind),
+            pltpu.VMEM(attended.shape, kind),
+            pltpu.SemaphoreType.DMA((8,)),
+            pltpu.SemaphoreType.DMA((8,)),
+            pltpu.SemaphoreType.DMA((4,)),
+            pltpu.SemaphoreType.DMA((16,)),
         ],
         collective_id,
         gradients.reshape(3, size, shard_rows, UNITS),
-        *attention_parts,
+        jnp.transpose(rows).reshape(by_block),
+        jnp.transpose(grad_rows).reshape(by_block),
+        projected,
+        attended,
+        gain_parts.astype(kind).reshape(size, shard_rows, -1),
     )
     return [out[i].astype(jnp.float32) for i in range(3)], attention
 
@@ -1471,7 +1471,7 @@
     unit_one_both, inverse_one_both = normalize_parts(residual_both)
     residual = residual_both[:rows_local]
     unit_one, inverse_one = unit_one_both[:rows_local], inverse_one_both[:rows_local]
-    normed = (unit_one_both * gain_one).astype(low)
+    normed = lax.optimization_barrier((unit_one_both * gain_one).astype(low))
     projected = jnp.dot(
         normed, attention_full[:, :output_start], preferred_element_type=jnp.float32
     )
@@ -1580,14 +1580,11 @@
     (gate_weight_grad, up_weight_grad, down_weight_grad), attention_grads = collect(
         feed_grads,
         feed_width,
-        [
-            part.astype(low).reshape(size, shard_rows, part.shape[1])
-            for part in (
-                contract_first(normed, projected_grad),
-                contract_first(attention_grad_rows, attended),
-                jnp.pad(jnp.transpose(gain_grads), ((0, 0), (0, LANES - 4))),
-            )
-        ],
+        normed,
+        projected_grad,
+        attention_grad_rows,
+        attended,
+        jnp.pad(jnp.transpose(gain_grads), ((0, 0), (0, LANES - 4))),
         9,
     )
     gain_shards = jnp.transpose(attention_grads[:, gain_start : gain_start + 4])

time: 654 us -> 651 us (level)
    dot_general x2 -> x0, matrix products: 9.09 us -> none  [contract_first(): lax.dot_general(left_rows, right_rows, (((0,), (0,)), ((), ())), preferre...]
where the time goes in v9:
time: 651 us; the launch traced here: 647 us
  Pallas kernels  565 us (87%)
  matrix products  32.6 us (5%)
  other arithmetic  25.1 us (4%)
  local copies, waits for them, and re-layouts  22.9 us (4%)
    pallas_call x9, Pallas kernels, scratch_call(): pl.pallas_call(kernel, out_shape=outputs, in_specs=[ANY] * len(operands),...  565 us

profile of v9, /device:TPU:0, one launch (start us, length us, event | category | flops | bytes accessed | tf_op | source)
XLA Modules:
  0.0 647.0 jit_solution(11147133601011496083)
XLA Ops:
  0.6 0.7 stack.33
  1.3 0.7 stack.32
  4.1 161.6 %shard_map.237 = (bf16[16,144,3200]{2,1,0:T(8,128)(2,1)}, bf16[96,2304]{1,0:T(8,128)(2,1)}, bf16[3,16,144,640]{3,2,1,0:T(8,128)(2,1)}) custom-call(bf16[96,2304]{1,0:T(8,128)(2,1)} %rows_ref.1, bf16[144,1024]{1,0:T(8,128)(2,1)} %query_ref.1, bf16[144,512]{1,0:T(8,128)(2,1)} %key_ref.1, bf16[144,512]{1,0:T(8,128)(2,1)} %value_ref.1, ...), custom_call_target="tpu_custom_call" | custom-call | tf_op jit(solution)/shard_map/pallas_call | solution.py:193
  165.7 1.2 slice_convert_fusion.2
  168.5 6.1 fusion.4
  174.6 0.8 reshape.336
  178.1 1.3 fusion.78
  179.4 0.7 fusion.21
  180.9 4.2 fusion.8
  185.1 0.8 slice.262.block_ref
  185.9 10.2 %shard_map.238 = bf16[96,2304]{1,0:T(8,128)(2,1)} custom-call(bf16[96,2304]{1,0:T(8,128)(2,1)} %slice.262.block_ref), custom_call_target="tpu_custom_call" | custom-call | tf_op jit(solution)/shard_map/pallas_call | solution.py:193
  196.0 1.3 multiply_reduce_fusion.9
  198.4 0.9 multiply_convert_fusion.2.block_ref
  199.3 47.2 %shard_map.239 = (bf16[16,96,2304]{2,1,0:T(8,128)(2,1)}, f32[2,1536,640]{2,1,0:T(8,128)}, bf16[1536,640]{1,0:T(8,128)(2,1)}) custom-call(bf16[96,2304]{1,0:T(8,128)(2,1)} %multiply_convert_fusion.2.block_ref, bf16[3,2304,640]{2,1,0:T(8,128)(2,1)} %bitcast.114), custom_call_target="tpu_custom_call" | custom-call | tf_op jit(solution)/shard_map/pallas_call | solution.py:193
  246.6 51.4 %shard_map.240 = f32[96,2304]{1,0:T(8,128)} custom-call(bf16[1536,640]{1,0:T(8,128)(2,1)} %get-tuple-element.28.hidden_ref, bf16[3,2304,640]{2,1,0:T(8,128)(2,1)} %bitcast.115), custom_call_target="tpu_custom_call" | custom-call | tf_op jit(solution)/shard_map/pallas_call | solution.py:193
  298.1 1.4 multiply_reduce_fusion.7
  299.5 2.2 fusion.30
  301.7 1.2 fusion.29
  302.9 46.1 %shard_map.241 = (bf16[16,96,2304]{2,1,0:T(8,128)(2,1)}, bf16[2,1536,640]{2,1,0:T(8,128)(2,1)}) custom-call(bf16[96,2304]{1,0:T(8,128)(2,1)} %get-tuple-element.67.block_ref, bf16[3,2304,640]{2,1,0:T(8,128)(2,1)} %bitcast.116, f32[2,1536,640]{2,1,0:T(8,128)} %get-tuple-element.29.gate_up_ref), custom_call_target="tpu_custom_call" | custom-call | tf_op jit(solution)/shard_map/pallas_call | solution.py:193
  349.1 64.9 %shard_map.242 = (f32[96,2304]{1,0:T(8,128)}, bf16[3,2304,640]{2,1,0:T(8,128)(2,1)}) custom-call(bf16[2,1536,640]{2,1,0:T(8,128)(2,1)} %get-tuple-element.30.unit_grads_ref, bf16[3,2304,640]{2,1,0:T(8,128)(2,1)} %bitcast.117, bf16[1536,2304]{1,0:T(8,128)(2,1)} %bitcast.119, bf16[1536,2304]{1,0:T(8,128)(2,1)} %bitcast.120, ...), custom_call_target="tpu_custom_call" | custom-call | tf_op jit(solution)/shard_map/pallas_call | solution.py:193
  414.0 1.6 multiply_reduce_fusion.3
  415.7 1.1 multiply_reduce_fusion.5
  416.8 0.9 copy-done.3
  417.7 1.1 multiply_convert_fusion.1.block_ref
  418.8 13.5 %shard_map.243 = bf16[96,2304]{1,0:T(8,128)(2,1)} custom-call(bf16[96,2304]{1,0:T(8,128)(2,1)} %multiply_convert_fusion.1.block_ref), custom_call_target="tpu_custom_call" | custom-call | tf_op jit(solution)/shard_map/pallas_call | solution.py:193
  432.3 3.7 fusion.18
  436.4 1.2 convolution_bitcast_fusion
  437.6 1.2 fusion.16
  438.8 2.7 fusion.32
  443.0 2.7 convolution_bitcast_fusion.2
  445.9 0.8 copy-done.24
  446.8 1.6 fusion.23
  448.5 7.2 %fusion.2 = f32[192,2304]{1,0:T(8,128)S(1)} fusion(bf16[192,2048]{1,0:T(8,128)(2,1)S(1)} %constant_dynamic-update-slice_fusion.projected_ref, bf16[2304,3200]{1,0:T(8,128)(2,1)} %bitcast.147), kind=kOutput, calls=%fused_computation.2 | convolution fusion | flops 1811939328 | bytes 11993088 | tf_op jit(solution)/shard_map/dot_general | solution.py:1273
  455.7 1.5 multiply_reduce_fusion
  457.4 0.8 fusion.41.block_ref
  458.2 13.0 %shard_map.244 = bf16[112,2304]{1,0:T(8,128)(2,1)} custom-call(bf16[112,2304]{1,0:T(8,128)(2,1)} %fusion.41.block_ref), custom_call_target="tpu_custom_call" | custom-call | tf_op jit(solution)/shard_map/pallas_call | solution.py:193
  471.3 1.3 convert_element_type.131
  472.5 1.4 multiply_reduce_fusion.2
  474.0 1.2 multiply_add_fusion
  475.2 2.4 copy.105
  477.6 1.4 copy.106
  479.4 0.9 pad.16.clone
  480.4 156.9 %shard_map.245 = (bf16[3,144,4608]{2,1,0:T(8,128)(2,1)}, f32[144,3200]{1,0:T(8,128)}) custom-call(bf16[3,16,144,640]{3,2,1,0:T(8,128)(2,1)} %bitcast.118, bf16[16,144,192]{2,1,0:T(8,128)(2,1)} %bitcast.121, bf16[16,144,192]{2,1,0:T(8,128)(2,1)} %bitcast.122, bf16[192,2048]{1,0:T(8,128)(2,1)} %copy-done.15, bf16[192,1024]{1,0:T(8,128)(2,1)} %copy-done.17, ...), custom_call_target="tpu_custom_call" | custom-call | tf_op jit(solution)/shard_map/pallas_call | solution.py:193
  637.3 1.0 slice_bitcast_fusion
  638.3 0.9 slice_reduce_fusion
  639.2 2.4 fusion.74
  641.6 1.9 fusion.75
  643.5 3.5 bitcast_convert_fusion
  (151 shorter events, 10.7 us)
Async XLA Ops:
  165.6 1.7 copy-start.1
  165.6 1.7 copy-start.5
  167.6 0.6 copy-start.35
  168.5 6.1 copy-start.12
  168.5 7.0 %copy-start.41 = (s32[1,9]{1,0:T(1,128)S(1)}, s32[1,9]{1,0:T(1,128)}, u32[]{:S(2)}) copy-start(s32[1,9]{1,0:T(1,128)} %param.15) | copy-start | bytes 112
  174.6 1.5 copy-start.18
  176.1 3.3 copy-start.34
  176.6 1.0 slice-start
  177.0 0.9 copy-start.13
  177.3 2.1 copy-start.21
  177.3 2.1 copy-start.25
  178.0 1.5 copy-start.19
  178.0 2.1 copy-start.28
  178.1 2.1 copy-start.30
  179.4 0.7 copy-start.42
  180.9 4.2 copy-start.17
  196.0 1.5 copy-start.2
  197.3 0.6 copy-start.39
  197.9 0.5 copy-start.37
  298.0 3.7 copy-start
  298.0 3.7 copy-start.8
  414.0 1.7 copy-start.9
  414.0 1.7 copy-start.11
  414.0 1.7 copy-start.38
  414.0 1.7 copy-start.40
  416.8 0.9 copy-start.3
  432.3 4.1 copy-start.20
  436.0 1.5 copy-start.22
  436.1 1.5 copy-start.26
  436.1 1.5 copy-start.29
  436.1 1.5 copy-start.31
  436.1 2.7 copy-start.43
  438.8 2.8 copy-start.14
  442.1 0.9 copy-start.23
  445.7 0.9 copy-start.24
  445.7 1.0 copy-start.27
  448.4 7.2 %copy-start.15 = (bf16[192,2048]{1,0:T(8,128)(2,1)}, bf16[192,2048]{1,0:T(8,128)(2,1)S(1)}, u32[]{:S(2)}) copy-start(bf16[192,2048]{1,0:T(8,128)(2,1)S(1)} %constant_dynamic-update-slice_fusion.projected_ref) | copy-start | bytes 2359300
  448.5 7.2 %copy-start.36 = (f32[192]{0:T(256)S(1)}, f32[192]{0:T(256)}, u32[]{:S(2)}) copy-start(f32[192]{0:T(256)} %copy-done.35) | copy-start | bytes 2308
  455.7 1.5 copy-start.32
  455.7 1.6 copy-start.33
  471.2 2.7 copy-start.4
  471.3 2.7 copy-start.6
  471.3 2.7 slice-start.1
  475.2 2.4 copy-start.7
  475.2 2.4 copy-start.16
  637.3 6.2 copy-start.10

commit v10 on v9

--- a/solution.py
+++ b/solution.py
@@ -603,7 +603,7 @@
 
 def partial_pair(scatter, units, weights, block_rows, j, core, target):
     amount, width, _ = weights.shape
-    step = 3 * 256
+    step = 6 * 192
     spots = [pl.ds(pl.multiple_of(scatter.index(k, core) * block_rows, block_rows), block_rows) for k in (j, 4 + j)]
 
     def body(d, carry):

time: 651 us -> 651 us (level)
  no operation moved by 1% of the time
where the time goes in v10:
time: 651 us; the launch traced here: 647 us
  Pallas kernels  564 us (87%)
  matrix products  32.6 us (5%)
  other arithmetic  25.1 us (4%)
  local copies, waits for them, and re-layouts  22.9 us (4%)
    pallas_call x9, Pallas kernels, scratch_call(): pl.pallas_call(kernel, out_shape=outputs, in_specs=[ANY] * len(operands),...  564 us

profile of v10, /device:TPU:0, one launch (start us, length us, event | category | flops | bytes accessed | tf_op | source)
XLA Modules:
  0.0 646.7 jit_solution(8951662763530079712)
XLA Ops:
  0.6 0.7 stack.33
  1.3 0.7 stack.32
  4.1 161.6 %shard_map.237 = (bf16[16,144,3200]{2,1,0:T(8,128)(2,1)}, bf16[96,2304]{1,0:T(8,128)(2,1)}, bf16[3,16,144,640]{3,2,1,0:T(8,128)(2,1)}) custom-call(bf16[96,2304]{1,0:T(8,128)(2,1)} %rows_ref.1, bf16[144,1024]{1,0:T(8,128)(2,1)} %query_ref.1, bf16[144,512]{1,0:T(8,128)(2,1)} %key_ref.1, bf16[144,512]{1,0:T(8,128)(2,1)} %value_ref.1, ...), custom_call_target="tpu_custom_call" | custom-call | tf_op jit(solution)/shard_map/pallas_call | solution.py:193
  165.7 1.2 slice_convert_fusion.2
  168.5 6.1 fusion.4
  174.6 0.8 reshape.336
  178.1 1.3 fusion.78
  179.4 0.7 fusion.21
  180.9 4.2 fusion.8
  185.1 0.8 slice.262.block_ref
  185.9 10.2 %shard_map.238 = bf16[96,2304]{1,0:T(8,128)(2,1)} custom-call(bf16[96,2304]{1,0:T(8,128)(2,1)} %slice.262.block_ref), custom_call_target="tpu_custom_call" | custom-call | tf_op jit(solution)/shard_map/pallas_call | solution.py:193
  196.0 1.3 multiply_reduce_fusion.9
  198.4 0.9 multiply_convert_fusion.2.block_ref
  199.3 47.2 %shard_map.239 = (bf16[16,96,2304]{2,1,0:T(8,128)(2,1)}, f32[2,1536,640]{2,1,0:T(8,128)}, bf16[1536,640]{1,0:T(8,128)(2,1)}) custom-call(bf16[96,2304]{1,0:T(8,128)(2,1)} %multiply_convert_fusion.2.block_ref, bf16[3,2304,640]{2,1,0:T(8,128)(2,1)} %bitcast.114), custom_call_target="tpu_custom_call" | custom-call | tf_op jit(solution)/shard_map/pallas_call | solution.py:193
  246.6 51.9 %shard_map.240 = f32[96,2304]{1,0:T(8,128)} custom-call(bf16[1536,640]{1,0:T(8,128)(2,1)} %get-tuple-element.28.hidden_ref, bf16[3,2304,640]{2,1,0:T(8,128)(2,1)} %bitcast.115), custom_call_target="tpu_custom_call" | custom-call | tf_op jit(solution)/shard_map/pallas_call | solution.py:193
  298.5 1.4 multiply_reduce_fusion.7
  300.0 2.2 fusion.30
  302.2 1.2 fusion.29
  303.4 47.1 %shard_map.241 = (bf16[16,96,2304]{2,1,0:T(8,128)(2,1)}, bf16[2,1536,640]{2,1,0:T(8,128)(2,1)}) custom-call(bf16[96,2304]{1,0:T(8,128)(2,1)} %get-tuple-element.67.block_ref, bf16[3,2304,640]{2,1,0:T(8,128)(2,1)} %bitcast.116, f32[2,1536,640]{2,1,0:T(8,128)} %get-tuple-element.29.gate_up_ref), custom_call_target="tpu_custom_call" | custom-call | tf_op jit(solution)/shard_map/pallas_call | solution.py:193
  350.5 65.3 %shard_map.242 = (f32[96,2304]{1,0:T(8,128)}, bf16[3,2304,640]{2,1,0:T(8,128)(2,1)}) custom-call(bf16[2,1536,640]{2,1,0:T(8,128)(2,1)} %get-tuple-element.30.unit_grads_ref, bf16[3,2304,640]{2,1,0:T(8,128)(2,1)} %bitcast.117, bf16[1536,2304]{1,0:T(8,128)(2,1)} %bitcast.119, bf16[1536,2304]{1,0:T(8,128)(2,1)} %bitcast.120, ...), custom_call_target="tpu_custom_call" | custom-call | tf_op jit(solution)/shard_map/pallas_call | solution.py:193
  415.9 1.6 multiply_reduce_fusion.3
  417.5 1.1 multiply_reduce_fusion.5
  418.7 0.9 copy-done.3
  419.6 1.1 multiply_convert_fusion.1.block_ref
  420.7 12.1 %shard_map.243 = bf16[96,2304]{1,0:T(8,128)(2,1)} custom-call(bf16[96,2304]{1,0:T(8,128)(2,1)} %multiply_convert_fusion.1.block_ref), custom_call_target="tpu_custom_call" | custom-call | tf_op jit(solution)/shard_map/pallas_call | solution.py:193
  432.8 3.7 fusion.18
  436.9 1.2 convolution_bitcast_fusion
  438.0 1.2 fusion.16
  439.2 2.7 fusion.32
  443.5 2.7 convolution_bitcast_fusion.2
  446.4 0.8 copy-done.24
  447.2 1.6 fusion.23
  448.9 7.2 %fusion.2 = f32[192,2304]{1,0:T(8,128)S(1)} fusion(bf16[192,2048]{1,0:T(8,128)(2,1)S(1)} %constant_dynamic-update-slice_fusion.projected_ref, bf16[2304,3200]{1,0:T(8,128)(2,1)} %bitcast.147), kind=kOutput, calls=%fused_computation.2 | convolution fusion | flops 1811939328 | bytes 11993088 | tf_op jit(solution)/shard_map/dot_general | solution.py:1273
  456.2 1.5 multiply_reduce_fusion
  457.9 0.8 fusion.41.block_ref
  458.7 12.8 %shard_map.244 = bf16[112,2304]{1,0:T(8,128)(2,1)} custom-call(bf16[112,2304]{1,0:T(8,128)(2,1)} %fusion.41.block_ref), custom_call_target="tpu_custom_call" | custom-call | tf_op jit(solution)/shard_map/pallas_call | solution.py:193
  471.6 1.3 convert_element_type.131
  472.8 1.4 multiply_reduce_fusion.2
  474.3 1.2 multiply_add_fusion
  475.4 2.4 copy.105
  477.9 1.4 copy.106
  479.7 0.9 pad.16.clone
  480.6 156.2 %shard_map.245 = (bf16[3,144,4608]{2,1,0:T(8,128)(2,1)}, f32[144,3200]{1,0:T(8,128)}) custom-call(bf16[3,16,144,640]{3,2,1,0:T(8,128)(2,1)} %bitcast.118, bf16[16,144,192]{2,1,0:T(8,128)(2,1)} %bitcast.121, bf16[16,144,192]{2,1,0:T(8,128)(2,1)} %bitcast.122, bf16[192,2048]{1,0:T(8,128)(2,1)} %copy-done.15, bf16[192,1024]{1,0:T(8,128)(2,1)} %copy-done.17, ...), custom_call_target="tpu_custom_call" | custom-call | tf_op jit(solution)/shard_map/pallas_call | solution.py:193
  636.9 1.0 slice_bitcast_fusion
  637.9 0.9 slice_reduce_fusion
  638.8 2.4 fusion.74
  641.2 1.9 fusion.75
  643.1 3.5 bitcast_convert_fusion
  (151 shorter events, 10.7 us)
Async XLA Ops:
  165.6 1.7 copy-start.1
  165.6 1.7 copy-start.5
  167.6 0.6 copy-start.35
  168.5 6.1 copy-start.12
  168.5 7.0 %copy-start.41 = (s32[1,9]{1,0:T(1,128)S(1)}, s32[1,9]{1,0:T(1,128)}, u32[]{:S(2)}) copy-start(s32[1,9]{1,0:T(1,128)} %param.15) | copy-start | bytes 112
  174.6 1.5 copy-start.18
  176.1 3.3 copy-start.34
  176.6 1.0 slice-start
  177.0 0.9 copy-start.13
  177.3 2.1 copy-start.21
  177.3 2.1 copy-start.25
  178.0 1.5 copy-start.19
  178.0 2.1 copy-start.28
  178.1 2.1 copy-start.30
  179.4 0.7 copy-start.42
  180.9 4.2 copy-start.17
  196.0 1.5 copy-start.2
  197.3 0.6 copy-start.39
  197.9 0.5 copy-start.37
  298.5 3.7 copy-start
  298.5 3.7 copy-start.8
  415.8 1.7 copy-start.9
  415.8 1.7 copy-start.11
  415.8 1.7 copy-start.38
  415.9 1.7 copy-start.40
  418.7 0.9 copy-start.3
  432.8 4.1 copy-start.20
  436.5 1.5 copy-start.22
  436.5 1.5 copy-start.26
  436.5 1.5 copy-start.29
  436.5 1.5 copy-start.31
  436.6 2.7 copy-start.43
  439.2 2.8 copy-start.14
  442.6 0.9 copy-start.23
  446.2 0.9 copy-start.24
  446.2 1.0 copy-start.27
  448.9 7.2 %copy-start.15 = (bf16[192,2048]{1,0:T(8,128)(2,1)}, bf16[192,2048]{1,0:T(8,128)(2,1)S(1)}, u32[]{:S(2)}) copy-start(bf16[192,2048]{1,0:T(8,128)(2,1)S(1)} %constant_dynamic-update-slice_fusion.projected_ref) | copy-start | bytes 2359300
  448.9 7.2 %copy-start.36 = (f32[192]{0:T(256)S(1)}, f32[192]{0:T(256)}, u32[]{:S(2)}) copy-start(f32[192]{0:T(256)} %copy-done.35) | copy-start | bytes 2308
  456.2 1.5 copy-start.32
  456.2 1.6 copy-start.33
  471.5 2.7 copy-start.4
  471.5 2.7 copy-start.6
  471.5 2.7 slice-start.1
  475.4 2.4 copy-start.7
  475.4 2.4 copy-start.16
  636.9 6.2 copy-start.10
